TPU v7x, 32 devices: a whole 2x2x4 slice. The times are simulated.
32 devices in a mesh: grp: 2 (over x), page: 16 (over z, y, core).
Axes of the slice: x: 2, y: 2, z: 4, core: 2. Of those that a mesh axis runs over, the one named last changes fastest.
Arguments:
- queries: bfloat16 [32, 32, 128], P(('grp', 'page')), may hold values from -2 to 2
- patches: bfloat16 [65536, 128], P(('grp', 'page')), may hold values from -2 to 2
- page_blocks: int32 [512, 2], P(('grp', 'page')), may hold values from -1 to 63, as said below
- lengths: int32 [64], replicated, may hold values from 2 to 4352, as said below
- labels: int32 [32, 64], replicated, may hold values 0 or 1
Outputs:
- patch_grad: float32 [65536, 128], P(('grp', 'page'))
- query_grad: float32 [32, 32, 128], P(('grp', 'page'))
- mean_loss: float32 [1], replicated
Inputs may be any that keep to these rules, and one draw needn't show every extreme that they name: `page_blocks`: row i describes block slot i (patch rows i * 128 to (i + 1) * 128 - 1): its page and which of that page's blocks it is, counting from 0, or -1 and 0 for an empty slot. On each device the live slots come first among its 16 slots; every device has 2 or more live slots, and in every group some device has all 16 live. Page p has ceil(lengths[p] / 128) blocks in consecutive live slots in order, which may continue over consecutive devices of the page axis; the pages of one grp index form a contiguous range of ids, lie only on that index's devices and appear in increasing order. `lengths`: A page's last block holds 2 to 128 of its patches.
All inputs are finite; a program needn't handle non-finite values.
Results may differ from a plain program's by a relative error of at most 0.0017.
Values may be sent and summed in bfloat16 or wider, within the bound.
No kernel may reach another device: no remote copies, remote signals or barrier semaphores. Data moves between devices by JAX's collectives and lax.ppermute only.
A program may use at most 64 MiB of HBM per device.

v0:
```python
import jax
import jax.numpy as jnp
from jax import lax
from jax.sharding import PartitionSpec as P

QUESTION_WORDS = 32
BROWS = 128


smoothing_divisor = 0.05
logit_scale = 10.0
logit_bias = -4.0
very_low = -1e30


def entering(value, axis, join, neutral, backward):
    count, mine = (lax.axis_size(axis), lax.axis_index(axis))
    pieces = jax.tree.map(lambda part: lax.all_gather(part, axis), value)
    if backward:
        pieces = jax.tree.map(lambda part: part[::-1], pieces)
        mine = count - 1 - mine
    total = jax.tree.map(
        lambda part, zero: jnp.full_like(part, 0) + jnp.asarray(zero, part.dtype), value, neutral
    )

    def turn(position, total):
        longer = join(total, jax.tree.map(lambda part: part[position], pieces))
        return jax.tree.map(lambda new, old: jnp.where(position < mine, new, old), longer, total)

    return lax.fori_loop(0, count - 1, turn, total)


def merge_pair(peak_one, mass_one, peak_two, mass_two):
    peak_both = jnp.maximum(peak_one, peak_two)
    mass_both = mass_one * jnp.exp(peak_one - peak_both) + mass_two * jnp.exp(peak_two - peak_both)
    return (peak_both, mass_both)


def tail_runs(earlier, later_run):
    head_early, tail_early, whole_early, peak_early, mass_early = earlier
    head_late, tail_late, whole_late, peak_late, mass_late = later_run
    vacant_early = head_early < 0.0
    vacant_late = head_late < 0.0
    joined = (
        (whole_late > 0.5) & (tail_early == tail_late) & (head_early >= 0.0) & (head_late >= 0.0)
    )
    peak_both, mass_both = merge_pair(peak_early, mass_early, peak_late, mass_late)
    peak_run = jnp.where(vacant_late, peak_early, jnp.where(joined, peak_both, peak_late))
    mass_run = jnp.where(vacant_late, mass_early, jnp.where(joined, mass_both, mass_late))
    head_run = jnp.where(vacant_early, head_late, head_early)
    tail_run = jnp.where(vacant_late, tail_early, tail_late)
    link = (tail_early == head_late).astype(jnp.float32)
    whole_run = jnp.where(
        vacant_early,
        whole_late,
        jnp.where(vacant_late, whole_early, whole_early * whole_late * link),
    )
    return (head_run, tail_run, whole_run, peak_run, mass_run)


def head_runs(higher, lower_run):
    head_high, tail_high, whole_high, peak_high, mass_high = higher
    head_low, tail_low, whole_low, peak_low, mass_low = lower_run
    vacant_high = head_high < 0.0
    vacant_low = head_low < 0.0
    joined = (whole_low > 0.5) & (head_low == head_high) & (head_low >= 0.0) & (head_high >= 0.0)
    peak_both, mass_both = merge_pair(peak_low, mass_low, peak_high, mass_high)
    peak_run = jnp.where(vacant_low, peak_high, jnp.where(joined, peak_both, peak_low))
    mass_run = jnp.where(vacant_low, mass_high, jnp.where(joined, mass_both, mass_low))
    head_run = jnp.where(vacant_low, head_high, head_low)
    tail_run = jnp.where(vacant_high, tail_low, tail_high)
    link = (tail_low == head_high).astype(jnp.float32)
    whole_run = jnp.where(
        vacant_low, whole_high, jnp.where(vacant_high, whole_low, whole_low * whole_high * link)
    )
    return (head_run, tail_run, whole_run, peak_run, mass_run)


def shards(queries, patches, page_blocks, lengths, labels):
    count_of_slots = page_blocks.shape[0]
    feature_width = patches.shape[1]
    local_rows = queries.reshape(-1, feature_width)
    question_word_vectors = lax.all_gather(local_rows, ("grp", "page"), axis=0, tiled=True)
    row_count = question_word_vectors.shape[0]
    count_of_queries = row_count // QUESTION_WORDS
    page_count = lengths.shape[0]
    slot_pages = page_blocks[:, 0]
    numbers = page_blocks[:, 1]
    selector = (jnp.arange(page_count, dtype=jnp.int32)[:, None] == slot_pages[None, :]).astype(
        jnp.float32
    )
    slot_length = jnp.dot(lengths.astype(jnp.float32), selector, precision=lax.Precision.HIGHEST)
    offsets = numbers[:, None] * BROWS + jnp.arange(BROWS, dtype=jnp.int32)[None, :]
    live_rows = (slot_pages[:, None] >= 0) & (offsets.astype(jnp.float32) < slot_length[:, None])
    live_count = jnp.sum((slot_pages >= 0).astype(jnp.int32))

    def score_block(slot_index):
        image_region_group = lax.dynamic_slice_in_dim(patches, slot_index * BROWS, BROWS, 0)
        tempered_similarity = lax.dot_general(
            question_word_vectors,
            image_region_group,
            (((1,), (1,)), ((), ())),
            preferred_element_type=jnp.float32,
        )
        return (image_region_group, tempered_similarity * (1.0 / smoothing_divisor))

    def stats_step(slot_index, running):
        peak_slots, mass_slots = running
        image_region_group, tempered_similarity = score_block(slot_index)
        live_mask = live_rows[slot_index]
        tempered_similarity = jnp.where(live_mask[None, :], tempered_similarity, very_low)
        peak_row = jnp.max(tempered_similarity, axis=1)
        mass_row = jnp.sum(
            jnp.where(live_mask[None, :], jnp.exp(tempered_similarity - peak_row[:, None]), 0.0),
            axis=1,
        )
        return (peak_slots.at[slot_index].set(peak_row), mass_slots.at[slot_index].set(mass_row))

    start_peaks = jnp.full((count_of_slots, row_count), very_low, jnp.float32)
    start_masses = jnp.zeros((count_of_slots, row_count), jnp.float32)
    peak_slots, mass_slots = lax.fori_loop(
        0, count_of_slots, stats_step, (start_peaks, start_masses)
    )
    same_page = (slot_pages[:, None] == slot_pages[None, :]) & (slot_pages[:, None] >= 0)

    def page_merge(slot_mask):
        peak_page = jnp.max(jnp.where(slot_mask[:, None], peak_slots, very_low), axis=0)
        mass_page = jnp.sum(
            jnp.where(
                slot_mask[:, None], mass_slots * jnp.exp(peak_slots - peak_page[None, :]), 0.0
            ),
            axis=0,
        )
        return (peak_page, mass_page)

    peak_page, mass_page = lax.map(page_merge, same_page)
    first_page = slot_pages[0].astype(jnp.float32).reshape(1)
    last_page = slot_pages[live_count - 1].astype(jnp.float32).reshape(1)
    single_page = (first_page == last_page).astype(jnp.float32)
    tail_record = (
        first_page,
        last_page,
        single_page,
        peak_page[live_count - 1],
        mass_page[live_count - 1],
    )
    head_record = (first_page, last_page, single_page, peak_page[0], mass_page[0])
    vacant = (
        jnp.full((1,), -1.0, jnp.float32),
        jnp.full((1,), -1.0, jnp.float32),
        jnp.ones((1,), jnp.float32),
        jnp.full((row_count,), very_low, jnp.float32),
        jnp.zeros((row_count,), jnp.float32),
    )
    lower_runs = entering(tail_record, "page", tail_runs, vacant, False)
    upper_runs = entering(head_record, "page", head_runs, vacant, True)
    page_values = slot_pages.astype(jnp.float32)
    from_below = ((page_values == lower_runs[1]) & (slot_pages >= 0))[:, None]
    peak_merge, mass_merge = merge_pair(
        peak_page, mass_page, lower_runs[3][None, :], lower_runs[4][None, :]
    )
    peak_page = jnp.where(from_below, peak_merge, peak_page)
    mass_page = jnp.where(from_below, mass_merge, mass_page)
    from_above = ((page_values == upper_runs[0]) & (slot_pages >= 0))[:, None]
    peak_merge, mass_merge = merge_pair(
        peak_page, mass_page, upper_runs[3][None, :], upper_runs[4][None, :]
    )
    peak_page = jnp.where(from_above, peak_merge, peak_page)
    mass_page = jnp.where(from_above, mass_merge, mass_page)
    live_slot = (slot_pages >= 0)[:, None]
    document_smooth_maximum = jnp.where(
        live_slot, peak_page + jnp.log(jnp.where(live_slot, mass_page, 1.0)), 0.0
    )
    similarity_values = smoothing_divisor * jnp.sum(
        document_smooth_maximum.reshape(count_of_slots, count_of_queries, QUESTION_WORDS), axis=2
    )
    logits = logit_scale / QUESTION_WORDS * similarity_values + logit_bias
    label_slots = jnp.dot(labels.astype(jnp.float32), selector, precision=lax.Precision.HIGHEST)
    label_signs = 2.0 * label_slots.T - 1.0
    pair_loss = jax.nn.softplus(-label_signs * logits)
    counted = ((slot_pages >= 0) & (numbers == 0)).astype(jnp.float32)
    loss_part = jnp.sum(pair_loss * counted[:, None])
    mean_loss = lax.psum(loss_part, ("grp", "page")) / count_of_queries
    logit_grad = -label_signs * jax.nn.sigmoid(-label_signs * logits)

    def grad_step(slot_index, running):
        query_grad, patch_grad = running
        image_region_group, tempered_similarity = score_block(slot_index)
        live_mask = live_rows[slot_index]
        weights = jnp.where(
            live_mask[None, :],
            jnp.exp(tempered_similarity - document_smooth_maximum[slot_index][:, None]),
            0.0,
        )
        row_grad = jnp.repeat(logit_grad[slot_index], QUESTION_WORDS) * (
            logit_scale / QUESTION_WORDS
        )
        coupling = (row_grad[:, None] * weights).astype(jnp.bfloat16)
        block_grad = lax.dot_general(
            coupling,
            question_word_vectors,
            (((0,), (0,)), ((), ())),
            preferred_element_type=jnp.float32,
        )
        query_grad = query_grad + jnp.dot(
            coupling, image_region_group, preferred_element_type=jnp.float32
        )
        patch_grad = lax.dynamic_update_slice_in_dim(patch_grad, block_grad, slot_index * BROWS, 0)
        return (query_grad, patch_grad)

    start_query = jnp.zeros((row_count, feature_width), jnp.float32)
    start_patch = jnp.zeros(patches.shape, jnp.float32)
    query_grad, patch_grad = lax.fori_loop(0, count_of_slots, grad_step, (start_query, start_patch))
    groups = lax.axis_size("grp")
    members = lax.axis_size("page")
    shaped = query_grad.reshape(groups, members, row_count // (groups * members), feature_width)
    within = lax.psum_scatter(shaped, "page", scatter_dimension=1, tiled=True)
    summed = lax.psum_scatter(within, "grp", scatter_dimension=0, tiled=True)
    return (patch_grad, summed.reshape(queries.shape), jnp.reshape(mean_loss, (1,)))


def solution(mesh):
    placed = (
        P(("grp", "page"), None, None),
        P(("grp", "page"), None),
        P(("grp", "page"), None),
        P(),
        P(),
    )
    return jax.shard_map(
        shards,
        mesh=mesh,
        in_specs=placed,
        out_specs=(P(("grp", "page"), None), P(("grp", "page"), None, None), P()),
        check_vma=False,
    )
```

profile of v0, /device:TPU:0, one launch (start us, length us, event | category | flops | bytes accessed | tf_op | source)
XLA Modules:
  0.0 548.1 jit_solution(5437650280501823290)
XLA Ops:
  14.4 1.3 bitcast_dynamic-update-slice_fusion
  16.3 35.0 %all-reduce.4 = (f32[16]{0:T(128)S(1)}, f32[16]{0:T(128)S(1)}, f32[16]{0:T(128)S(1)}) all-reduce(f32[16]{0:T(128)S(1)} %bitcast_dynamic-update-slice_fusion.2, f32[16]{0:T(128)S(1)} %bitcast_dynamic-update-slice_fusion.1, f32[16]{0:T(128)S(1)} %bitcast_dynamic-update-slice_fusion), channel_id=1, replica_groups=mesh['grp'=2,'page'=16] {'page'}, use_global_device_ids=true, to_apply=%add | all-reduce | flops 48 | bytes 384
  52.2 37.0 %all-gather = bf16[1,1024,128]{2,1,0:T(8,128)(2,1)S(1)} all-gather(bf16[1,32,128]{2,1,0:T(8,128)(2,1)S(1)} %copy-done.3), channel_id=2, replica_groups=mesh['grp'=2,'page'=16] {'grp','page'}, dimensions={1}, use_global_device_ids=true | all-gather | bytes 270336 | tf_op jit(solution)/shard_map/all_gather | solution.py:83
  90.0 42.7 %while.83 = (s32[]{:T(128)}, f32[16,1024]{1,0:T(8,128)S(1)}, f32[16,1024]{1,0:T(8,128)S(1)}, pred[16,128]{1,0:T(8,128)(4,1)S(1)}, bf16[2048,128]{1,0:T(8,128)(2,...) while((s32[]{:T(128)}, f32[16,1024]{1,0:T(8,128)S(1)}, ...), condition=%wide.region_5.0_spmd, body=%wide.region_1.5_spmd.sunk | while | flops 34340876 | bytes 1397457 | solution.py:121
  132.8 7.2 %while.84 = (s32[]{:T(128)}, f32[16,1024]{1,0:T(8,128)S(1)}, f32[16,1024]{1,0:T(8,128)S(1)}, pred[16,16]{1,0:T(8,128)(4,1)S(1)}, f32[16,1024]{1,0:T(8,128)S(1)},...) while((s32[]{:T(128)}, f32[16,1024]{1,0:T(8,128)S(1)}, f32[16,1024]{1,0:T(8,128)S(1)}, ...), condition=%wide.region_9.10_spmd, body=%wide.region_6.9_spmd.sunk | while | flops 96258 | bytes 225449 | solution.py:136
  140.0 19.3 %all-gather.3 = f32[16,1,1024]{2,1,0:T(1,128)S(1)} all-gather(f32[1,1,1024]{2,1,0:T(1,128)S(1)} %get-tuple-element.876), channel_id=1, replica_groups=mesh['grp'=2,'page'=16] {'page'}, dimensions={0}, use_global_device_ids=true | all-gather | bytes 69632 | tf_op jit(solution)/shard_map/all_gather | solution.py:18
  159.3 17.6 %all-gather.4 = f32[16,1,1024]{2,1,0:T(1,128)S(1)} all-gather(f32[1,1,1024]{2,1,0:T(1,128)S(1)} %get-tuple-element.874), channel_id=1, replica_groups=mesh['grp'=2,'page'=16] {'page'}, dimensions={0}, use_global_device_ids=true | all-gather | bytes 69632 | tf_op jit(solution)/shard_map/all_gather | solution.py:18
  176.9 81.7 %while.86 = (s32[]{:T(128)}, f32[1]{0:T(128)}, f32[1]{0:T(128)}, f32[1024]{0:T(1024)S(1)}, f32[1024]{0:T(1024)S(1)}, /*index=5*/s32[]{:T(128)}, f32[16,1]{0,1:T(...) while((s32[]{:T(128)}, f32[1]{0:T(128)}, f32[1]{0:T(128)}, ...), condition=%wide.region_13.14_spmd.clone, body=%wide.region_12.13_spmd.clone.sunk | while | flops 14353 | bytes 41262 | solution.py:30
  258.7 18.9 %all-gather.1 = f32[16,1,1024]{2,1,0:T(1,128)S(1)} all-gather(f32[1,1,1024]{2,1,0:T(1,128)S(1)} %get-tuple-element.877), channel_id=1, replica_groups=mesh['grp'=2,'page'=16] {'page'}, dimensions={0}, use_global_device_ids=true | all-gather | bytes 69632 | tf_op jit(solution)/shard_map/all_gather | solution.py:18
  277.8 17.6 %all-gather.2 = f32[16,1,1024]{2,1,0:T(1,128)S(1)} all-gather(f32[1,1,1024]{2,1,0:T(1,128)S(1)} %get-tuple-element.875), channel_id=1, replica_groups=mesh['grp'=2,'page'=16] {'page'}, dimensions={0}, use_global_device_ids=true | all-gather | bytes 69632 | tf_op jit(solution)/shard_map/all_gather | solution.py:18
  295.6 67.7 %while.85 = (s32[]{:T(128)}, f32[1]{0:T(128)}, f32[1024]{0:T(1024)S(1)}, f32[1024]{0:T(1024)S(1)}, s32[]{:T(128)}, /*index=5*/f32[16,1]{0,1:T(1,128)S(1)}, f32[1...) while((s32[]{:T(128)}, f32[1]{0:T(128)}, ...), condition=%wide.region_11.12_spmd.clone, body=%wide.region_10.11_spmd.clone.sunk | while | flops 14350 | bytes 41203 | solution.py:30
  365.1 41.4 %while.87 = (s32[]{:T(128)}, f32[1024,128]{1,0:T(8,128)S(1)}, f32[2048,128]{1,0:T(8,128)S(1)}, f32[16,32]{1,0:T(8,128)S(1)}, pred[16,128]{1,0:T(8,128)(4,1)S(1)}...) while((s32[]{:T(128)}, f32[1024,128]{1,0:T(8,128)S(1)}, ...), condition=%wide.region_16.17_spmd.clone, body=%wide.region_15.16_spmd.clone.sunk | while | flops 101580832 | bytes 2520013 | solution.py:213
  369.0 1.1 convolution_add_fusion.2
  371.6 1.1 convolution_add_fusion.2
  379.3 1.1 convolution_add_fusion.2
  381.9 1.1 convolution_add_fusion.2
  384.5 1.1 convolution_add_fusion.2
  387.1 1.1 convolution_add_fusion.2
  397.4 1.1 convolution_add_fusion.2
  400.0 1.1 convolution_add_fusion.2
  405.2 1.1 convolution_add_fusion.2
  407.4 89.2 %all-reduce.7.cloned.1.call-done = f32[2,16,32,128]{3,2,1,0:T(8,128)} async-done(((f32[2,16,32,128]{3,2,1,0:T(8,128)}), f32[2,16,32,128]{3,2,1,0:T(8,128)}) %all-reduce.7.cloned.1.call-update) | async-done | bytes 524304
  496.5 2.1 constant_dynamic-slice_fusion.12
  498.6 40.8 %psum.7 = f32[]{:T(128)} all-reduce(f32[]{:T(128)} %get-tuple-element.878), channel_id=1, replica_groups=mesh['grp'=2,'page'=16] {'grp','page'}, use_global_device_ids=true, to_apply=%region_20.21 | all-reduce | flops 1 | bytes 8 | tf_op jit(solution)/shard_map/psum | solution.py:183
  (491 shorter events, 127.3 us)
Async XLA Ops:
  7.2 489.4 %all-reduce.7.cloned.1.call-start = ((), (), s32[]{:S(2)}) async-start(), calls=%async_computation.2 | async-start | bytes 1048576
  7.2 0.7 copy-start.4
  12.5 0.7 copy-start.5
  51.4 0.7 copy-start.7
  51.4 0.9 copy-start.3
  89.4 0.7 copy-start.2
  363.5 0.7 copy-start.6
  406.5 0.8 copy-start
  406.5 133.6 %copy-start.1 = (f32[2048,128]{1,0:T(8,128)}, f32[2048,128]{1,0:T(8,128)S(1)}, u32[]{:S(2)}) copy-start(f32[2048,128]{1,0:T(8,128)S(1)} %get-tuple-element.669) | copy-start | bytes 3145732
  407.3 132.8 %reduce-scatter.5.cloned.1.call-start = ((), (), s32[]{:S(2)}) async-start(), calls=%async_computation.1 | async-start | bytes 49152 | tf_op jit(solution)/shard_map/reduce_scatter | solution.py:218
Sparse Core Ops, SparseCore 0:
  407.4 89.0 all-reduce.6
  499.3 10.4 reduce-scatter.4
where the time goes:
time: 554 us; the launch traced here: 548 us
  blocking collectives  186 us (34%)
  loops' own time  114 us (21%)
  waiting for transfers between devices  89.2 us (16%)
  matrix products  54.2 us (10%)
  other arithmetic  46.4 us (8%)
  local copies, waits for them, and re-layouts  39.6 us (7%)
  between operations  18.8 us (3%)
    another operation x2, loops' own time, entering(): return lax.fori_loop(0, count - 1, turn, total)  111 us
    unnamed x3, waiting for transfers between devices  89.2 us
    all_gather x4, blocking collectives, entering(): pieces = jax.tree.map(lambda part: lax.all_gather(part, axis), value)  73.4 us
    psum x1, blocking collectives, shards(): mean_loss = lax.psum(loss_part, ('grp', 'page')) / count_of_queries  40.8 us
    all_gather x1, blocking collectives, shards(): lax.all_gather(local_rows, ('grp', 'page'), axis=0, tiled=True)  37 us
    unnamed x1, blocking collectives  35 us
    dot_general x32, matrix products, score_block(): lax.dot_general(question_word_vectors, image_region_group, (((1,), (1,)),...  32.5 us
    another operation x32, other arithmetic  20.4 us
  transfers between devices with their start and end apart: 2, of which 1 were waited for; matrix products, arithmetic and copies ran while one was open for 0% of the time, Pallas kernels for 0%

commit v1 on v0

v1 whole, which is shorter than its diff:
```python
import jax
import jax.numpy as jnp
from jax import lax
from jax.experimental import pallas as pl
from jax.experimental.pallas import tpu as pltpu
from jax.sharding import PartitionSpec as P

QUESTION_WORDS = 32
BROWS = 128

smoothing_divisor = 0.05
logit_scale = 10.0
logit_bias = -4.0
very_low = -1e30
LOG2E = 1.4426950408889634
LN2 = 0.6931471805599453
SCALE2 = LOG2E / smoothing_divisor
CHUNK = 256
LOSS_ROWS = 8

f32 = jnp.float32
bf16 = jnp.bfloat16
VMEM = pl.BlockSpec(memory_space=pltpu.VMEM)
SMEM = pl.BlockSpec(memory_space=pltpu.SMEM)


def live_of_slot(pb_ref, len_ref, slot):
    page = pb_ref[slot, 0]
    length = len_ref[jnp.maximum(page, 0)]
    return jnp.where(page < 0, 0, length - pb_ref[slot, 1] * BROWS)


def lse_rows(values, mask):
    peak = jnp.max(jnp.where(mask, values, very_low), axis=0, keepdims=True)
    mass = jnp.sum(jnp.where(mask, jnp.exp2(values - peak), 0.0), axis=0, keepdims=True)
    return peak + jnp.log2(mass)


def scored(q_ref, p_ref, live, slot, lo):
    block = p_ref[pl.ds(pl.multiple_of(slot * BROWS, BROWS), BROWS), :]
    z = lax.dot_general(
        block, q_ref[lo : lo + CHUNK, :], (((1,), (1,)), ((), ())), preferred_element_type=f32
    )
    rows = lax.broadcasted_iota(jnp.int32, (BROWS, 1), 0)
    return jnp.where(rows < live, z * SCALE2, very_low)


def stats_kernel(pb_ref, len_ref, pbv_ref, q_ref, p_ref, lse_ref, send_ref):
    slots, rows = lse_ref.shape

    def one(slot, carry):
        live = live_of_slot(pb_ref, len_ref, slot)
        for lo in range(0, rows, CHUNK):
            z = scored(q_ref, p_ref, live, slot, lo)
            peak = jnp.max(z, axis=0, keepdims=True)
            mass = jnp.sum(jnp.exp2(z - peak), axis=0, keepdims=True)
            lse_ref[pl.ds(slot, 1), lo : lo + CHUNK] = peak + jnp.log2(mass)
        return carry

    lax.fori_loop(0, slots, one, 0)
    pages = pbv_ref[:, 0:1]
    first = pb_ref[0, 0]
    last = jnp.max(pages)
    values = lse_ref[...]
    head = lse_rows(values, pages == first)
    tail = lse_rows(values, pages == last)
    mine = lax.axis_index("page")
    peers = send_ref.shape[0]
    for peer in range(peers):
        up = peer > mine
        send_ref[peer, :, :rows] = jnp.where(up, tail, head)
        send_ref[peer, :, rows:] = jnp.full((1, 128), jnp.where(up, last, first).astype(f32))


def merge_kernel(pb_ref, pbv_ref, lab_ref, lse_ref, page_ref, sign_ref):
    slots, rows = lse_ref.shape
    pages = pbv_ref[:, 0:1]
    values = lse_ref[...]
    for slot in range(slots):
        page_ref[slot : slot + 1, :] = lse_rows(values, pages == pb_ref[slot, 0])
    queries, page_count = lab_ref.shape
    ids = lax.broadcasted_iota(jnp.int32, (slots, page_count), 1)
    picked = lax.dot_general(
        (ids == pages).astype(bf16),
        lab_ref[...].astype(bf16),
        (((1,), (1,)), ((), ())),
        preferred_element_type=f32,
    )
    spread = (
        lax.broadcasted_iota(jnp.int32, (queries, rows), 1) // QUESTION_WORDS
        == lax.broadcasted_iota(jnp.int32, (queries, rows), 0)
    ).astype(bf16)
    sign_ref[...] = 2.0 * jnp.dot(picked.astype(bf16), spread, preferred_element_type=f32) - 1.0


def add_lse(one, two):
    peak = jnp.maximum(one, two)
    return peak + jnp.log2(jnp.exp2(one - peak) + jnp.exp2(two - peak))


def three_terms(value):
    high = value.astype(bf16)
    rest = value - high.astype(f32)
    mid = rest.astype(bf16)
    return high, mid, (rest - mid.astype(f32)).astype(bf16)


def query_kernel(
    pb_ref, len_ref, pbv_ref, page_ref, sign_ref, recv_ref, q_ref, p_ref, out_ref, lse_ref, row_ref,
    acc_ref,
):
    slots, rows = page_ref.shape
    peers = recv_ref.shape[0]
    mine = lax.axis_index("page")
    pages = pbv_ref[:, 0:1]
    first = pb_ref[0, 0]
    last = jnp.max(pages)

    def gathered(wanted, below):
        peak = jnp.full((1, rows), very_low, f32)
        parts = []
        for peer in range(peers):
            side = peer < mine if below else peer > mine
            same = (recv_ref[peer, :, rows : rows + 1] == wanted.astype(f32)) & side
            parts.append(jnp.where(same, recv_ref[peer, :, :rows], very_low))
            peak = jnp.maximum(peak, parts[-1])
        mass = jnp.zeros((1, rows), f32)
        for part in parts:
            mass = mass + jnp.where(part > 0.5 * very_low, jnp.exp2(part - peak), 0.0)
        return peak + jnp.log2(jnp.maximum(mass, 1e-30))

    value = page_ref[...]
    value = jnp.where(pages == first, add_lse(value, gathered(first, True)), value)
    value = jnp.where(pages == last, add_lse(value, gathered(last, False)), value)
    value = jnp.where(pages >= 0, value, 0.0)
    lse_ref[...] = value
    same_group = (
        lax.broadcasted_iota(jnp.int32, (CHUNK, CHUNK), 0) // QUESTION_WORDS
        == lax.broadcasted_iota(jnp.int32, (CHUNK, CHUNK), 1) // QUESTION_WORDS
    ).astype(bf16)
    counted = (pages >= 0) & (pbv_ref[:, 1:2] == 0)
    loss = jnp.zeros((), f32)
    for lo in range(0, rows, CHUNK):
        piece = jnp.concatenate(three_terms(value[:, lo : lo + CHUNK]), axis=0)
        total = jnp.dot(piece, same_group, preferred_element_type=f32)
        total = total[:slots] + total[slots : 2 * slots] + total[2 * slots :]
        scores = (smoothing_divisor * LN2) * total
        logits = (logit_scale / QUESTION_WORDS) * scores + logit_bias
        sign = sign_ref[:, lo : lo + CHUNK]
        margin = -sign * logits
        small = jnp.exp(-jnp.abs(margin))
        pair = jnp.maximum(margin, 0.0) + jnp.log1p(small)
        loss = loss + jnp.sum(jnp.where(counted, pair, 0.0))
        sigmoid = jnp.where(margin >= 0.0, 1.0, small) / (1.0 + small)
        row_ref[:, lo : lo + CHUNK] = -sign * sigmoid * (logit_scale / QUESTION_WORDS)
    loss = loss * (1.0 / QUESTION_WORDS)

    acc_ref[...] = jnp.zeros_like(acc_ref)

    def one(slot, carry):
        live = live_of_slot(pb_ref, len_ref, slot)
        block = p_ref[pl.ds(pl.multiple_of(slot * BROWS, BROWS), BROWS), :]
        for lo in range(0, rows, CHUNK):
            coupling = coupled(q_ref, p_ref, lse_ref, row_ref, live, slot, lo)
            acc_ref[:, lo : lo + CHUNK] += lax.dot_general(
                block, coupling, (((0,), (0,)), ((), ())), preferred_element_type=f32
            )
        return carry

    lax.fori_loop(0, slots, one, 0)
    devices = out_ref.shape[0]
    local = rows // devices
    out_ref[:, :local, :] = acc_ref[...].T.astype(bf16).reshape(devices, local, BROWS)
    terms = three_terms(jnp.full((1, BROWS), loss))
    tail = jnp.concatenate([t.astype(f32) for t in terms] + [jnp.zeros((LOSS_ROWS - 3, BROWS), f32)], axis=0)
    for device in range(devices):
        out_ref[device, local:, :] = tail.astype(bf16)


def coupled(q_ref, p_ref, lse_ref, row_ref, live, slot, lo):
    z = scored(q_ref, p_ref, live, slot, lo)
    weights = jnp.exp2(z - lse_ref[pl.ds(slot, 1), lo : lo + CHUNK])
    return (row_ref[pl.ds(slot, 1), lo : lo + CHUNK] * weights).astype(bf16)


def patch_kernel(pb_ref, len_ref, lse_ref, row_ref, q_ref, p_ref, out_ref):
    slots, rows = lse_ref.shape

    def one(slot, carry):
        live = live_of_slot(pb_ref, len_ref, slot)
        total = jnp.zeros((BROWS, BROWS), f32)
        for lo in range(0, rows, CHUNK):
            coupling = coupled(q_ref, p_ref, lse_ref, row_ref, live, slot, lo)
            total = total + jnp.dot(
                coupling, q_ref[lo : lo + CHUNK, :], preferred_element_type=f32
            )
        out_ref[pl.ds(pl.multiple_of(slot * BROWS, BROWS), BROWS), :] = total
        return carry

    lax.fori_loop(0, slots, one, 0)


def final_kernel(scale, recv_ref, grad_ref, loss_ref):
    devices, padded, _ = recv_ref.shape
    total = jnp.zeros((padded, BROWS), f32)
    for device in range(devices):
        total = total + recv_ref[device].astype(f32)
    local = padded - LOSS_ROWS
    grad_ref[...] = total[:local]
    loss_ref[...] = (total[local : local + 1] + total[local + 1 : local + 2] + total[local + 2 : local + 3]) * scale


def cost(flops, bytes_accessed=0, transcendentals=0):
    return pl.CostEstimate(
        flops=flops, bytes_accessed=bytes_accessed, transcendentals=transcendentals
    )


def shards(queries, patches, page_blocks, lengths, labels):
    axes = ("grp", "page")
    devices = lax.axis_size(axes)
    peers = lax.axis_size("page")
    slots = page_blocks.shape[0]
    width = patches.shape[1]
    local_rows = queries.reshape(-1, width)
    local = local_rows.shape[0]
    rows = local * devices
    matmul = 2 * rows * patches.shape[0] * width
    q = lax.all_to_all(
        jnp.broadcast_to(local_rows[None], (devices, local, width)), axes, 0, 0, tiled=True
    ).reshape(rows, width)

    lse, send = pl.pallas_call(
        stats_kernel,
        in_specs=[SMEM, SMEM, VMEM, VMEM, VMEM],
        out_specs=[VMEM, VMEM],
        out_shape=[
            jax.ShapeDtypeStruct((slots, rows), f32),
            jax.ShapeDtypeStruct((peers, 1, rows + 128), f32),
        ],
        cost_estimate=cost(matmul),
        name="stats",
    )(page_blocks, lengths, page_blocks, q, patches)
    recv = lax.all_to_all(send, "page", 0, 0, tiled=True)

    page_lse, sign = pl.pallas_call(
        merge_kernel,
        in_specs=[SMEM, VMEM, VMEM, VMEM],
        out_specs=[VMEM, VMEM],
        out_shape=[
            jax.ShapeDtypeStruct((slots, rows), f32),
            jax.ShapeDtypeStruct((slots, rows), f32),
        ],
        cost_estimate=cost(matmul),
        name="merge",
    )(page_blocks, page_blocks, labels, lse)

    parts, full_lse, row_grad = pl.pallas_call(
        query_kernel,
        in_specs=[SMEM, SMEM, VMEM, VMEM, VMEM, VMEM, VMEM, VMEM],
        out_specs=[VMEM, VMEM, VMEM],
        out_shape=[
            jax.ShapeDtypeStruct((devices, local + LOSS_ROWS, width), bf16),
            jax.ShapeDtypeStruct((slots, rows), f32),
            jax.ShapeDtypeStruct((slots, rows), f32),
        ],
        scratch_shapes=[pltpu.VMEM((width, rows), f32)],
        cost_estimate=cost(2 * matmul),
        name="query",
    )(page_blocks, lengths, page_blocks, page_lse, sign, recv, q, patches)
    gathered = lax.all_to_all(parts, axes, 0, 0, tiled=True)

    patch_grad = pl.pallas_call(
        patch_kernel,
        in_specs=[SMEM, SMEM, VMEM, VMEM, VMEM, VMEM],
        out_specs=VMEM,
        out_shape=jax.ShapeDtypeStruct(patches.shape, f32),
        cost_estimate=cost(2 * matmul),
        name="patch",
    )(page_blocks, lengths, full_lse, row_grad, q, patches)

    query_grad, loss = pl.pallas_call(
        lambda *refs: final_kernel(QUESTION_WORDS / rows, *refs),
        in_specs=[VMEM],
        out_specs=[VMEM, VMEM],
        out_shape=[
            jax.ShapeDtypeStruct((local, width), f32),
            jax.ShapeDtypeStruct((1, BROWS), f32),
        ],
        cost_estimate=cost(devices * local * width),
        name="final",
    )(gathered)
    return (patch_grad, query_grad.reshape(queries.shape), loss[0, :1])


def solution(mesh):
    placed = (
        P(("grp", "page"), None, None),
        P(("grp", "page"), None),
        P(("grp", "page"), None),
        P(),
        P(),
    )
    return jax.shard_map(
        shards,
        mesh=mesh,
        in_specs=placed,
        out_specs=(P(("grp", "page"), None), P(("grp", "page"), None, None), P()),
        check_vma=False,
    )
```

time: 554 us -> 68.5 us (0.12)
  blocking collectives: 186 us -> 0 us
  loops' own time: 114 us -> 0 us
  waiting for transfers between devices: 89.2 us -> 15.2 us
  matrix products: 54.2 us -> 0 us
  other arithmetic: 46.4 us -> 0 us
  local copies, waits for them, and re-layouts: 39.6 us -> 4.15 us
  Pallas kernels: 0 us -> 34.5 us
  between operations: 18.8 us -> 0.67 us
  starting transfers between devices: 0.08 us -> 13.5 us
    another operation x5 -> x0, loops' own time: 114 us -> none  [the longest x2 111 us: entering(): return lax.fori_loop(0, count - 1, turn, total)]
    all_gather x5 -> x0, blocking collectives: 110 us -> none  [the longest x4 73.4 us: entering(): pieces = jax.tree.map(lambda part: lax.all_gather(part, axis), value)]
    unnamed x3 -> x0, waiting for transfers between devices: 89.2 us -> none
    dot_general x66 -> x0, matrix products: 54.2 us -> none  [the longest x32 32.5 us: score_block(): lax.dot_general(question_word_vectors, image_region_group, (((1,), (1,)),...]
    psum x1 -> x0, blocking collectives: 40.8 us -> none  [shards(): mean_loss = lax.psum(loss_part, ('grp', 'page')) / count_of_queries]
    unnamed x1 -> x0, blocking collectives: 35 us -> none
    pallas_call x0 -> x5, Pallas kernels: none -> 34.5 us  [the longest x1 12.4 us: shards(): pl.pallas_call(query_kernel, in_specs=[SMEM, SMEM, VMEM, VMEM, VMEM, VMEM...]
    another operation x32 -> x0, other arithmetic: 20.4 us -> none
  transfers between devices with their start and end apart: 2 -> 3, of which waited for: 1 -> 3; matrix products, arithmetic and copies ran while one was open for 0% -> 1% of each run, Pallas kernels for 0% -> 19%
where the time goes in v1:
time: 68.5 us; the launch traced here: 68 us
  Pallas kernels  34.5 us (50%)
  waiting for transfers between devices  15.2 us (22%)
  starting transfers between devices  13.5 us (20%)
  local copies, waits for them, and re-layouts  4.15 us (6%)
    pallas_call x1, Pallas kernels, shards(): pl.pallas_call(query_kernel, in_specs=[SMEM, SMEM, VMEM, VMEM, VMEM, VMEM...  12.4 us
    pallas_call x1, Pallas kernels, shards(): pl.pallas_call(patch_kernel, in_specs=[SMEM, SMEM, VMEM, VMEM, VMEM, VMEM...  10.8 us
    all_to_all x1, waiting for transfers between devices, shards(): lax.all_to_all(jnp.broadcast_to(local_rows[None], (devices, local, width)...  9.56 us
    pallas_call x1, Pallas kernels, shards(): pl.pallas_call(stats_kernel, in_specs=[SMEM, SMEM, VMEM, VMEM, VMEM], out...  7.51 us
    all_to_all x1, starting transfers between devices, shards(): lax.all_to_all(jnp.broadcast_to(local_rows[None], (devices, local, width)...  7.33 us
    all_to_all x1, waiting for transfers between devices, shards(): recv = lax.all_to_all(send, 'page', 0, 0, tiled=True)  4.78 us
    all_to_all x1, starting transfers between devices, shards(): recv = lax.all_to_all(send, 'page', 0, 0, tiled=True)  3.56 us
    unnamed x9, local copies, waits for them, and re-layouts  2.72 us
  transfers between devices with their start and end apart: 3, of which 3 were waited for; matrix products, arithmetic and copies ran while one was open for 1% of the time, Pallas kernels for 19%

profile of v1, /device:TPU:0, one launch (start us, length us, event | category | flops | bytes accessed | tf_op | source)
XLA Modules:
  0.0 68.0 jit_solution(7190331403868200084)
XLA Ops:
  0.6 1.4 %broadcast_in_dim.8 = bf16[32,32,128]{2,1,0:T(8,128)(2,1)} broadcast(bf16[32,128]{1,0:T(8,128)(2,1)} %bitcast.8), dimensions={1,2} | broadcast | bytes 270336 | tf_op jit(solution)/shard_map/broadcast_in_dim | solution.py:230
  2.1 0.0 copy-start.3
  2.1 7.3 %all-to-all-start = ((bf16[32,32,128]{2,1,0:T(8,128)(2,1)}), bf16[32,32,128]{2,1,0:T(8,128)(2,1)S(1)}, u32[]{:S(2)}, u32[]{:S(2)}) async-start(bf16[32,32,128]{2,1,0:T(8,128)(2,1)} %broadcast_in_dim.8), calls=%async_computation | async-start | bytes 524288 | tf_op jit(solution)/shard_map/all_to_all | solution.py:229
  9.4 0.0 copy-done.3
  9.4 0.7 %copy.14.pb_ref.pbv_ref = s32[16,2]{1,0:T(8,128)} copy(s32[16,2]{0,1:T(2,128)S(1)} %copy-done.3) | data formatting | bytes 256 | tf_op args[2]
  10.1 9.6 %all-to-all-done = bf16[32,32,128]{2,1,0:T(8,128)(2,1)S(1)} async-done(((bf16[32,32,128]{2,1,0:T(8,128)(2,1)}), bf16[32,32,128]{2,1,0:T(8,128)(2,1)S(1)}, u32[]{:S(2)}, u32[]{:S(2)}) %all-to-all-start) | async-done | bytes 262176 | tf_op jit(solution)/shard_map/all_to_all | solution.py:229
  19.7 0.0 copy-start.1
  19.7 0.7 %copy-done.1 = bf16[32,32,128]{2,1,0:T(8,128)(2,1)} copy-done((bf16[32,32,128]{2,1,0:T(8,128)(2,1)}, bf16[32,32,128]{2,1,0:T(8,128)(2,1)S(1)}, u32[]{:S(2)}) %copy-start.1) | copy-done | bytes 262168
  20.3 7.5 %stats.1 = (f32[16,1024]{1,0:T(8,128)}, f32[16,1,1152]{2,1,0:T(1,128)}) custom-call(s32[16,2]{1,0:T(8,128)} %copy.14.pb_ref.pbv_ref, s32[64]{0:T(128)} %len_ref.5, s32[16,2]{1,0:T(8,128)} %copy.14.pb_ref.pbv_ref, bf16[1024,128]{1,0:T(8,128)(2,1)} %bitcast.5, bf16[2048,128]{1,0:T(8,128)(2,1)} %p_ref.5), custom_call_target="tpu_custom_call" | custom-call | flops 536870912 | tf_op jit(solution)/shard_map/stats/pallas_call | solution.py:233
  27.9 3.6 %all-to-all-start.1 = ((f32[16,1,1152]{2,1,0:T(1,128)}), f32[16,1,1152]{2,1,0:T(1,128)S(1)}, u32[]{:S(2)}, u32[]{:S(2)}) async-start(f32[16,1,1152]{2,1,0:T(1,128)} %get-tuple-element.15), calls=%async_computation.1 | async-start | bytes 147456 | tf_op jit(solution)/shard_map/all_to_all | solution.py:244
  31.4 2.2 %merge.1 = (f32[16,1024]{1,0:T(8,128)}, f32[16,1024]{1,0:T(8,128)}) custom-call(s32[16,2]{1,0:T(8,128)} %copy.14.pb_ref.pbv_ref, s32[16,2]{1,0:T(8,128)} %copy.14.pb_ref.pbv_ref, s32[32,64]{1,0:T(8,128)} %lab_ref.1, f32[16,1024]{1,0:T(8,128)} %get-tuple-element.12.lse_ref), custom_call_target="tpu_custom_call" | custom-call | flops 536870912 | tf_op jit(solution)/shard_map/merge/pallas_call | solution.py:246
  33.6 4.8 %all-to-all-done.1.recv_ref = f32[16,1,1152]{2,1,0:T(1,128)S(1)} async-done(((f32[16,1,1152]{2,1,0:T(1,128)}), f32[16,1,1152]{2,1,0:T(1,128)S(1)}, u32[]{:S(2)}, u32[]{:S(2)}) %all-to-all-start.1) | async-done | bytes 73760 | tf_op jit(solution)/shard_map/all_to_all | solution.py:244
  38.4 0.0 copy-start.2
  38.4 0.6 copy-done.2
  39.0 12.4 %query.1 = (bf16[32,40,128]{2,1,0:T(8,128)(2,1)}, f32[16,1024]{1,0:T(8,128)}, f32[16,1024]{1,0:T(8,128)}) custom-call(s32[16,2]{1,0:T(8,128)} %copy.14.pb_ref.pbv_ref, s32[64]{0:T(128)} %len_ref.5, s32[16,2]{1,0:T(8,128)} %copy.14.pb_ref.pbv_ref, f32[16,1024]{1,0:T(8,128)} %get-tuple-element.13.page_ref, f32[16,1024]{1,0:T(8,128)} %get-tuple-element.14.sign_ref, ...), custom_call_target="tpu_custom_call" | custom-call | flops 1073741824 | tf_op jit(solution)/shard_map/query/pallas_call | solution.py:258
  51.4 2.6 %all-to-all-start.2 = ((bf16[32,40,128]{2,1,0:T(8,128)(2,1)}), bf16[32,40,128]{2,1,0:T(8,128)(2,1)S(1)}, u32[]{:S(2)}, u32[]{:S(2)}) async-start(bf16[32,40,128]{2,1,0:T(8,128)(2,1)} %get-tuple-element.18), calls=%async_computation.2 | async-start | bytes 655360 | tf_op jit(solution)/shard_map/all_to_all | solution.py:271
  54.0 10.8 %patch.1 = f32[2048,128]{1,0:T(8,128)} custom-call(s32[16,2]{1,0:T(8,128)} %copy.14.pb_ref.pbv_ref, s32[64]{0:T(128)} %len_ref.5, f32[16,1024]{1,0:T(8,128)} %get-tuple-element.16.lse_ref, f32[16,1024]{1,0:T(8,128)} %get-tuple-element.17.row_ref, bf16[1024,128]{1,0:T(8,128)(2,1)} %bitcast.7, bf16[2048,128]{1,0:T(8,128)(2,1)} %p_ref.5), custom_call_target="tpu_custom_call" | custom-call | flops 1073741824 | tf_op jit(solution)/shard_map/patch/pallas_call | solution.py:273
  64.8 0.8 %all-to-all-done.2.refs_0_ = bf16[32,40,128]{2,1,0:T(8,128)(2,1)S(1)} async-done(((bf16[32,40,128]{2,1,0:T(8,128)(2,1)}), bf16[32,40,128]{2,1,0:T(8,128)(2,1)S(1)}, u32[]{:S(2)}, u32[]{:S(2)}) %all-to-all-start.2) | async-done | bytes 327712 | tf_op jit(solution)/shard_map/all_to_all | solution.py:271
  65.6 0.0 copy-start
  65.6 0.7 %copy-done = bf16[32,40,128]{2,1,0:T(8,128)(2,1)} copy-done((bf16[32,40,128]{2,1,0:T(8,128)(2,1)}, bf16[32,40,128]{2,1,0:T(8,128)(2,1)S(1)}, u32[]{:S(2)}) %copy-start) | copy-done | bytes 327704
  66.4 1.6 %final.1 = (f32[32,128]{1,0:T(8,128)}, f32[1,128]{1,0:T(1,128)}) custom-call(bf16[32,40,128]{2,1,0:T(8,128)(2,1)} %copy-done), custom_call_target="tpu_custom_call" | custom-call | flops 131072 | tf_op jit(solution)/shard_map/final/pallas_call | solution.py:282
Async XLA Ops:
  2.1 7.3 %copy-start.3 = (s32[16,2]{0,1:T(2,128)S(1)}, s32[16,2]{0,1:T(2,128)}, u32[]{:S(2)}) copy-start(s32[16,2]{0,1:T(2,128)} %param.7) | copy-start | bytes 388
  2.1 17.6 %all-to-all-start = ((bf16[32,32,128]{2,1,0:T(8,128)(2,1)}), bf16[32,32,128]{2,1,0:T(8,128)(2,1)S(1)}, u32[]{:S(2)}, u32[]{:S(2)}) async-start(bf16[32,32,128]{2,1,0:T(8,128)(2,1)} %broadcast_in_dim.8), calls=%async_computation | async-start | bytes 524288 | tf_op jit(solution)/shard_map/all_to_all | solution.py:229
  19.7 0.7 %copy-start.1 = (bf16[32,32,128]{2,1,0:T(8,128)(2,1)}, bf16[32,32,128]{2,1,0:T(8,128)(2,1)S(1)}, u32[]{:S(2)}) copy-start(bf16[32,32,128]{2,1,0:T(8,128)(2,1)S(1)} %all-to-all-done) | copy-start | bytes 786436
  27.9 10.5 %all-to-all-start.1 = ((f32[16,1,1152]{2,1,0:T(1,128)}), f32[16,1,1152]{2,1,0:T(1,128)S(1)}, u32[]{:S(2)}, u32[]{:S(2)}) async-start(f32[16,1,1152]{2,1,0:T(1,128)} %get-tuple-element.15), calls=%async_computation.1 | async-start | bytes 147456 | tf_op jit(solution)/shard_map/all_to_all | solution.py:244
  38.4 0.6 copy-start.2
  51.4 14.3 %all-to-all-start.2 = ((bf16[32,40,128]{2,1,0:T(8,128)(2,1)}), bf16[32,40,128]{2,1,0:T(8,128)(2,1)S(1)}, u32[]{:S(2)}, u32[]{:S(2)}) async-start(bf16[32,40,128]{2,1,0:T(8,128)(2,1)} %get-tuple-element.18), calls=%async_computation.2 | async-start | bytes 655360 | tf_op jit(solution)/shard_map/all_to_all | solution.py:271
  65.6 0.7 %copy-start = (bf16[32,40,128]{2,1,0:T(8,128)(2,1)}, bf16[32,40,128]{2,1,0:T(8,128)(2,1)S(1)}, u32[]{:S(2)}) copy-start(bf16[32,40,128]{2,1,0:T(8,128)(2,1)S(1)} %all-to-all-done.2.refs_0_) | copy-start | bytes 983044

commit v2 on v1

v2 whole, which is shorter than its diff:
```python
import jax
import jax.numpy as jnp
from jax import lax
from jax.experimental import pallas as pl
from jax.experimental.pallas import tpu as pltpu
from jax.sharding import PartitionSpec as P

QUESTION_WORDS = 32
BROWS = 128

smoothing_divisor = 0.05
logit_scale = 10.0
logit_bias = -4.0
very_low = -1e30
LOG2E = 1.4426950408889634
LN2 = 0.6931471805599453
SCALE2 = LOG2E / smoothing_divisor
CHUNK = 256
LOSS_ROWS = 8
INSIDE, HEAD, TAIL = 0, 1, 2

f32 = jnp.float32
bf16 = jnp.bfloat16
VMEM = pl.BlockSpec(memory_space=pltpu.VMEM)
SMEM = pl.BlockSpec(memory_space=pltpu.SMEM)


def lse_rows(values, mask):
    peak = jnp.max(jnp.where(mask, values, very_low), axis=0, keepdims=True)
    mass = jnp.sum(jnp.where(mask, jnp.exp2(values - peak), 0.0), axis=0, keepdims=True)
    return peak + jnp.log2(mass)


def add_lse(one, two):
    peak = jnp.maximum(one, two)
    return peak + jnp.log2(jnp.exp2(one - peak) + jnp.exp2(two - peak))


def chosen_row(values, mask):
    return jnp.max(jnp.where(mask, values, very_low), axis=0, keepdims=True)


def three_terms(value):
    high = value.astype(bf16)
    rest = value - high.astype(f32)
    mid = rest.astype(bf16)
    return high, mid, (rest - mid.astype(f32)).astype(bf16)


def block_of(p_ref, slot):
    return p_ref[pl.ds(pl.multiple_of(slot * BROWS, BROWS), BROWS), :]


def scored(qt_ref, block, live_ref, slot, lo):
    z = jnp.dot(block, qt_ref[:, lo : lo + CHUNK], preferred_element_type=f32)
    rows = lax.broadcasted_iota(jnp.int32, (BROWS, 1), 0)
    return jnp.where(rows < live_ref[pl.ds(slot, 1), 0:1], z * SCALE2, very_low)


def prep_kernel(pb_ref, len_ref, lab_ref, live_ref, sign_ref):
    slots, rows = sign_ref.shape
    queries, page_count = lab_ref.shape
    pages = pb_ref[:, 0:1]
    ids = lax.broadcasted_iota(jnp.int32, (slots, page_count), 1)
    hit = ids == pages
    length = jnp.sum(jnp.where(hit, len_ref[...], 0).astype(f32), axis=1, keepdims=True)
    live = length.astype(jnp.int32) - pb_ref[:, 1:2] * BROWS
    live_ref[...] = jnp.broadcast_to(jnp.where(pages < 0, 0, live), live_ref.shape)
    picked = lax.dot_general(
        hit.astype(bf16),
        lab_ref[...].astype(bf16),
        (((1,), (1,)), ((), ())),
        preferred_element_type=f32,
    )
    spread = (
        lax.broadcasted_iota(jnp.int32, (queries, rows), 1) // QUESTION_WORDS
        == lax.broadcasted_iota(jnp.int32, (queries, rows), 0)
    ).astype(bf16)
    sign_ref[...] = 2.0 * jnp.dot(picked.astype(bf16), spread, preferred_element_type=f32) - 1.0


def stats_kernel(pb_ref, live_ref, q_ref, p_ref, lse_ref, send_ref, qt_ref):
    slots, rows = lse_ref.shape
    qt_ref[...] = q_ref[...].T
    for slot in range(slots):
        block = block_of(p_ref, slot)
        for lo in range(0, rows, CHUNK):
            z = scored(qt_ref, block, live_ref, slot, lo)
            peak = jnp.max(z, axis=0, keepdims=True)
            mass = jnp.sum(jnp.exp2(z - peak), axis=0, keepdims=True)
            lse_ref[pl.ds(slot, 1), lo : lo + CHUNK] = peak + jnp.log2(mass)
    pages = pb_ref[:, 0:1]
    first = pages[0:1]
    last = jnp.max(pages, axis=0, keepdims=True)
    values = lse_ref[...]
    head = lse_rows(values, pages == first)
    tail = lse_rows(values, pages == last)
    mine = lax.axis_index("page")
    for peer in range(send_ref.shape[0]):
        up = peer > mine
        send_ref[peer, :, :rows] = jnp.where(up, tail, head)
        send_ref[peer, :, rows:] = jnp.broadcast_to(jnp.where(up, last, first).astype(f32), (1, 128))


def gradients(value, sign):
    count, rows = value.shape
    same_group = (
        lax.broadcasted_iota(jnp.int32, (CHUNK, CHUNK), 0) // QUESTION_WORDS
        == lax.broadcasted_iota(jnp.int32, (CHUNK, CHUNK), 1) // QUESTION_WORDS
    ).astype(bf16)
    totals = []
    for lo in range(0, rows, CHUNK):
        total = [
            jnp.dot(term, same_group, preferred_element_type=f32)
            for term in three_terms(value[:, lo : lo + CHUNK])
        ]
        totals.append(total[0] + total[1] + total[2])
    scores = (smoothing_divisor * LN2) * jnp.concatenate(totals, axis=1)
    logits = (logit_scale / QUESTION_WORDS) * scores + logit_bias
    margin = -sign * logits
    small = jnp.exp(-jnp.abs(margin))
    pair = jnp.maximum(margin, 0.0) + jnp.log1p(small)
    sigmoid = jnp.where(margin >= 0.0, 1.0, small) / (1.0 + small)
    return -sign * sigmoid * (logit_scale / QUESTION_WORDS), pair


def inner_kernel(
    pbs_ref, pb_ref, live_ref, sign_ref, lse_ref, q_ref, p_ref, page_ref, row_ref, loss_ref, acc_ref,
    qt_ref, weight_ref,
):
    slots, rows = lse_ref.shape
    qt_ref[...] = q_ref[...].T
    pages = pb_ref[:, 0:1]
    first = pages[0:1]
    last = jnp.max(pages, axis=0, keepdims=True)
    values = lse_ref[...]
    for slot in range(slots):
        page_ref[slot : slot + 1, :] = lse_rows(values, pages == pages[slot : slot + 1])
    value = jnp.where(pages >= 0, page_ref[...], 0.0)
    row, pair = gradients(value, sign_ref[...])
    inside = (pages != first) & (pages != last)
    counted = inside & (pages >= 0) & (pb_ref[:, 1:2] == 0)
    row_ref[...] = row
    weight_ref[...] = jnp.where(inside, row, 1.0)
    page_ref[...] = value
    loss = jnp.sum(jnp.where(counted, pair, 0.0), axis=0, keepdims=True)
    loss_ref[...] = jnp.broadcast_to(jnp.sum(loss, axis=1, keepdims=True), loss_ref.shape)
    acc_ref[...] = jnp.zeros_like(acc_ref)
    head_page = pbs_ref[0, 0]
    tail_page = head_page
    for slot in range(1, slots):
        tail_page = jnp.maximum(tail_page, pbs_ref[slot, 0])

    def one(step, carry):
        for half in range(2):
            slot = step * 2 + half
            page = pbs_ref[slot, 0]
            kind = jnp.where(page == head_page, HEAD, jnp.where(page == tail_page, TAIL, INSIDE))
            block = block_of(p_ref, slot)
            for lo in range(0, rows, CHUNK):
                z = scored(qt_ref, block, live_ref, slot, lo)
                weights = jnp.exp2(z - page_ref[pl.ds(slot, 1), lo : lo + CHUNK])
                part = (weight_ref[pl.ds(slot, 1), lo : lo + CHUNK] * weights).astype(bf16)
                acc_ref[kind, :, lo : lo + CHUNK] += lax.dot_general(
                    block, part, (((0,), (0,)), ((), ())), preferred_element_type=f32
                )
        return carry

    lax.fori_loop(0, slots // 2, one, 0)


def close_kernel(
    pb_ref, sign_ref, page_ref, row_ref, loss_ref, acc_ref, recv_ref, out_ref, lse_ref, full_ref
):
    slots, rows = page_ref.shape
    peers = recv_ref.shape[0]
    devices = out_ref.shape[0]
    local = rows // devices
    mine = lax.axis_index("page")
    pages = pb_ref[:, 0:1]
    first = pages[0:1]
    last = jnp.max(pages, axis=0, keepdims=True)
    is_first = pages == first
    is_last = pages == last
    alone = first == last

    def gathered(wanted, below):
        parts = []
        for peer in range(peers):
            side = peer < mine if below else peer > mine
            same = (recv_ref[peer, :, rows : rows + 1] == wanted.astype(f32)) & side
            parts.append(jnp.where(same, recv_ref[peer, :, :rows], very_low))
        peak = parts[0]
        for part in parts[1:]:
            peak = jnp.maximum(peak, part)
        mass = jnp.zeros((1, rows), f32)
        for part in parts:
            mass = mass + jnp.where(part > 0.5 * very_low, jnp.exp2(part - peak), 0.0)
        return peak + jnp.log2(jnp.maximum(mass, 1e-30))

    below = gathered(first, True)
    above = gathered(last, False)
    value = page_ref[...]
    head = value[0:1]
    tail = chosen_row(value, is_last)
    head_full = add_lse(head, below)
    head_full = jnp.where(alone, add_lse(head_full, above), head_full)
    tail_full = jnp.where(alone, head_full, add_lse(tail, above))
    both = jnp.concatenate([head_full, tail_full], axis=0)
    sign = sign_ref[...]
    signs = jnp.concatenate([sign[0:1], chosen_row(sign, is_last)], axis=0)
    row, pair = gradients(both, signs)
    starts = pb_ref[:, 1:2] == 0
    head_counts = starts[0:1]
    tail_counts = (jnp.max((starts & is_last).astype(jnp.int32), axis=0, keepdims=True) > 0) & jnp.logical_not(alone)
    loss = jnp.sum(
        jnp.where(head_counts, pair[0:1], 0.0) + jnp.where(tail_counts, pair[1:2], 0.0),
        axis=1,
        keepdims=True,
    )
    loss = (loss + loss_ref[...]) * (1.0 / QUESTION_WORDS)
    lse_ref[...] = jnp.where(is_last, tail_full, jnp.where(is_first, head_full, value))
    full_ref[...] = jnp.where(is_last, row[1:2], jnp.where(is_first, row[0:1], row_ref[...]))
    head_scale = row[0:1] * jnp.exp2(head - head_full)
    tail_scale = row[1:2] * jnp.exp2(tail - tail_full)
    for lo in range(0, rows, CHUNK):
        span = slice(lo, lo + CHUNK)
        total = (
            acc_ref[INSIDE, :, span]
            + acc_ref[HEAD, :, span] * head_scale[:, span]
            + acc_ref[TAIL, :, span] * tail_scale[:, span]
        )
        turned = total.T.astype(bf16).reshape(CHUNK // local, local, BROWS)
        out_ref[lo // local : (lo + CHUNK) // local, :local, :] = turned
    terms = three_terms(loss)
    zeros = jnp.zeros((LOSS_ROWS - 3, BROWS), f32)
    last_rows = jnp.concatenate([t.astype(f32) for t in terms] + [zeros], axis=0).astype(bf16)
    for device in range(devices):
        out_ref[device, local:, :] = last_rows


def patch_kernel(live_ref, lse_ref, row_ref, q_ref, p_ref, out_ref, qt_ref):
    slots, rows = lse_ref.shape
    qt_ref[...] = q_ref[...].T

    def one(step, carry):
        for half in range(2):
            slot = step * 2 + half
            block = block_of(p_ref, slot)
            total = jnp.zeros((BROWS, BROWS), f32)
            for lo in range(0, rows, CHUNK):
                z = scored(qt_ref, block, live_ref, slot, lo)
                weights = jnp.exp2(z - lse_ref[pl.ds(slot, 1), lo : lo + CHUNK])
                coupling = (row_ref[pl.ds(slot, 1), lo : lo + CHUNK] * weights).astype(bf16)
                total = total + jnp.dot(
                    coupling, q_ref[lo : lo + CHUNK, :], preferred_element_type=f32
                )
            out_ref[pl.ds(pl.multiple_of(slot * BROWS, BROWS), BROWS), :] = total
        return carry

    lax.fori_loop(0, slots // 2, one, 0)


def final_kernel(scale, recv_ref, grad_ref, loss_ref):
    devices, padded, _ = recv_ref.shape
    total = jnp.zeros((padded, BROWS), f32)
    for device in range(devices):
        total = total + recv_ref[device].astype(f32)
    local = padded - LOSS_ROWS
    grad_ref[...] = total[:local]
    loss_ref[...] = (total[local : local + 1] + total[local + 1 : local + 2] + total[local + 2 : local + 3]) * scale


def call(kernel, name, flops, in_specs, shapes, scratch=(), limit=24):
    return pl.pallas_call(
        kernel,
        in_specs=in_specs,
        out_specs=[VMEM] * len(shapes),
        out_shape=[jax.ShapeDtypeStruct(*shape) for shape in shapes],
        scratch_shapes=[pltpu.VMEM(*shape) for shape in scratch],
        cost_estimate=pl.CostEstimate(flops=flops, bytes_accessed=0, transcendentals=0),
        compiler_params=pltpu.CompilerParams(vmem_limit_bytes=limit << 20),
        name=name,
    )


def shards(queries, patches, page_blocks, lengths, labels):
    axes = ("grp", "page")
    devices = lax.axis_size(axes)
    peers = lax.axis_size("page")
    slots = page_blocks.shape[0]
    width = patches.shape[1]
    local_rows = queries.reshape(-1, width)
    local = local_rows.shape[0]
    rows = local * devices
    matmul = 2 * rows * patches.shape[0] * width
    table = ((slots, rows), f32)
    turned = ((width, rows), bf16)
    q = lax.all_to_all(
        jnp.broadcast_to(local_rows[None], (devices, local, width)), axes, 0, 0, tiled=True
    ).reshape(rows, width)
    live, sign = call(
        prep_kernel, "prep", matmul, [VMEM] * 3, [((slots, 128), jnp.int32), table]
    )(page_blocks, lengths.reshape(1, -1), labels)
    lse, send = call(
        stats_kernel, "stats", matmul, [VMEM] * 4, [table, ((peers, 1, rows + 128), f32)], [turned]
    )(page_blocks, live, q, patches)
    recv = lax.all_to_all(send, "page", 0, 0, tiled=True)
    page_lse, row, loss, acc = call(
        inner_kernel,
        "inner",
        2 * matmul,
        [SMEM] + [VMEM] * 6,
        [table, table, ((1, BROWS), f32), ((3, width, rows), f32)],
        [turned, table],
    )(page_blocks, page_blocks, live, sign, lse, q, patches)
    parts, full_lse, row_grad = call(
        close_kernel,
        "close",
        matmul,
        [VMEM] * 7,
        [((devices, local + LOSS_ROWS, width), bf16), table, table],
    )(page_blocks, sign, page_lse, row, loss, acc, recv)
    gathered = lax.all_to_all(parts, axes, 0, 0, tiled=True)
    (patch_grad,) = call(
        patch_kernel, "patch", 2 * matmul, [VMEM] * 5, [(patches.shape, f32)], [turned]
    )(live, full_lse, row_grad, q, patches)
    query_grad, loss = call(
        lambda *refs: final_kernel(QUESTION_WORDS / rows, *refs),
        "final",
        devices * local * width,
        [VMEM],
        [((local, width), f32), ((1, BROWS), f32)],
    )(gathered)
    return (patch_grad, query_grad.reshape(queries.shape), loss[0, :1])


def solution(mesh):
    placed = (
        P(("grp", "page"), None, None),
        P(("grp", "page"), None),
        P(("grp", "page"), None),
        P(),
        P(),
    )
    return jax.shard_map(
        shards,
        mesh=mesh,
        in_specs=placed,
        out_specs=(P(("grp", "page"), None), P(("grp", "page"), None, None), P()),
        check_vma=False,
    )
```

time: 68.5 us -> 52.5 us (0.77)
  Pallas kernels: 34.5 us -> 20.5 us
  waiting for transfers between devices: 15.2 us -> 11.9 us
  starting transfers between devices: 13.5 us -> 15.2 us
    pallas_call x5 -> x6, Pallas kernels: 34.5 us -> 20.5 us  [the longest x1 8.21 us: shards(): call(patch_kernel, 'patch', 2 * matmul, [VMEM] * 5, [(patches.shape, f32)...]
    all_to_all x1, waiting for transfers between devices: 4.78 us -> 0.67 us  [shards(): recv = lax.all_to_all(send, 'page', 0, 0, tiled=True)]
    all_to_all x1, waiting for transfers between devices: 0.81 us -> 3.45 us  [shards(): gathered = lax.all_to_all(parts, axes, 0, 0, tiled=True)]
    all_to_all x1, starting transfers between devices: 2.59 us -> 4.36 us  [shards(): gathered = lax.all_to_all(parts, axes, 0, 0, tiled=True)]
    all_to_all x1, waiting for transfers between devices: 9.56 us -> 7.8 us  [shards(): lax.all_to_all(jnp.broadcast_to(local_rows[None], (devices, local, width)...]
    unnamed x9 -> x7, local copies, waits for them, and re-layouts: 2.72 us -> 2.13 us
  transfers between devices with their start and end apart: 3 -> 3, of which waited for: 3 -> 3; matrix products, arithmetic and copies ran while one was open for 1% -> 1% of each run, Pallas kernels for 19% -> 29%
where the time goes in v2:
time: 52.5 us; the launch traced here: 51.9 us
  Pallas kernels  20.5 us (39%)
  starting transfers between devices  15.2 us (29%)
  waiting for transfers between devices  11.9 us (23%)
  local copies, waits for them, and re-layouts  3.62 us (7%)
  between operations  0.68 us (1%)
    pallas_call x1, Pallas kernels, shards(): call(patch_kernel, 'patch', 2 * matmul, [VMEM] * 5, [(patches.shape, f32)...  8.21 us
    all_to_all x1, waiting for transfers between devices, shards(): lax.all_to_all(jnp.broadcast_to(local_rows[None], (devices, local, width)...  7.8 us
    all_to_all x1, starting transfers between devices, shards(): lax.all_to_all(jnp.broadcast_to(local_rows[None], (devices, local, width)...  7.33 us
    pallas_call x1, Pallas kernels, shards(): call(inner_kernel, 'inner', 2 * matmul, [SMEM] + [VMEM] * 6, [table, tabl...  6.3 us
    all_to_all x1, starting transfers between devices, shards(): gathered = lax.all_to_all(parts, axes, 0, 0, tiled=True)  4.36 us
    pallas_call x1, Pallas kernels, shards(): call(stats_kernel, 'stats', matmul, [VMEM] * 4, [table, ((peers, 1, rows...  3.62 us
    all_to_all x1, starting transfers between devices, shards(): recv = lax.all_to_all(send, 'page', 0, 0, tiled=True)  3.56 us
    all_to_all x1, waiting for transfers between devices, shards(): gathered = lax.all_to_all(parts, axes, 0, 0, tiled=True)  3.45 us
  transfers between devices with their start and end apart: 3, of which 3 were waited for; matrix products, arithmetic and copies ran while one was open for 1% of the time, Pallas kernels for 29%

profile of v2, /device:TPU:0, one launch (start us, length us, event | category | flops | bytes accessed | tf_op | source)
XLA Modules:
  0.0 51.9 jit_solution(4426973083421416182)
XLA Ops:
  0.6 0.0 copy-start
  0.6 1.5 %broadcast_in_dim.8 = bf16[32,32,128]{2,1,0:T(8,128)(2,1)} broadcast(bf16[32,128]{1,0:T(8,128)(2,1)} %bitcast.10), dimensions={1,2} | broadcast | bytes 270336 | tf_op jit(solution)/shard_map/broadcast_in_dim | solution.py:300
  2.1 7.3 %all-to-all-start = ((bf16[32,32,128]{2,1,0:T(8,128)(2,1)}), bf16[32,32,128]{2,1,0:T(8,128)(2,1)S(1)}, u32[]{:S(2)}, u32[]{:S(2)}) async-start(bf16[32,32,128]{2,1,0:T(8,128)(2,1)} %broadcast_in_dim.8), calls=%async_computation | async-start | bytes 524288 | tf_op jit(solution)/shard_map/all_to_all | solution.py:299
  9.5 0.8 %copy.8.pb_ref.pbs_ref = s32[16,2]{1,0:T(8,128)S(1)} copy(s32[16,2]{0,1:T(2,128)} %param.7) | data formatting | bytes 256 | tf_op args[2]
  10.2 0.0 copy-start.1
  10.2 0.7 %copy-done.1 = s32[32,64]{1,0:T(8,128)S(1)} copy-done((s32[32,64]{1,0:T(8,128)S(1)}, s32[32,64]{1,0:T(8,128)}, u32[]{:S(2)}) %copy-start.1) | copy-done | bytes 8216
  10.9 0.0 copy-start.2
  10.9 0.7 %copy-done.2 = s32[64]{0:T(128)S(1)} copy-done((s32[64]{0:T(128)S(1)}, s32[64]{0:T(128)}, u32[]{:S(2)}) %copy-start.2) | copy-done | bytes 280
  11.6 0.3 prep.1
  11.9 7.8 %all-to-all-done = bf16[32,32,128]{2,1,0:T(8,128)(2,1)S(1)} async-done(((bf16[32,32,128]{2,1,0:T(8,128)(2,1)}), bf16[32,32,128]{2,1,0:T(8,128)(2,1)S(1)}, u32[]{:S(2)}, u32[]{:S(2)}) %all-to-all-start) | async-done | bytes 262176 | tf_op jit(solution)/shard_map/all_to_all | solution.py:299
  19.7 0.0 copy-done
  19.7 3.6 %stats.1 = (f32[16,1024]{1,0:T(8,128)S(1)}, f32[16,1,1152]{2,1,0:T(1,128)}) custom-call(s32[16,2]{1,0:T(8,128)S(1)} %copy.8.pb_ref.pbs_ref, s32[16,128]{1,0:T(8,128)S(1)} %get-tuple-element.16.live_ref, bf16[1024,128]{1,0:T(8,128)(2,1)S(1)} %bitcast.6, bf16[2048,128]{1,0:T(8,128)(2,1)S(1)} %copy-done), custom_call_target="tpu_custom_call" | custom-call | flops 536870912 | tf_op jit(solution)/shard_map/stats/pallas_call | solution.py:305
  23.3 3.6 %all-to-all-start.1 = ((f32[16,1,1152]{2,1,0:T(1,128)}), f32[16,1,1152]{2,1,0:T(1,128)S(1)}, u32[]{:S(2)}, u32[]{:S(2)}) async-start(f32[16,1,1152]{2,1,0:T(1,128)} %get-tuple-element.23), calls=%async_computation.1 | async-start | bytes 147456 | tf_op jit(solution)/shard_map/all_to_all | solution.py:308
  26.9 6.3 %inner.1 = (f32[16,1024]{1,0:T(8,128)S(1)}, f32[16,1024]{1,0:T(8,128)S(1)}, f32[1,128]{1,0:T(1,128)S(1)}, f32[3,128,1024]{2,1,0:T(8,128)S(1)}) custom-call(s32[16,2]{1,0:T(8,128)S(1)} %copy.8.pb_ref.pbs_ref, s32[16,2]{1,0:T(8,128)S(1)} %copy.8.pb_ref.pbs_ref, s32[16,128]{1,0:T(8,128)S(1)} %get-tuple-element.16.live_ref, ...), custom_call_target="tpu_custom_call" | custom-call | flops 1073741824 | tf_op jit(solution)/shard_map/inner/pallas_call | solution.py:309
  33.2 0.7 %all-to-all-done.1.recv_ref = f32[16,1,1152]{2,1,0:T(1,128)S(1)} async-done(((f32[16,1,1152]{2,1,0:T(1,128)}), f32[16,1,1152]{2,1,0:T(1,128)S(1)}, u32[]{:S(2)}, u32[]{:S(2)}) %all-to-all-start.1) | async-done | bytes 73760 | tf_op jit(solution)/shard_map/all_to_all | solution.py:308
  33.9 1.4 %close.1 = (bf16[32,40,128]{2,1,0:T(8,128)(2,1)}, f32[16,1024]{1,0:T(8,128)S(1)}, f32[16,1024]{1,0:T(8,128)S(1)}) custom-call(s32[16,2]{1,0:T(8,128)S(1)} %copy.8.pb_ref.pbs_ref, f32[16,1024]{1,0:T(8,128)S(1)} %get-tuple-element.17.sign_ref, f32[16,1024]{1,0:T(8,128)S(1)} %get-tuple-element.19.page_ref, f32[16,1024]{1,0:T(8,128)S(1)} %get-tuple-element.20.row_ref, ...), custom_call_target="tpu_custom_call" | custom-call | flops 536870912 | tf_op jit(solution)/shard_map/close/pallas_call | solution.py:317
  35.3 4.4 %all-to-all-start.2 = ((bf16[32,40,128]{2,1,0:T(8,128)(2,1)}), bf16[32,40,128]{2,1,0:T(8,128)(2,1)S(1)}, u32[]{:S(2)}, u32[]{:S(2)}) async-start(bf16[32,40,128]{2,1,0:T(8,128)(2,1)} %get-tuple-element.26), calls=%async_computation.2 | async-start | bytes 655360 | tf_op jit(solution)/shard_map/all_to_all | solution.py:324
  39.6 8.2 %patch.1 = f32[2048,128]{1,0:T(8,128)} custom-call(s32[16,128]{1,0:T(8,128)S(1)} %get-tuple-element.16.live_ref, f32[16,1024]{1,0:T(8,128)S(1)} %get-tuple-element.24.lse_ref, f32[16,1024]{1,0:T(8,128)S(1)} %get-tuple-element.25.row_ref, bf16[1024,128]{1,0:T(8,128)(2,1)S(1)} %bitcast.8, bf16[2048,128]{1,0:T(8,128)(2,1)S(1)} %copy-done), custom_call_target="tpu_custom_call" | custom-call | flops 1073741824 | tf_op jit(solution)/shard_map/patch/pallas_call | solution.py:325
  47.8 3.4 %all-to-all-done.2.refs_0_ = bf16[32,40,128]{2,1,0:T(8,128)(2,1)S(1)} async-done(((bf16[32,40,128]{2,1,0:T(8,128)(2,1)}), bf16[32,40,128]{2,1,0:T(8,128)(2,1)S(1)}, u32[]{:S(2)}, u32[]{:S(2)}) %all-to-all-start.2) | async-done | bytes 327712 | tf_op jit(solution)/shard_map/all_to_all | solution.py:324
  51.3 0.7 %final.1 = (f32[32,128]{1,0:T(8,128)}, f32[1,128]{1,0:T(1,128)}) custom-call(bf16[32,40,128]{2,1,0:T(8,128)(2,1)S(1)} %all-to-all-done.2.refs_0_), custom_call_target="tpu_custom_call" | custom-call | flops 131072 | tf_op jit(solution)/shard_map/final/pallas_call | solution.py:328
Async XLA Ops:
  0.6 19.1 %copy-start = (bf16[2048,128]{1,0:T(8,128)(2,1)S(1)}, bf16[2048,128]{1,0:T(8,128)(2,1)}, u32[]{:S(2)}) copy-start(bf16[2048,128]{1,0:T(8,128)(2,1)} %p_ref.5) | copy-start | bytes 1572868
  2.1 17.6 %all-to-all-start = ((bf16[32,32,128]{2,1,0:T(8,128)(2,1)}), bf16[32,32,128]{2,1,0:T(8,128)(2,1)S(1)}, u32[]{:S(2)}, u32[]{:S(2)}) async-start(bf16[32,32,128]{2,1,0:T(8,128)(2,1)} %broadcast_in_dim.8), calls=%async_computation | async-start | bytes 524288 | tf_op jit(solution)/shard_map/all_to_all | solution.py:299
  10.2 0.7 %copy-start.1 = (s32[32,64]{1,0:T(8,128)S(1)}, s32[32,64]{1,0:T(8,128)}, u32[]{:S(2)}) copy-start(s32[32,64]{1,0:T(8,128)} %lab_ref.1) | copy-start | bytes 24580
  10.9 0.7 %copy-start.2 = (s32[64]{0:T(128)S(1)}, s32[64]{0:T(128)}, u32[]{:S(2)}) copy-start(s32[64]{0:T(128)} %param.8) | copy-start | bytes 772
  23.3 10.5 %all-to-all-start.1 = ((f32[16,1,1152]{2,1,0:T(1,128)}), f32[16,1,1152]{2,1,0:T(1,128)S(1)}, u32[]{:S(2)}, u32[]{:S(2)}) async-start(f32[16,1,1152]{2,1,0:T(1,128)} %get-tuple-element.23), calls=%async_computation.1 | async-start | bytes 147456 | tf_op jit(solution)/shard_map/all_to_all | solution.py:308
  35.3 16.0 %all-to-all-start.2 = ((bf16[32,40,128]{2,1,0:T(8,128)(2,1)}), bf16[32,40,128]{2,1,0:T(8,128)(2,1)S(1)}, u32[]{:S(2)}, u32[]{:S(2)}) async-start(bf16[32,40,128]{2,1,0:T(8,128)(2,1)} %get-tuple-element.26), calls=%async_computation.2 | async-start | bytes 655360 | tf_op jit(solution)/shard_map/all_to_all | solution.py:324

commit v3 on v2

v3 whole, which is shorter than its diff:
```python
import functools

import jax
import jax.numpy as jnp
from jax import lax
from jax.experimental import pallas as pl
from jax.experimental.pallas import tpu as pltpu
from jax.sharding import PartitionSpec as P

QUESTION_WORDS = 32
BROWS = 128

smoothing_divisor = 0.05
logit_scale = 10.0
logit_bias = -4.0
very_low = -1e30
LOG2E = 1.4426950408889634
LN2 = 0.6931471805599453
SCALE2 = LOG2E / smoothing_divisor
CHUNK = 256
LOSS_ROWS = 8
GROUP = 4
INNER_UNROLL = 1
DEAD = -(2.0**93)
INSIDE, HEAD, TAIL = 0, 1, 2

f32 = jnp.float32
bf16 = jnp.bfloat16
VMEM = pl.BlockSpec(memory_space=pltpu.VMEM)
SMEM = pl.BlockSpec(memory_space=pltpu.SMEM)
HBM = pl.BlockSpec(memory_space=pltpu.HBM)


def lse_rows(values, mask):
    peak = jnp.max(jnp.where(mask, values, very_low), axis=0, keepdims=True)
    mass = jnp.sum(jnp.where(mask, jnp.exp2(values - peak), 0.0), axis=0, keepdims=True)
    return peak + jnp.log2(mass)


def add_lse(one, two):
    peak = jnp.maximum(one, two)
    return peak + jnp.log2(jnp.exp2(one - peak) + jnp.exp2(two - peak))


def chosen_row(values, mask):
    return jnp.max(jnp.where(mask, values, very_low), axis=0, keepdims=True)


def three_terms(value):
    high = value.astype(bf16)
    rest = value - high.astype(f32)
    mid = rest.astype(bf16)
    return high, mid, (rest - mid.astype(f32)).astype(bf16)


def block_of(p_ref, slot):
    return p_ref[pl.ds(pl.multiple_of(slot * BROWS, BROWS), BROWS), :]


def masked(z, live_ref, slot):
    rows = lax.broadcasted_iota(jnp.int32, z.shape, 0)
    live = jnp.concatenate([live_ref[pl.ds(slot, 1), :]] * (z.shape[1] // BROWS), axis=1)
    return jnp.where(rows < live, z, DEAD)


def columns(row, count):
    diagonal = lax.broadcasted_iota(jnp.int32, (count, count), 0) == lax.broadcasted_iota(
        jnp.int32, (count, count), 1
    )
    spread = jnp.where(diagonal, jnp.broadcast_to(row, (count, count)), 0).astype(f32)
    return jnp.sum(spread, axis=1, keepdims=True).astype(jnp.int32)


def slot_stats(live_ref, q_ref, p_ref, lse_ref, qt_ref, base):
    slots = lse_ref.shape[0]
    qt_ref[...] = q_ref[...].T

    def one(step, carry):
        start = step * GROUP
        blocks = p_ref[pl.ds(pl.multiple_of(start * BROWS, BROWS), GROUP * BROWS), :]
        for lo in range(0, q_ref.shape[0], CHUNK):
            product = jnp.dot(blocks, qt_ref[:, lo : lo + CHUNK], preferred_element_type=f32)
            for part in range(GROUP):
                slot = start + part
                z = masked(product[part * BROWS : (part + 1) * BROWS], live_ref, slot)
                top = jnp.max(z, axis=0, keepdims=True)
                mass = jnp.sum(jnp.exp2((z - top) * SCALE2), axis=0, keepdims=True)
                lse_ref[pl.ds(slot, 1), base + lo : base + lo + CHUNK] = top * SCALE2 + jnp.log2(mass)
        return carry

    steps = slots // GROUP
    lax.fori_loop(0, steps, one, 0, unroll=steps if q_ref.shape[0] <= 1024 else 1)


def start_kernel(
    pbt_hbm, len_hbm, p_hbm, rows_hbm, spread_ref, live_ref, page_ref, number_ref, p_ref, pbt_ref, len_ref, rows_ref,
    sems,
):
    slots = live_ref.shape[0]
    pairs = ((rows_hbm, rows_ref), (pbt_hbm, pbt_ref), (len_hbm, len_ref), (p_hbm, p_ref))
    copies = [pltpu.make_async_copy(*pair, sems.at[at]) for at, pair in enumerate(pairs)]
    for copy in copies:
        copy.start()
    for copy in copies[:-1]:
        copy.wait()
    spread_ref[...] = jnp.broadcast_to(rows_ref[...][None], spread_ref.shape)
    pages = columns(pbt_ref[0:1, :], slots)
    numbers = columns(pbt_ref[1:2, :], slots)
    page_count = len_ref.shape[1]
    hit = lax.broadcasted_iota(jnp.int32, (slots, page_count), 1) == pages
    length = jnp.sum(jnp.where(hit, len_ref[...], 0).astype(f32), axis=1, keepdims=True)
    live = length.astype(jnp.int32) - numbers * BROWS
    live_ref[...] = jnp.broadcast_to(jnp.where(pages < 0, 0, live), live_ref.shape)
    page_ref[...] = jnp.broadcast_to(pages, page_ref.shape)
    number_ref[...] = jnp.broadcast_to(numbers, number_ref.shape)
    copies[-1].wait()


def own_kernel(live_ref, q_ref, p_ref, lse_ref, qt_ref):
    slot_stats(live_ref, q_ref, p_ref, lse_ref, qt_ref, 0)


def stats_kernel(
    ids_ref, live_ref, own_lse_ref, q_ref, p_ref, lse_ref, send_ref, qt_ref
):
    slots, rows = lse_ref.shape
    half = rows // 2
    lse_ref[:, :half] = own_lse_ref[...]
    slot_stats(live_ref, q_ref, p_ref, lse_ref, qt_ref, half)
    pages = ids_ref[:, 0:1]
    first = pages[0:1]
    last = jnp.max(pages, axis=0, keepdims=True)
    values = lse_ref[...]
    head = lse_rows(values, pages == first)
    tail = lse_rows(values, pages == last)
    mine = lax.axis_index("page")
    for peer in range(send_ref.shape[0]):
        up = peer > mine
        send_ref[peer, :, :rows] = jnp.where(up, tail, head)
        send_ref[peer, :, rows:] = jnp.broadcast_to(jnp.where(up, last, first).astype(f32), (1, 128))


def label_signs(pages, lab_ref, rows, local):
    slots = pages.shape[0]
    queries, page_count = lab_ref.shape
    half = rows // 2
    core = lax.axis_index("page") % 2
    hit = lax.broadcasted_iota(jnp.int32, (slots, page_count), 1) == pages
    picked = lax.dot_general(
        hit.astype(bf16),
        lab_ref[...].astype(bf16),
        (((1,), (1,)), ((), ())),
        preferred_element_type=f32,
    )
    lane = lax.broadcasted_iota(jnp.int32, (queries, rows), 1)
    other = (lane >= half).astype(jnp.int32)
    within = lane - other * half
    device = 2 * (within // local) + (core + other) % 2
    question = device * (local // QUESTION_WORDS) + within % local // QUESTION_WORDS
    spread = (question == lax.broadcasted_iota(jnp.int32, (queries, rows), 0)).astype(bf16)
    return 2.0 * jnp.dot(picked.astype(bf16), spread, preferred_element_type=f32) - 1.0


def gradients(value, sign):
    count, rows = value.shape
    same_group = (
        lax.broadcasted_iota(jnp.int32, (CHUNK, CHUNK), 0) // QUESTION_WORDS
        == lax.broadcasted_iota(jnp.int32, (CHUNK, CHUNK), 1) // QUESTION_WORDS
    ).astype(bf16)
    totals = []
    for lo in range(0, rows, CHUNK):
        total = [
            jnp.dot(term, same_group, preferred_element_type=f32)
            for term in three_terms(value[:, lo : lo + CHUNK])
        ]
        totals.append(total[0] + total[1] + total[2])
    scores = (smoothing_divisor * LN2) * jnp.concatenate(totals, axis=1)
    logits = (logit_scale / QUESTION_WORDS) * scores + logit_bias
    margin = -sign * logits
    small = jnp.exp(-jnp.abs(margin))
    pair = jnp.maximum(margin, 0.0) + jnp.log1p(small)
    sigmoid = jnp.where(margin >= 0.0, 1.0, small) / (1.0 + small)
    return -sign * sigmoid * (logit_scale / QUESTION_WORDS), pair


def inner_kernel(
    local, pbs_ref, ids_ref, number_ref, live_ref, lab_ref, lse_ref, own_ref, oth_ref, p_ref, page_ref,
    row_ref, sign_ref, loss_ref, acc_ref, weight_ref, qt_ref,
):
    slots, rows = lse_ref.shape
    half = rows // 2
    pages = ids_ref[:, 0:1]
    first = pages[0:1]
    last = jnp.max(pages, axis=0, keepdims=True)
    values = lse_ref[...]
    qt_ref[:, :half] = own_ref[...].T
    qt_ref[:, half:] = oth_ref[...].T
    sign_ref[...] = label_signs(pages, lab_ref, rows, local)
    for slot in range(slots):
        page_ref[slot : slot + 1, :] = chosen_row(values, pages == pages[slot : slot + 1])
    peak = page_ref[...]
    square = jnp.broadcast_to(pages, (slots, slots))
    diagonal = lax.broadcasted_iota(jnp.int32, (slots, slots), 0) == lax.broadcasted_iota(
        jnp.int32, (slots, slots), 1
    )
    across = jnp.sum(jnp.where(diagonal, square, 0).astype(f32), axis=0, keepdims=True)
    same_page = (square.astype(f32) == across).astype(bf16)
    mass = [
        jnp.dot(same_page, term, preferred_element_type=f32)
        for term in three_terms(jnp.exp2(values - peak))
    ]
    value = jnp.where(pages >= 0, peak + jnp.log2(mass[0] + mass[1] + mass[2]), 0.0)
    row, pair = gradients(value, sign_ref[...])
    inside = (pages != first) & (pages != last)
    counted = inside & (pages >= 0) & (number_ref[:, 0:1] == 0)
    row_ref[...] = row
    weight_ref[...] = jnp.where(inside, row, 1.0)
    page_ref[...] = value
    loss = jnp.sum(jnp.where(counted, pair, 0.0), axis=0, keepdims=True)
    loss_ref[...] = jnp.broadcast_to(jnp.sum(loss, axis=1, keepdims=True), loss_ref.shape)
    acc_ref[...] = jnp.zeros_like(acc_ref)
    head_page = pbs_ref[0, 0]
    tail_page = head_page
    for slot in range(1, slots):
        tail_page = jnp.maximum(tail_page, pbs_ref[0, slot])

    def one(step, carry):
        start = step * GROUP
        blocks = p_ref[pl.ds(pl.multiple_of(start * BROWS, BROWS), GROUP * BROWS), :]
        kinds, turned = [], []
        for part in range(GROUP):
            page = pbs_ref[0, start + part]
            kinds.append(jnp.where(page == head_page, HEAD, jnp.where(page == tail_page, TAIL, INSIDE)))
            turned.append(blocks[part * BROWS : (part + 1) * BROWS].T)
        for lo in range(0, rows, CHUNK):
            product = jnp.dot(blocks, qt_ref[:, lo : lo + CHUNK], preferred_element_type=f32)
            for part in range(GROUP):
                slot = start + part
                at = pl.ds(slot, 1)
                z = masked(product[part * BROWS : (part + 1) * BROWS], live_ref, slot)
                e = jnp.exp2(z * SCALE2 - page_ref[at, lo : lo + CHUNK])
                coupling = (e * weight_ref[at, lo : lo + CHUNK]).astype(bf16)
                acc_ref[kinds[part], :, lo : lo + CHUNK] += jnp.dot(
                    turned[part], coupling, preferred_element_type=f32
                )
        return carry

    steps = slots // GROUP
    lax.fori_loop(0, steps, one, 0, unroll=INNER_UNROLL if rows <= 1024 else 1)


def close_kernel(
    ids_ref, number_ref, sign_ref, page_ref, row_ref, loss_ref, acc_ref, recv_ref, out_ref, lse_ref, full_ref
):
    slots, rows = page_ref.shape
    peers = recv_ref.shape[0]
    devices = out_ref.shape[0]
    local = rows // devices
    mine = lax.axis_index("page")
    core = mine % 2
    half = rows // 2
    pages = ids_ref[:, 0:1]
    first = pages[0:1]
    last = jnp.max(pages, axis=0, keepdims=True)
    is_first = pages == first
    is_last = pages == last
    alone = first == last

    def gathered(wanted, below):
        parts = []
        for peer in range(peers):
            side = peer < mine if below else peer > mine
            same = (recv_ref[peer, :, rows : rows + 1] == wanted.astype(f32)) & side
            row = recv_ref[peer, :, :rows]
            crossed = jnp.concatenate([row[:, half:], row[:, :half]], axis=1)
            row = jnp.where(peer % 2 == core, row, crossed)
            parts.append(jnp.where(same, row, very_low))
        peak = parts[0]
        for part in parts[1:]:
            peak = jnp.maximum(peak, part)
        mass = jnp.zeros((1, rows), f32)
        for part in parts:
            mass = mass + jnp.where(part > 0.5 * very_low, jnp.exp2(part - peak), 0.0)
        return peak + jnp.log2(jnp.maximum(mass, 1e-30))

    below = gathered(first, True)
    above = gathered(last, False)
    value = page_ref[...]
    head = value[0:1]
    tail = chosen_row(value, is_last)
    head_full = add_lse(head, below)
    head_full = jnp.where(alone, add_lse(head_full, above), head_full)
    tail_full = jnp.where(alone, head_full, add_lse(tail, above))
    both = jnp.concatenate([head_full, tail_full], axis=0)
    sign = sign_ref[...]
    signs = jnp.concatenate([sign[0:1], chosen_row(sign, is_last)], axis=0)
    row, pair = gradients(both, signs)
    starts = number_ref[:, 0:1] == 0
    head_counts = starts[0:1]
    tail_counts = (jnp.max((starts & is_last).astype(jnp.int32), axis=0, keepdims=True) > 0) & jnp.logical_not(alone)
    loss = jnp.sum(
        jnp.where(head_counts, pair[0:1], 0.0) + jnp.where(tail_counts, pair[1:2], 0.0),
        axis=1,
        keepdims=True,
    )
    loss = (loss + loss_ref[...]) * (1.0 / QUESTION_WORDS)
    lse_ref[...] = jnp.where(is_last, tail_full, jnp.where(is_first, head_full, value))
    full_ref[...] = jnp.where(is_last, row[1:2], jnp.where(is_first, row[0:1], row_ref[...]))
    head_scale = row[0:1] * jnp.exp2(head - head_full)
    tail_scale = row[1:2] * jnp.exp2(tail - tail_full)
    for lo in range(0, rows, CHUNK):
        span = slice(lo, lo + CHUNK)
        total = (
            acc_ref[INSIDE, :, span]
            + acc_ref[HEAD, :, span] * head_scale[:, span]
            + acc_ref[TAIL, :, span] * tail_scale[:, span]
        )
        turned = total.T.astype(bf16).reshape(CHUNK // local, local, BROWS)
        other = int(lo >= half)
        for place in range(CHUNK // local):
            chip = (lo - other * half) // local + place
            out_ref[2 * chip + (core + other) % 2, :local, :] = turned[place]
    terms = three_terms(loss)
    zeros = jnp.zeros((LOSS_ROWS - 3, BROWS), f32)
    last_rows = jnp.concatenate([t.astype(f32) for t in terms] + [zeros], axis=0).astype(bf16)
    for device in range(devices):
        out_ref[device, local:, :] = last_rows


def patch_kernel(live_ref, lse_ref, row_ref, own_ref, oth_ref, p_ref, out_ref, qt_ref):
    slots, rows = lse_ref.shape
    half = rows // 2
    qt_ref[:, :half] = own_ref[...].T
    qt_ref[:, half:] = oth_ref[...].T

    def one(step, carry):
        for part in range(2):
            slot = step * 2 + part
            block = block_of(p_ref, slot)
            total = jnp.zeros((BROWS, BROWS), f32)
            for lo in range(0, rows, CHUNK):
                product = jnp.dot(block, qt_ref[:, lo : lo + CHUNK], preferred_element_type=f32)
                z = masked(product, live_ref, slot)
                weights = jnp.exp2(z * SCALE2 - lse_ref[pl.ds(slot, 1), lo : lo + CHUNK])
                coupling = (row_ref[pl.ds(slot, 1), lo : lo + CHUNK] * weights).astype(bf16)
                q_ref, at = (own_ref, lo) if lo < half else (oth_ref, lo - half)
                total = total + jnp.dot(
                    coupling, q_ref[at : at + CHUNK, :], preferred_element_type=f32
                )
            out_ref[pl.ds(pl.multiple_of(slot * BROWS, BROWS), BROWS), :] = total
        return carry

    lax.fori_loop(0, slots // 2, one, 0)


def final_kernel(scale, recv_ref, grad_ref, loss_ref):
    devices, padded, _ = recv_ref.shape
    total = jnp.zeros((padded, BROWS), f32)
    for device in range(devices):
        total = total + recv_ref[device].astype(f32)
    local = padded - LOSS_ROWS
    grad_ref[...] = total[:local]
    loss_ref[...] = (total[local : local + 1] + total[local + 1 : local + 2] + total[local + 2 : local + 3]) * scale


def call(kernel, name, flops, in_specs, shapes, scratch=(), limit=24):
    return pl.pallas_call(
        kernel,
        in_specs=in_specs,
        out_specs=[VMEM] * len(shapes),
        out_shape=[jax.ShapeDtypeStruct(*shape) for shape in shapes],
        scratch_shapes=[pltpu.VMEM(*shape) if isinstance(shape, tuple) else shape for shape in scratch],
        cost_estimate=pl.CostEstimate(flops=flops, bytes_accessed=0, transcendentals=0),
        compiler_params=pltpu.CompilerParams(vmem_limit_bytes=limit << 20),
        name=name,
    )


def shards(queries, patches, page_blocks, lengths, labels):
    axes = ("grp", "page")
    devices = lax.axis_size(axes)
    peers = lax.axis_size("page")
    slots = page_blocks.shape[0]
    width = patches.shape[1]
    local_rows = queries.reshape(-1, width)
    local = local_rows.shape[0]
    rows = local * devices
    matmul = 2 * rows * patches.shape[0] * width
    half = rows // 2
    table = ((slots, rows), f32)
    half_table = ((slots, half), f32)
    ids = ((slots, BROWS), jnp.int32)
    turned_half = ((width, half), bf16)
    limit = 24 if rows <= 1024 else 52
    pbt = page_blocks.T
    same_core = [list(range(core, devices, 2)) for core in range(2)]
    inputs = (pbt, lengths.reshape(1, -1), patches, local_rows)
    spread, live, pages, numbers, p = call(
        start_kernel,
        "start",
        matmul // 4,
        [HBM] * 4,
        [((devices // 2, local, width), bf16), ids, ids, ids, (patches.shape, bf16)],
        [
            (pbt.shape, jnp.int32),
            ((1, lengths.shape[0]), jnp.int32),
            (local_rows.shape, bf16),
            pltpu.SemaphoreType.DMA((4,)),
        ],
    )(*(pltpu.with_memory_space_constraint(x, pltpu.HBM) for x in inputs))
    own = lax.all_to_all(
        spread,
        axes,
        0,
        0,
        axis_index_groups=same_core,
        tiled=True,
    ).reshape(half, width)
    other = lax.ppermute(own, axes, [(i, i ^ 1) for i in range(devices)])
    (own_lse,) = call(
        own_kernel, "own", matmul // 2, [VMEM] * 3, [half_table], [turned_half], limit
    )(live, own, p)
    lse, send = call(
        stats_kernel,
        "stats",
        matmul // 2,
        [VMEM] * 5,
        [table, ((peers, 1, rows + 128), f32)],
        [turned_half],
        limit,
    )(pages, live, own_lse, other, p)
    recv = lax.all_to_all(send, "page", 0, 0, tiled=True)
    page_lse, row, sign, loss, acc = call(
        functools.partial(inner_kernel, local),
        "inner",
        2 * matmul,
        [SMEM] + [VMEM] * 8,
        [table, table, table, ((1, BROWS), f32), ((3, width, rows), f32)],
        [table, ((width, rows), bf16)],
        limit,
    )(pbt, pages, numbers, live, labels, lse, own, other, p)
    parts, full_lse, row_grad = call(
        close_kernel,
        "close",
        matmul,
        [VMEM] * 8,
        [((devices, local + LOSS_ROWS, width), bf16), table, table],
    )(pages, numbers, sign, page_lse, row, loss, acc, recv)
    gathered = lax.all_to_all(parts, axes, 0, 0, tiled=True)
    (patch_grad,) = call(
        patch_kernel, "patch", 2 * matmul, [VMEM] * 6, [(patches.shape, f32)], [((width, rows), bf16)]
    )(live, full_lse, row_grad, own, other, p)
    query_grad, loss = call(
        lambda *refs: final_kernel(QUESTION_WORDS / rows, *refs),
        "final",
        devices * local * width,
        [VMEM],
        [((local, width), f32), ((1, BROWS), f32)],
    )(gathered)
    return (patch_grad, query_grad.reshape(queries.shape), loss[0, :1])


def solution(mesh):
    placed = (
        P(("grp", "page"), None, None),
        P(("grp", "page"), None),
        P(("grp", "page"), None),
        P(),
        P(),
    )
    return jax.shard_map(
        shards,
        mesh=mesh,
        in_specs=placed,
        out_specs=(P(("grp", "page"), None), P(("grp", "page"), None, None), P()),
        check_vma=False,
    )
```

time: 52.5 us -> 49.2 us (0.937)
  blocking collectives: 0 us -> 15.9 us
  starting transfers between devices: 15.2 us -> 6.68 us
  waiting for transfers between devices: 11.9 us -> 5.34 us
  local copies, waits for them, and re-layouts: 3.62 us -> 0.01 us
    all_to_all x0 -> x1, blocking collectives: none -> 15.9 us  [shards(): lax.all_to_all(spread, axes, 0, 0, axis_index_groups=same_core, tiled=True)]
    all_to_all x1 -> x0, waiting for transfers between devices: 7.8 us -> none  [shards(): lax.all_to_all(jnp.broadcast_to(local_rows[None], (devices, local, width)...]
    all_to_all x1 -> x0, starting transfers between devices: 7.33 us -> none  [shards(): lax.all_to_all(jnp.broadcast_to(local_rows[None], (devices, local, width)...]
    unnamed x7 -> x4, local copies, waits for them, and re-layouts: 2.13 us -> 0.01 us
    broadcast_in_dim x1 -> x0, local copies, waits for them, and re-layouts: 1.49 us -> none  [shards(): jnp.broadcast_to(local_rows[None], (devices, local, width))]
    all_to_all x1, waiting for transfers between devices: 0.67 us -> 2.05 us  [shards(): recv = lax.all_to_all(send, 'page', 0, 0, tiled=True)]
    all_to_all x1, starting transfers between devices: 4.36 us -> 3.18 us  [shards(): gathered = lax.all_to_all(parts, axes, 0, 0, tiled=True)]
    pallas_call x5 -> x6, Pallas kernels: 19.8 us -> 19.5 us  [the longest x1 8.37 us: shards(): call(patch_kernel, 'patch', 2 * matmul, [VMEM] * 6, [(patches.shape, f32)...]
  transfers between devices with their start and end apart: 3 -> 3, of which waited for: 3 -> 2; matrix products, arithmetic and copies ran while one was open for 1% -> 0% of each run, Pallas kernels for 29% -> 30%
where the time goes in v3:
time: 49.2 us; the launch traced here: 48.8 us
  Pallas kernels  20.1 us (41%)
  blocking collectives  15.9 us (32%)
  starting transfers between devices  6.68 us (14%)
  waiting for transfers between devices  5.34 us (11%)
  between operations  0.71 us (1%)
    all_to_all x1, blocking collectives, shards(): lax.all_to_all(spread, axes, 0, 0, axis_index_groups=same_core, tiled=True)  15.9 us
    pallas_call x1, Pallas kernels, shards(): call(patch_kernel, 'patch', 2 * matmul, [VMEM] * 6, [(patches.shape, f32)...  8.37 us
    pallas_call x1, Pallas kernels, shards(): call(functools.partial(inner_kernel, local), 'inner', 2 * matmul, [SMEM]...  4.88 us
    all_to_all x1, starting transfers between devices, shards(): recv = lax.all_to_all(send, 'page', 0, 0, tiled=True)  3.5 us
    all_to_all x1, waiting for transfers between devices, shards(): gathered = lax.all_to_all(parts, axes, 0, 0, tiled=True)  3.29 us
    all_to_all x1, starting transfers between devices, shards(): gathered = lax.all_to_all(parts, axes, 0, 0, tiled=True)  3.18 us
    pallas_call x1, Pallas kernels, shards(): call(stats_kernel, 'stats', matmul // 2, [VMEM] * 5, [table, ((peers, 1,...  2.23 us
    all_to_all x1, waiting for transfers between devices, shards(): recv = lax.all_to_all(send, 'page', 0, 0, tiled=True)  2.05 us
  transfers between devices with their start and end apart: 3, of which 2 were waited for; matrix products, arithmetic and copies ran while one was open for 0% of the time, Pallas kernels for 30%

profile of v3, /device:TPU:0, one launch (start us, length us, event | category | flops | bytes accessed | tf_op | source)
XLA Modules:
  0.0 48.8 jit_solution(6665223041646367246)
XLA Ops:
  0.6 0.0 copy-start
  0.6 0.0 copy-start.1
  0.7 1.1 %start.1 = (bf16[16,32,128]{2,1,0:T(8,128)(2,1)S(1)}, s32[16,128]{1,0:T(8,128)S(1)}, s32[16,128]{1,0:T(8,128)S(1)}, s32[16,128]{1,0:T(8,128)S(1)}, bf16[2048,128]{1,0:T(8,128)(2,1)S(1)}) custom-call(s32[2,16]{1,0:T(2,128)} %bitcast.11, s32[1,64]{1,0:T(1,128)} %bitcast.14, bf16[2048,128]{1,0:T(8,128)(2,1)} %p_hbm.1, bf16[32,128]{1,0:T(8,128)(2,1)} %bitcast.13), custom_call_target="tpu_custom_call" | custom-call | flops 134217728 | tf_op jit(solution)/shard_map/start/pallas_call | solution.py:398
  1.8 15.9 %all_to_all.15 = bf16[16,32,128]{2,1,0:T(8,128)(2,1)S(1)} all-to-all(bf16[16,32,128]{2,1,0:T(8,128)(2,1)S(1)} %get-tuple-element.23), channel_id=1, replica_groups={{0,2,4,6,8,10,12,14,16,18,20,22,24,26,28,30},{1,3,5,7,9,11,13,15,17,19,..., dimensions={0} | all-to-all | bytes 262144 | tf_op jit(solution)/shard_map/all_to_all | solution.py:411
  17.7 0.0 collective-permute-start
  17.7 1.5 %own.1.own_lse_ref = f32[16,512]{1,0:T(8,128)S(1)} custom-call(s32[16,128]{1,0:T(8,128)S(1)} %get-tuple-element.20.live_ref, bf16[512,128]{1,0:T(8,128)(2,1)S(1)} %bitcast.8, bf16[2048,128]{1,0:T(8,128)(2,1)S(1)} %get-tuple-element.24.p_ref), custom_call_target="tpu_custom_call" | custom-call | flops 268435456 | tf_op jit(solution)/shard_map/own/pallas_call | solution.py:420
  19.2 0.0 collective-permute-done.q_ref.oth_ref
  19.2 2.2 %stats.1 = (f32[16,1024]{1,0:T(8,128)S(1)}, f32[16,1,1152]{2,1,0:T(1,128)}) custom-call(s32[16,128]{1,0:T(8,128)S(1)} %get-tuple-element.21.ids_ref, s32[16,128]{1,0:T(8,128)S(1)} %get-tuple-element.20.live_ref, f32[16,512]{1,0:T(8,128)S(1)} %own.1.own_lse_ref, bf16[512,128]{1,0:T(8,128)(2,1)S(1)} %collective-permute-done.q_ref.oth_ref, ...), custom_call_target="tpu_custom_call" | custom-call | flops 268435456 | tf_op jit(solution)/shard_map/stats/pallas_call | solution.py:423
  21.5 3.5 %all-to-all-start.1 = ((f32[16,1,1152]{2,1,0:T(1,128)}), f32[16,1,1152]{2,1,0:T(1,128)S(1)}, u32[]{:S(2)}, u32[]{:S(2)}) async-start(f32[16,1,1152]{2,1,0:T(1,128)} %get-tuple-element.31), calls=%async_computation.1 | async-start | bytes 147456 | tf_op jit(solution)/shard_map/all_to_all | solution.py:432
  25.0 0.0 copy-done
  25.0 0.0 copy-done.1
  25.0 4.9 %inner.1 = (f32[16,1024]{1,0:T(8,128)S(1)}, f32[16,1024]{1,0:T(8,128)S(1)}, f32[16,1024]{1,0:T(8,128)S(1)}, f32[1,128]{1,0:T(1,128)S(1)}, f32[3,128,1024]{2,1,0:T(8,128)S(1)}) custom-call(s32[2,16]{1,0:T(2,128)S(1)} %bitcast.12, s32[16,128]{1,0:T(8,128)S(1)} %get-tuple-element.21.ids_ref, s32[16,128]{1,0:T(8,128)S(1)} %get-tuple-element.22.number_ref, ...), custom_call_target="tpu_custom_call" | custom-call | flops 1073741824 | tf_op jit(solution)/shard_map/inner/pallas_call | solution.py:433
  29.9 2.0 %all-to-all-done.1.recv_ref = f32[16,1,1152]{2,1,0:T(1,128)S(1)} async-done(((f32[16,1,1152]{2,1,0:T(1,128)}), f32[16,1,1152]{2,1,0:T(1,128)S(1)}, u32[]{:S(2)}, u32[]{:S(2)}) %all-to-all-start.1) | async-done | bytes 73760 | tf_op jit(solution)/shard_map/all_to_all | solution.py:432
  31.9 1.4 %close.1 = (bf16[32,40,128]{2,1,0:T(8,128)(2,1)}, f32[16,1024]{1,0:T(8,128)S(1)}, f32[16,1024]{1,0:T(8,128)S(1)}) custom-call(s32[16,128]{1,0:T(8,128)S(1)} %get-tuple-element.21.ids_ref, s32[16,128]{1,0:T(8,128)S(1)} %get-tuple-element.22.number_ref, f32[16,1024]{1,0:T(8,128)S(1)} %get-tuple-element.26.sign_ref, f32[16,1024]{1,0:T(8,128)S(1)} %get-tuple-element.27.page_ref, ...), custom_call_target="tpu_custom_call" | custom-call | flops 536870912 | tf_op jit(solution)/shard_map/close/pallas_call | solution.py:442
  33.3 3.2 %all-to-all-start.2 = ((bf16[32,40,128]{2,1,0:T(8,128)(2,1)}), bf16[32,40,128]{2,1,0:T(8,128)(2,1)S(1)}, u32[]{:S(2)}, u32[]{:S(2)}) async-start(bf16[32,40,128]{2,1,0:T(8,128)(2,1)} %get-tuple-element.34), calls=%async_computation.2 | async-start | bytes 655360 | tf_op jit(solution)/shard_map/all_to_all | solution.py:449
  36.5 8.4 %patch.1 = f32[2048,128]{1,0:T(8,128)} custom-call(s32[16,128]{1,0:T(8,128)S(1)} %get-tuple-element.20.live_ref, f32[16,1024]{1,0:T(8,128)S(1)} %get-tuple-element.32.lse_ref, f32[16,1024]{1,0:T(8,128)S(1)} %get-tuple-element.33.row_ref, bf16[512,128]{1,0:T(8,128)(2,1)S(1)} %bitcast.10, bf16[512,128]{1,0:T(8,128)(2,1)S(1)} %collective-permute-done.q_ref.oth_ref, ...), custom_call_target="tpu_custom_call" | custom-call | flops 1073741824 | tf_op jit(solution)/shard_map/patch/pallas_call | solution.py:450
  44.9 3.3 %all-to-all-done.2.refs_0_ = bf16[32,40,128]{2,1,0:T(8,128)(2,1)S(1)} async-done(((bf16[32,40,128]{2,1,0:T(8,128)(2,1)}), bf16[32,40,128]{2,1,0:T(8,128)(2,1)S(1)}, u32[]{:S(2)}, u32[]{:S(2)}) %all-to-all-start.2) | async-done | bytes 327712 | tf_op jit(solution)/shard_map/all_to_all | solution.py:449
  48.2 0.7 %final.1 = (f32[32,128]{1,0:T(8,128)}, f32[1,128]{1,0:T(1,128)}) custom-call(bf16[32,40,128]{2,1,0:T(8,128)(2,1)S(1)} %all-to-all-done.2.refs_0_), custom_call_target="tpu_custom_call" | custom-call | flops 131072 | tf_op jit(solution)/shard_map/final/pallas_call | solution.py:453
Async XLA Ops:
  0.6 24.4 %copy-start = (s32[16,2]{0,1:T(2,128)S(1)}, s32[16,2]{0,1:T(2,128)}, u32[]{:S(2)}) copy-start(s32[16,2]{0,1:T(2,128)} %param.7) | copy-start | bytes 388
  0.6 24.4 %copy-start.1 = (s32[32,64]{1,0:T(8,128)S(1)}, s32[32,64]{1,0:T(8,128)}, u32[]{:S(2)}) copy-start(s32[32,64]{1,0:T(8,128)} %lab_ref.1) | copy-start | bytes 24580
  17.7 1.5 %collective-permute-start = (bf16[512,128]{1,0:T(8,128)(2,1)S(1)}, bf16[512,128]{1,0:T(8,128)(2,1)S(1)}, u32[]{:S(2)}, u32[]{:S(2)}) collective-permute-start(bf16[512,128]{1,0:T(8,128)(2,1)S(1)} %bitcast.7), channel_id=1, source_target_pairs={{0,1},{1,0},{2,3},{3,2},{4,5},{5,4},{6,7},{7,6},{8,9},{9,8},{10,11... | collective-permute-start | bytes 393224 | tf_op jit(solution)/shard_map/ppermute | solution.py:419
  21.5 10.5 %all-to-all-start.1 = ((f32[16,1,1152]{2,1,0:T(1,128)}), f32[16,1,1152]{2,1,0:T(1,128)S(1)}, u32[]{:S(2)}, u32[]{:S(2)}) async-start(f32[16,1,1152]{2,1,0:T(1,128)} %get-tuple-element.31), calls=%async_computation.1 | async-start | bytes 147456 | tf_op jit(solution)/shard_map/all_to_all | solution.py:432
  33.3 14.8 %all-to-all-start.2 = ((bf16[32,40,128]{2,1,0:T(8,128)(2,1)}), bf16[32,40,128]{2,1,0:T(8,128)(2,1)S(1)}, u32[]{:S(2)}, u32[]{:S(2)}) async-start(bf16[32,40,128]{2,1,0:T(8,128)(2,1)} %get-tuple-element.34), calls=%async_computation.2 | async-start | bytes 655360 | tf_op jit(solution)/shard_map/all_to_all | solution.py:449

commit v4 on v3

--- a/solution.py
+++ b/solution.py
@@ -21,6 +21,7 @@
 LOSS_ROWS = 8
 GROUP = 4
 INNER_UNROLL = 1
+PATCH_UNROLL = 1
 DEAD = -(2.0**93)
 INSIDE, HEAD, TAIL = 0, 1, 2
 
@@ -63,6 +64,22 @@
     return jnp.where(rows < live, z, DEAD)
 
 
+def widened(blocks, live_ref, start):
+    rows = lax.broadcasted_iota(jnp.int32, (BROWS, BROWS), 0)
+    dead = [
+        jnp.where(rows < live_ref[pl.ds(start + part, 1), :], 0.0, 1.0).astype(bf16)
+        for part in range(blocks.shape[0] // BROWS)
+    ]
+    return jnp.concatenate([blocks, jnp.concatenate(dead, axis=0)], axis=1)
+
+
+def marked_queries(qt_ref, q_ref):
+    width = q_ref.shape[1]
+    qt_ref[:width, :] = q_ref[...].T
+    rows = lax.broadcasted_iota(jnp.int32, (BROWS, q_ref.shape[0]), 0)
+    qt_ref[width:, :] = jnp.where(rows == 0, DEAD, 0.0).astype(bf16)
+
+
 def columns(row, count):
     diagonal = lax.broadcasted_iota(jnp.int32, (count, count), 0) == lax.broadcasted_iota(
         jnp.int32, (count, count), 1
@@ -73,16 +90,17 @@
 
 def slot_stats(live_ref, q_ref, p_ref, lse_ref, qt_ref, base):
     slots = lse_ref.shape[0]
-    qt_ref[...] = q_ref[...].T
+    marked_queries(qt_ref, q_ref)
 
     def one(step, carry):
         start = step * GROUP
         blocks = p_ref[pl.ds(pl.multiple_of(start * BROWS, BROWS), GROUP * BROWS), :]
+        blocks = widened(blocks, live_ref, start)
         for lo in range(0, q_ref.shape[0], CHUNK):
             product = jnp.dot(blocks, qt_ref[:, lo : lo + CHUNK], preferred_element_type=f32)
             for part in range(GROUP):
                 slot = start + part
-                z = masked(product[part * BROWS : (part + 1) * BROWS], live_ref, slot)
+                z = product[part * BROWS : (part + 1) * BROWS]
                 top = jnp.max(z, axis=0, keepdims=True)
                 mass = jnp.sum(jnp.exp2((z - top) * SCALE2), axis=0, keepdims=True)
                 lse_ref[pl.ds(slot, 1), base + lo : base + lo + CHUNK] = top * SCALE2 + jnp.log2(mass)
@@ -250,12 +268,12 @@
 
 
 def close_kernel(
-    ids_ref, number_ref, sign_ref, page_ref, row_ref, loss_ref, acc_ref, recv_ref, out_ref, lse_ref, full_ref
+    ids_ref, number_ref, sign_ref, page_ref, row_ref, loss_ref, acc_ref, recv_ref, keep_ref, give_ref, lse_ref,
+    full_ref, part_ref,
 ):
     slots, rows = page_ref.shape
     peers = recv_ref.shape[0]
-    devices = out_ref.shape[0]
-    local = rows // devices
+    local = rows // keep_ref.shape[0]
     mine = lax.axis_index("page")
     core = mine % 2
     half = rows // 2
@@ -315,16 +333,25 @@
             + acc_ref[HEAD, :, span] * head_scale[:, span]
             + acc_ref[TAIL, :, span] * tail_scale[:, span]
         )
-        turned = total.T.astype(bf16).reshape(CHUNK // local, local, BROWS)
+        turned = total.T.reshape(CHUNK // local, 2, local // 2, BROWS)
         other = int(lo >= half)
         for place in range(CHUNK // local):
             chip = (lo - other * half) // local + place
-            out_ref[2 * chip + (core + other) % 2, :local, :] = turned[place]
-    terms = three_terms(loss)
+            target = 2 * chip + (core + other) % 2
+            keep_ref[target] = jnp.where(core == 0, turned[place, 0], turned[place, 1])
+            give_ref[target] = jnp.where(core == 0, turned[place, 1], turned[place, 0]).astype(bf16)
+    part_ref[...] = loss
+
+
+def join_kernel(keep_ref, give_ref, part_ref, row_ref, out_ref, again_ref):
+    devices, count, _ = keep_ref.shape
+    again_ref[...] = row_ref[...]
+    terms = three_terms(part_ref[...])
     zeros = jnp.zeros((LOSS_ROWS - 3, BROWS), f32)
     last_rows = jnp.concatenate([t.astype(f32) for t in terms] + [zeros], axis=0).astype(bf16)
     for device in range(devices):
-        out_ref[device, local:, :] = last_rows
+        out_ref[device, :count, :] = (keep_ref[device] + give_ref[device].astype(f32)).astype(bf16)
+        out_ref[device, count:, :] = last_rows
 
 
 def patch_kernel(live_ref, lse_ref, row_ref, own_ref, oth_ref, p_ref, out_ref, qt_ref):
@@ -334,33 +361,39 @@
     qt_ref[:, half:] = oth_ref[...].T
 
     def one(step, carry):
-        for part in range(2):
-            slot = step * 2 + part
-            block = block_of(p_ref, slot)
-            total = jnp.zeros((BROWS, BROWS), f32)
-            for lo in range(0, rows, CHUNK):
-                product = jnp.dot(block, qt_ref[:, lo : lo + CHUNK], preferred_element_type=f32)
-                z = masked(product, live_ref, slot)
-                weights = jnp.exp2(z * SCALE2 - lse_ref[pl.ds(slot, 1), lo : lo + CHUNK])
-                coupling = (row_ref[pl.ds(slot, 1), lo : lo + CHUNK] * weights).astype(bf16)
-                q_ref, at = (own_ref, lo) if lo < half else (oth_ref, lo - half)
-                total = total + jnp.dot(
-                    coupling, q_ref[at : at + CHUNK, :], preferred_element_type=f32
-                )
-            out_ref[pl.ds(pl.multiple_of(slot * BROWS, BROWS), BROWS), :] = total
+        start = step * GROUP
+        span = pl.ds(pl.multiple_of(start * BROWS, BROWS), GROUP * BROWS)
+        blocks = p_ref[span, :]
+        total = jnp.zeros((GROUP * BROWS, BROWS), f32)
+        for lo in range(0, rows, CHUNK):
+            product = jnp.dot(blocks, qt_ref[:, lo : lo + CHUNK], preferred_element_type=f32)
+            couplings = []
+            for part in range(GROUP):
+                at = pl.ds(start + part, 1)
+                z = masked(product[part * BROWS : (part + 1) * BROWS], live_ref, start + part)
+                weights = jnp.exp2(z * SCALE2 - lse_ref[at, lo : lo + CHUNK])
+                couplings.append((row_ref[at, lo : lo + CHUNK] * weights).astype(bf16))
+            q_ref, at = (own_ref, lo) if lo < half else (oth_ref, lo - half)
+            total = total + jnp.dot(
+                jnp.concatenate(couplings, axis=0), q_ref[at : at + CHUNK, :], preferred_element_type=f32
+            )
+        out_ref[span, :] = total
         return carry
 
-    lax.fori_loop(0, slots // 2, one, 0)
+    steps = slots // GROUP
+    lax.fori_loop(0, steps, one, 0, unroll=PATCH_UNROLL if rows <= 1024 else 1)
 
 
 def final_kernel(scale, recv_ref, grad_ref, loss_ref):
     devices, padded, _ = recv_ref.shape
-    total = jnp.zeros((padded, BROWS), f32)
+    count = padded - LOSS_ROWS
+    totals = [jnp.zeros((padded, BROWS), f32)] * 2
     for device in range(devices):
-        total = total + recv_ref[device].astype(f32)
-    local = padded - LOSS_ROWS
-    grad_ref[...] = total[:local]
-    loss_ref[...] = (total[local : local + 1] + total[local + 1 : local + 2] + total[local + 2 : local + 3]) * scale
+        totals[device % 2] = totals[device % 2] + recv_ref[device].astype(f32)
+    grad_ref[:count, :] = totals[0][:count]
+    grad_ref[count:, :] = totals[1][:count]
+    both = totals[0][count:] + totals[1][count:]
+    loss_ref[...] = (both[0:1] + both[1:2] + both[2:3]) * scale
 
 
 def call(kernel, name, flops, in_specs, shapes, scratch=(), limit=24):
@@ -390,7 +423,7 @@
     table = ((slots, rows), f32)
     half_table = ((slots, half), f32)
     ids = ((slots, BROWS), jnp.int32)
-    turned_half = ((width, half), bf16)
+    turned_half = ((width + BROWS, half), bf16)
     limit = 24 if rows <= 1024 else 52
     pbt = page_blocks.T
     same_core = [list(range(core, devices, 2)) for core in range(2)]
@@ -439,13 +472,27 @@
         [table, ((width, rows), bf16)],
         limit,
     )(pbt, pages, numbers, live, labels, lse, own, other, p)
-    parts, full_lse, row_grad = call(
+    keep, give, full_lse, row_grad, part = call(
         close_kernel,
         "close",
         matmul,
         [VMEM] * 8,
-        [((devices, local + LOSS_ROWS, width), bf16), table, table],
+        [
+            ((devices, local // 2, width), f32),
+            ((devices, local // 2, width), bf16),
+            table,
+            table,
+            ((1, BROWS), f32),
+        ],
     )(pages, numbers, sign, page_lse, row, loss, acc, recv)
+    give = lax.ppermute(give, axes, [(i, i ^ 1) for i in range(devices)])
+    parts, row_grad = call(
+        join_kernel,
+        "join",
+        matmul // 8,
+        [VMEM] * 4,
+        [((devices, local // 2 + LOSS_ROWS, width), bf16), table],
+    )(keep, give, part, row_grad)
     gathered = lax.all_to_all(parts, axes, 0, 0, tiled=True)
     (patch_grad,) = call(
         patch_kernel, "patch", 2 * matmul, [VMEM] * 6, [(patches.shape, f32)], [((width, rows), bf16)]

time: 49.2 us -> 47.7 us (0.970)
  Pallas kernels: 20.1 us -> 16.1 us
  waiting for transfers between devices: 5.34 us -> 7.82 us
    pallas_call x1, Pallas kernels: 8.37 us -> 4.52 us  [shards(): call(patch_kernel, 'patch', 2 * matmul, [VMEM] * 6, [(patches.shape, f32)...]
    ppermute x0 -> x1, waiting for transfers between devices: none -> 1.33 us  [shards(): give = lax.ppermute(give, axes, [(i, i ^ 1) for i in range(devices)])]
    all_to_all x1, waiting for transfers between devices: 3.29 us -> 4.43 us  [shards(): gathered = lax.all_to_all(parts, axes, 0, 0, tiled=True)]
    pallas_call x1 -> x2, Pallas kernels: 1.38 us -> 1.4 us  [the longest x1 0.71 us: shards(): call(join_kernel, 'join', matmul // 8, [VMEM] * 4, [((devices, local // 2...]
  transfers between devices with their start and end apart: 3 -> 4, of which waited for: 2 -> 3; matrix products, arithmetic and copies ran while one was open for 0% -> 0% of each run, Pallas kernels for 30% -> 23%
where the time goes in v4:
time: 47.7 us; the launch traced here: 47.3 us
  Pallas kernels  16.1 us (34%)
  blocking collectives  15.9 us (33%)
  waiting for transfers between devices  7.82 us (16%)
  starting transfers between devices  6.75 us (14%)
  between operations  0.72 us (2%)
    all_to_all x1, blocking collectives, shards(): lax.all_to_all(spread, axes, 0, 0, axis_index_groups=same_core, tiled=True)  15.9 us
    pallas_call x1, Pallas kernels, shards(): call(functools.partial(inner_kernel, local), 'inner', 2 * matmul, [SMEM]...  4.87 us
    pallas_call x1, Pallas kernels, shards(): call(patch_kernel, 'patch', 2 * matmul, [VMEM] * 6, [(patches.shape, f32)...  4.52 us
    all_to_all x1, waiting for transfers between devices, shards(): gathered = lax.all_to_all(parts, axes, 0, 0, tiled=True)  4.43 us
    all_to_all x1, starting transfers between devices, shards(): recv = lax.all_to_all(send, 'page', 0, 0, tiled=True)  3.5 us
    all_to_all x1, starting transfers between devices, shards(): gathered = lax.all_to_all(parts, axes, 0, 0, tiled=True)  3.17 us
    pallas_call x1, Pallas kernels, shards(): call(stats_kernel, 'stats', matmul // 2, [VMEM] * 5, [table, ((peers, 1,...  2.12 us
    all_to_all x1, waiting for transfers between devices, shards(): recv = lax.all_to_all(send, 'page', 0, 0, tiled=True)  2.05 us
  transfers between devices with their start and end apart: 4, of which 3 were waited for; matrix products, arithmetic and copies ran while one was open for 0% of the time, Pallas kernels for 23%

profile of v4, /device:TPU:0, one launch (start us, length us, event | category | flops | bytes accessed | tf_op | source)
XLA Modules:
  0.0 47.3 jit_solution(8755902081113988050)
XLA Ops:
  0.6 0.0 copy-start
  0.6 0.0 copy-start.1
  0.7 1.1 %start.1 = (bf16[16,32,128]{2,1,0:T(8,128)(2,1)S(1)}, s32[16,128]{1,0:T(8,128)S(1)}, s32[16,128]{1,0:T(8,128)S(1)}, s32[16,128]{1,0:T(8,128)S(1)}, bf16[2048,128]{1,0:T(8,128)(2,1)S(1)}) custom-call(s32[2,16]{1,0:T(2,128)} %bitcast.11, s32[1,64]{1,0:T(1,128)} %bitcast.14, bf16[2048,128]{1,0:T(8,128)(2,1)} %p_hbm.1, bf16[32,128]{1,0:T(8,128)(2,1)} %bitcast.13), custom_call_target="tpu_custom_call" | custom-call | flops 134217728 | tf_op jit(solution)/shard_map/start/pallas_call | solution.py:431
  1.8 15.9 %all_to_all.15 = bf16[16,32,128]{2,1,0:T(8,128)(2,1)S(1)} all-to-all(bf16[16,32,128]{2,1,0:T(8,128)(2,1)S(1)} %get-tuple-element.27), channel_id=1, replica_groups={{0,2,4,6,8,10,12,14,16,18,20,22,24,26,28,30},{1,3,5,7,9,11,13,15,17,19,..., dimensions={0} | all-to-all | bytes 262144 | tf_op jit(solution)/shard_map/all_to_all | solution.py:444
  17.7 0.0 collective-permute-start
  17.7 1.4 %own.1.own_lse_ref = f32[16,512]{1,0:T(8,128)S(1)} custom-call(s32[16,128]{1,0:T(8,128)S(1)} %get-tuple-element.24.live_ref, bf16[512,128]{1,0:T(8,128)(2,1)S(1)} %bitcast.8, bf16[2048,128]{1,0:T(8,128)(2,1)S(1)} %get-tuple-element.28.p_ref), custom_call_target="tpu_custom_call" | custom-call | flops 268435456 | tf_op jit(solution)/shard_map/own/pallas_call | solution.py:453
  19.1 0.0 collective-permute-done.q_ref.oth_ref
  19.1 2.1 %stats.1 = (f32[16,1024]{1,0:T(8,128)S(1)}, f32[16,1,1152]{2,1,0:T(1,128)}) custom-call(s32[16,128]{1,0:T(8,128)S(1)} %get-tuple-element.25.ids_ref, s32[16,128]{1,0:T(8,128)S(1)} %get-tuple-element.24.live_ref, f32[16,512]{1,0:T(8,128)S(1)} %own.1.own_lse_ref, bf16[512,128]{1,0:T(8,128)(2,1)S(1)} %collective-permute-done.q_ref.oth_ref, ...), custom_call_target="tpu_custom_call" | custom-call | flops 268435456 | tf_op jit(solution)/shard_map/stats/pallas_call | solution.py:456
  21.2 3.5 %all-to-all-start.1 = ((f32[16,1,1152]{2,1,0:T(1,128)}), f32[16,1,1152]{2,1,0:T(1,128)S(1)}, u32[]{:S(2)}, u32[]{:S(2)}) async-start(f32[16,1,1152]{2,1,0:T(1,128)} %get-tuple-element.35), calls=%async_computation.1 | async-start | bytes 147456 | tf_op jit(solution)/shard_map/all_to_all | solution.py:465
  24.8 0.0 copy-done
  24.8 0.0 copy-done.1
  24.8 4.9 %inner.1 = (f32[16,1024]{1,0:T(8,128)S(1)}, f32[16,1024]{1,0:T(8,128)S(1)}, f32[16,1024]{1,0:T(8,128)S(1)}, f32[1,128]{1,0:T(1,128)S(1)}, f32[3,128,1024]{2,1,0:T(8,128)S(1)}) custom-call(s32[2,16]{1,0:T(2,128)S(1)} %bitcast.12, s32[16,128]{1,0:T(8,128)S(1)} %get-tuple-element.25.ids_ref, s32[16,128]{1,0:T(8,128)S(1)} %get-tuple-element.26.number_ref, ...), custom_call_target="tpu_custom_call" | custom-call | flops 1073741824 | tf_op jit(solution)/shard_map/inner/pallas_call | solution.py:466
  29.7 2.0 %all-to-all-done.1.recv_ref = f32[16,1,1152]{2,1,0:T(1,128)S(1)} async-done(((f32[16,1,1152]{2,1,0:T(1,128)}), f32[16,1,1152]{2,1,0:T(1,128)S(1)}, u32[]{:S(2)}, u32[]{:S(2)}) %all-to-all-start.1) | async-done | bytes 73760 | tf_op jit(solution)/shard_map/all_to_all | solution.py:465
  31.7 0.7 %close.1 = (f32[32,16,128]{2,1,0:T(8,128)S(1)}, bf16[32,16,128]{2,1,0:T(8,128)(2,1)S(1)}, f32[16,1024]{1,0:T(8,128)S(1)}, f32[16,1024]{1,0:T(8,128)S(1)}, f32[1,128]{1,0:T(1,128)S(1)}) custom-call(s32[16,128]{1,0:T(8,128)S(1)} %get-tuple-element.25.ids_ref, s32[16,128]{1,0:T(8,128)S(1)} %get-tuple-element.26.number_ref, ...), custom_call_target="tpu_custom_call" | custom-call | flops 536870912 | tf_op jit(solution)/shard_map/close/pallas_call | solution.py:475
  32.4 0.1 collective-permute-start.1
  32.5 1.3 %collective-permute-done.1.give_ref = bf16[32,16,128]{2,1,0:T(8,128)(2,1)S(1)} collective-permute-done((bf16[32,16,128]{2,1,0:T(8,128)(2,1)S(1)}, bf16[32,16,128]{2,1,0:T(8,128)(2,1)S(1)}, u32[]{:S(2)}, u32[]{:S(2)}) %collective-permute-start.1) | collective-permute-done | bytes 131104 | tf_op jit(solution)/shard_map/ppermute | solution.py:488
  33.8 0.7 %join.1 = (bf16[32,24,128]{2,1,0:T(8,128)(2,1)}, f32[16,1024]{1,0:T(8,128)S(1)}) custom-call(f32[32,16,128]{2,1,0:T(8,128)S(1)} %get-tuple-element.37.keep_ref, bf16[32,16,128]{2,1,0:T(8,128)(2,1)S(1)} %collective-permute-done.1.give_ref, f32[1,128]{1,0:T(1,128)S(1)} %get-tuple-element.39.part_ref, f32[16,1024]{1,0:T(8,128)S(1)} %get-tuple-element.40.row_ref), custom_call_target="tpu_custom_call" | custom-call | flops 67108864 | tf_op jit(solution)/shard_map/join/pallas_call | solution.py:489
  34.5 3.2 %all-to-all-start.2 = ((bf16[32,24,128]{2,1,0:T(8,128)(2,1)}), bf16[32,24,128]{2,1,0:T(8,128)(2,1)S(1)}, u32[]{:S(2)}, u32[]{:S(2)}) async-start(bf16[32,24,128]{2,1,0:T(8,128)(2,1)} %get-tuple-element.42), calls=%async_computation.2 | async-start | bytes 393216 | tf_op jit(solution)/shard_map/all_to_all | solution.py:496
  37.7 4.5 %patch.1 = f32[2048,128]{1,0:T(8,128)} custom-call(s32[16,128]{1,0:T(8,128)S(1)} %get-tuple-element.24.live_ref, f32[16,1024]{1,0:T(8,128)S(1)} %get-tuple-element.36.lse_ref, f32[16,1024]{1,0:T(8,128)S(1)} %get-tuple-element.41.row_ref, bf16[512,128]{1,0:T(8,128)(2,1)S(1)} %bitcast.10, bf16[512,128]{1,0:T(8,128)(2,1)S(1)} %collective-permute-done.q_ref.oth_ref, ...), custom_call_target="tpu_custom_call" | custom-call | flops 1073741824 | tf_op jit(solution)/shard_map/patch/pallas_call | solution.py:497
  42.2 4.4 %all-to-all-done.2.refs_0_ = bf16[32,24,128]{2,1,0:T(8,128)(2,1)S(1)} async-done(((bf16[32,24,128]{2,1,0:T(8,128)(2,1)}), bf16[32,24,128]{2,1,0:T(8,128)(2,1)S(1)}, u32[]{:S(2)}, u32[]{:S(2)}) %all-to-all-start.2) | async-done | bytes 196640 | tf_op jit(solution)/shard_map/all_to_all | solution.py:496
  46.7 0.6 %final.1 = (f32[32,128]{1,0:T(8,128)}, f32[1,128]{1,0:T(1,128)}) custom-call(bf16[32,24,128]{2,1,0:T(8,128)(2,1)S(1)} %all-to-all-done.2.refs_0_), custom_call_target="tpu_custom_call" | custom-call | flops 131072 | tf_op jit(solution)/shard_map/final/pallas_call | solution.py:500
Async XLA Ops:
  0.6 24.1 %copy-start = (s32[16,2]{0,1:T(2,128)S(1)}, s32[16,2]{0,1:T(2,128)}, u32[]{:S(2)}) copy-start(s32[16,2]{0,1:T(2,128)} %param.7) | copy-start | bytes 388
  0.6 24.1 %copy-start.1 = (s32[32,64]{1,0:T(8,128)S(1)}, s32[32,64]{1,0:T(8,128)}, u32[]{:S(2)}) copy-start(s32[32,64]{1,0:T(8,128)} %lab_ref.1) | copy-start | bytes 24580
  17.7 1.4 %collective-permute-start = (bf16[512,128]{1,0:T(8,128)(2,1)S(1)}, bf16[512,128]{1,0:T(8,128)(2,1)S(1)}, u32[]{:S(2)}, u32[]{:S(2)}) collective-permute-start(bf16[512,128]{1,0:T(8,128)(2,1)S(1)} %bitcast.7), channel_id=1, source_target_pairs={{0,1},{1,0},{2,3},{3,2},{4,5},{5,4},{6,7},{7,6},{8,9},{9,8},{10,11... | collective-permute-start | bytes 393224 | tf_op jit(solution)/shard_map/ppermute | solution.py:452
  21.2 10.5 %all-to-all-start.1 = ((f32[16,1,1152]{2,1,0:T(1,128)}), f32[16,1,1152]{2,1,0:T(1,128)S(1)}, u32[]{:S(2)}, u32[]{:S(2)}) async-start(f32[16,1,1152]{2,1,0:T(1,128)} %get-tuple-element.35), calls=%async_computation.1 | async-start | bytes 147456 | tf_op jit(solution)/shard_map/all_to_all | solution.py:465
  32.4 1.4 %collective-permute-start.1 = (bf16[32,16,128]{2,1,0:T(8,128)(2,1)S(1)}, bf16[32,16,128]{2,1,0:T(8,128)(2,1)S(1)}, u32[]{:S(2)}, u32[]{:S(2)}) collective-permute-start(bf16[32,16,128]{2,1,0:T(8,128)(2,1)S(1)} %get-tuple-element.38), channel_id=1, source_target_pairs={{0,1},{1,0},{2,3},{3,2},{4,5},{5,4},{6,7},{7,6},{8,9},{9,8},{10,11... | collective-permute-start | bytes 393224 | tf_op jit(solution)/shard_map/ppermute | solution.py:488
  34.5 12.1 %all-to-all-start.2 = ((bf16[32,24,128]{2,1,0:T(8,128)(2,1)}), bf16[32,24,128]{2,1,0:T(8,128)(2,1)S(1)}, u32[]{:S(2)}, u32[]{:S(2)}) async-start(bf16[32,24,128]{2,1,0:T(8,128)(2,1)} %get-tuple-element.42), calls=%async_computation.2 | async-start | bytes 393216 | tf_op jit(solution)/shard_map/all_to_all | solution.py:496

commit v5 on v4

--- a/solution.py
+++ b/solution.py
@@ -1,5 +1,3 @@
-import functools
-
 import jax
 import jax.numpy as jnp
 from jax import lax
@@ -8,6 +6,7 @@
 from jax.sharding import PartitionSpec as P
 
 QUESTION_WORDS = 32
+HALF_WORDS = QUESTION_WORDS // 2
 BROWS = 128
 
 smoothing_divisor = 0.05
@@ -18,7 +17,7 @@
 LN2 = 0.6931471805599453
 SCALE2 = LOG2E / smoothing_divisor
 CHUNK = 256
-LOSS_ROWS = 8
+LOW_LANES = 64
 GROUP = 4
 INNER_UNROLL = 1
 PATCH_UNROLL = 1
@@ -111,8 +110,8 @@
 
 
 def start_kernel(
-    pbt_hbm, len_hbm, p_hbm, rows_hbm, spread_ref, live_ref, page_ref, number_ref, p_ref, pbt_ref, len_ref, rows_ref,
-    sems,
+    rows_hbm, pbt_hbm, len_hbm, p_hbm, spread_ref, live_ref, page_ref, number_ref, p_ref, rows_ref, pbt_ref,
+    len_ref, sems,
 ):
     slots = live_ref.shape[0]
     pairs = ((rows_hbm, rows_ref), (pbt_hbm, pbt_ref), (len_hbm, len_ref), (p_hbm, p_ref))
@@ -158,11 +157,10 @@
         send_ref[peer, :, rows:] = jnp.broadcast_to(jnp.where(up, last, first).astype(f32), (1, 128))
 
 
-def label_signs(pages, lab_ref, rows, local):
+def label_signs(pages, lab_ref, rows):
     slots = pages.shape[0]
     queries, page_count = lab_ref.shape
     half = rows // 2
-    core = lax.axis_index("page") % 2
     hit = lax.broadcasted_iota(jnp.int32, (slots, page_count), 1) == pages
     picked = lax.dot_general(
         hit.astype(bf16),
@@ -171,27 +169,27 @@
         preferred_element_type=f32,
     )
     lane = lax.broadcasted_iota(jnp.int32, (queries, rows), 1)
-    other = (lane >= half).astype(jnp.int32)
-    within = lane - other * half
-    device = 2 * (within // local) + (core + other) % 2
-    question = device * (local // QUESTION_WORDS) + within % local // QUESTION_WORDS
+    question = (lane - jnp.where(lane >= half, half, 0)) // HALF_WORDS
     spread = (question == lax.broadcasted_iota(jnp.int32, (queries, rows), 0)).astype(bf16)
     return 2.0 * jnp.dot(picked.astype(bf16), spread, preferred_element_type=f32) - 1.0
 
 
 def gradients(value, sign):
     count, rows = value.shape
+    half = rows // 2
     same_group = (
-        lax.broadcasted_iota(jnp.int32, (CHUNK, CHUNK), 0) // QUESTION_WORDS
-        == lax.broadcasted_iota(jnp.int32, (CHUNK, CHUNK), 1) // QUESTION_WORDS
+        lax.broadcasted_iota(jnp.int32, (CHUNK, CHUNK), 0) // HALF_WORDS
+        == lax.broadcasted_iota(jnp.int32, (CHUNK, CHUNK), 1) // HALF_WORDS
     ).astype(bf16)
     totals = []
-    for lo in range(0, rows, CHUNK):
+    for lo in range(0, half, CHUNK):
         total = [
             jnp.dot(term, same_group, preferred_element_type=f32)
-            for term in three_terms(value[:, lo : lo + CHUNK])
+            for at in (lo, half + lo)
+            for term in three_terms(value[:, at : at + CHUNK])
         ]
-        totals.append(total[0] + total[1] + total[2])
+        totals.append(total[0] + total[1] + total[2] + (total[3] + total[4] + total[5]))
+    totals = totals + totals
     scores = (smoothing_divisor * LN2) * jnp.concatenate(totals, axis=1)
     logits = (logit_scale / QUESTION_WORDS) * scores + logit_bias
     margin = -sign * logits
@@ -202,7 +200,7 @@
 
 
 def inner_kernel(
-    local, pbs_ref, ids_ref, number_ref, live_ref, lab_ref, lse_ref, own_ref, oth_ref, p_ref, page_ref,
+    pbs_ref, ids_ref, number_ref, live_ref, lab_ref, lse_ref, own_ref, oth_ref, p_ref, page_ref,
     row_ref, sign_ref, loss_ref, acc_ref, weight_ref, qt_ref,
 ):
     slots, rows = lse_ref.shape
@@ -213,7 +211,7 @@
     values = lse_ref[...]
     qt_ref[:, :half] = own_ref[...].T
     qt_ref[:, half:] = oth_ref[...].T
-    sign_ref[...] = label_signs(pages, lab_ref, rows, local)
+    sign_ref[...] = label_signs(pages, lab_ref, rows)
     for slot in range(slots):
         page_ref[slot : slot + 1, :] = chosen_row(values, pages == pages[slot : slot + 1])
     peak = page_ref[...]
@@ -273,7 +271,6 @@
 ):
     slots, rows = page_ref.shape
     peers = recv_ref.shape[0]
-    local = rows // keep_ref.shape[0]
     mine = lax.axis_index("page")
     core = mine % 2
     half = rows // 2
@@ -333,25 +330,23 @@
             + acc_ref[HEAD, :, span] * head_scale[:, span]
             + acc_ref[TAIL, :, span] * tail_scale[:, span]
         )
-        turned = total.T.reshape(CHUNK // local, 2, local // 2, BROWS)
-        other = int(lo >= half)
-        for place in range(CHUNK // local):
-            chip = (lo - other * half) // local + place
-            target = 2 * chip + (core + other) % 2
-            keep_ref[target] = jnp.where(core == 0, turned[place, 0], turned[place, 1])
-            give_ref[target] = jnp.where(core == 0, turned[place, 1], turned[place, 0]).astype(bf16)
+        side, at = (keep_ref, lo) if lo < half else (give_ref, lo - half)
+        side[at : at + CHUNK, :] = total.T
     part_ref[...] = loss
 
 
 def join_kernel(keep_ref, give_ref, part_ref, row_ref, out_ref, again_ref):
-    devices, count, _ = keep_ref.shape
+    devices, pairs = out_ref.shape[0], out_ref.shape[1] - 1
     again_ref[...] = row_ref[...]
-    terms = three_terms(part_ref[...])
-    zeros = jnp.zeros((LOSS_ROWS - 3, BROWS), f32)
-    last_rows = jnp.concatenate([t.astype(f32) for t in terms] + [zeros], axis=0).astype(bf16)
+    high, mid, low = (term.astype(f32) for term in three_terms(part_ref[...]))
+    lane = lax.broadcasted_iota(jnp.int32, (1, BROWS), 1)
+    loss = jnp.concatenate([jnp.where(lane < LOW_LANES, high, mid), low], axis=0).astype(bf16)
     for device in range(devices):
-        out_ref[device, :count, :] = (keep_ref[device] + give_ref[device].astype(f32)).astype(bf16)
-        out_ref[device, count:, :] = last_rows
+        base = device * 2 * pairs
+        total = keep_ref[base : base + 2 * pairs, :] + give_ref[base : base + 2 * pairs, :]
+        for pair in range(pairs):
+            out_ref[device, pair] = total[2 * pair : 2 * pair + 2].astype(bf16)
+        out_ref[device, pairs] = loss
 
 
 def patch_kernel(live_ref, lse_ref, row_ref, own_ref, oth_ref, p_ref, out_ref, qt_ref):
@@ -385,15 +380,17 @@
 
 
 def final_kernel(scale, recv_ref, grad_ref, loss_ref):
-    devices, padded, _ = recv_ref.shape
-    count = padded - LOSS_ROWS
-    totals = [jnp.zeros((padded, BROWS), f32)] * 2
+    devices, pairs = recv_ref.shape[0], recv_ref.shape[1] - 1
+    totals = [jnp.zeros((pairs + 1, 2, BROWS), f32)] * 2
     for device in range(devices):
         totals[device % 2] = totals[device % 2] + recv_ref[device].astype(f32)
-    grad_ref[:count, :] = totals[0][:count]
-    grad_ref[count:, :] = totals[1][:count]
-    both = totals[0][count:] + totals[1][count:]
-    loss_ref[...] = (both[0:1] + both[1:2] + both[2:3]) * scale
+    each = HALF_WORDS // 2
+    for core in range(2):
+        for pair in range(pairs):
+            at = pair % each * 2
+            grad_ref[pair // each, core, at : at + 2, :] = totals[core][pair]
+    both = totals[0][pairs] + totals[1][pairs]
+    loss_ref[...] = (both[0:1, :1] + both[0:1, LOW_LANES : LOW_LANES + 1] + both[1:2]) * scale
 
 
 def call(kernel, name, flops, in_specs, shapes, scratch=(), limit=24):
@@ -426,30 +423,27 @@
     turned_half = ((width + BROWS, half), bf16)
     limit = 24 if rows <= 1024 else 52
     pbt = page_blocks.T
-    same_core = [list(range(core, devices, 2)) for core in range(2)]
-    inputs = (pbt, lengths.reshape(1, -1), patches, local_rows)
+    questions = local // QUESTION_WORDS
+    halves = local_rows.reshape(questions, 2, HALF_WORDS, width).swapaxes(0, 1).reshape(2, local // 2, width)
+    inputs = (halves, page_blocks.T, lengths.reshape(1, -1), patches)
     spread, live, pages, numbers, p = call(
         start_kernel,
         "start",
         matmul // 4,
         [HBM] * 4,
-        [((devices // 2, local, width), bf16), ids, ids, ids, (patches.shape, bf16)],
+        [((devices // 2, *halves.shape), bf16), ids, ids, ids, (patches.shape, bf16)],
         [
+            (halves.shape, bf16),
             (pbt.shape, jnp.int32),
             ((1, lengths.shape[0]), jnp.int32),
-            (local_rows.shape, bf16),
             pltpu.SemaphoreType.DMA((4,)),
         ],
     )(*(pltpu.with_memory_space_constraint(x, pltpu.HBM) for x in inputs))
     own = lax.all_to_all(
-        spread,
-        axes,
-        0,
-        0,
-        axis_index_groups=same_core,
-        tiled=True,
+        spread.reshape(devices, local // 2, width), axes, 0, 0, tiled=True
     ).reshape(half, width)
-    other = lax.ppermute(own, axes, [(i, i ^ 1) for i in range(devices)])
+    pairs = [(i, i ^ 1) for i in range(devices)]
+    other = lax.ppermute(own, axes, pairs)
     (own_lse,) = call(
         own_kernel, "own", matmul // 2, [VMEM] * 3, [half_table], [turned_half], limit
     )(live, own, p)
@@ -464,7 +458,7 @@
     )(pages, live, own_lse, other, p)
     recv = lax.all_to_all(send, "page", 0, 0, tiled=True)
     page_lse, row, sign, loss, acc = call(
-        functools.partial(inner_kernel, local),
+        inner_kernel,
         "inner",
         2 * matmul,
         [SMEM] + [VMEM] * 8,
@@ -478,20 +472,20 @@
         matmul,
         [VMEM] * 8,
         [
-            ((devices, local // 2, width), f32),
-            ((devices, local // 2, width), bf16),
+            ((half, width), f32),
+            ((half, width), f32),
             table,
             table,
             ((1, BROWS), f32),
         ],
     )(pages, numbers, sign, page_lse, row, loss, acc, recv)
-    give = lax.ppermute(give, axes, [(i, i ^ 1) for i in range(devices)])
+    give = lax.ppermute(give, axes, pairs)
     parts, row_grad = call(
         join_kernel,
         "join",
         matmul // 8,
         [VMEM] * 4,
-        [((devices, local // 2 + LOSS_ROWS, width), bf16), table],
+        [((devices, local // 4 + 1, 2, width), bf16), table],
     )(keep, give, part, row_grad)
     gathered = lax.all_to_all(parts, axes, 0, 0, tiled=True)
     (patch_grad,) = call(
@@ -502,7 +496,7 @@
         "final",
         devices * local * width,
         [VMEM],
-        [((local, width), f32), ((1, BROWS), f32)],
+        [((questions, 2, HALF_WORDS, width), f32), ((1, BROWS), f32)],
     )(gathered)
     return (patch_grad, query_grad.reshape(queries.shape), loss[0, :1])
 

time: 47.7 us -> 46.9 us (0.983)
  blocking collectives: 15.9 us -> 15.3 us
    all_to_all x1, blocking collectives: 15.9 us -> 15.3 us  [shards(): lax.all_to_all(spread.reshape(devices, local // 2, width), axes, 0, 0, ti...]
    all_to_all x1, waiting for transfers between devices: 4.43 us -> 3.9 us  [shards(): gathered = lax.all_to_all(parts, axes, 0, 0, tiled=True)]
where the time goes in v5:
time: 46.9 us; the launch traced here: 46.6 us
  Pallas kernels  16.4 us (35%)
  blocking collectives  15.3 us (33%)
  waiting for transfers between devices  7.44 us (16%)
  starting transfers between devices  6.78 us (14%)
  between operations  0.72 us (2%)
    all_to_all x1, blocking collectives, shards(): lax.all_to_all(spread.reshape(devices, local // 2, width), axes, 0, 0, ti...  15.3 us
    pallas_call x1, Pallas kernels, shards(): call(inner_kernel, 'inner', 2 * matmul, [SMEM] + [VMEM] * 8, [table, tabl...  4.91 us
    pallas_call x1, Pallas kernels, shards(): call(patch_kernel, 'patch', 2 * matmul, [VMEM] * 6, [(patches.shape, f32)...  4.51 us
    all_to_all x1, waiting for transfers between devices, shards(): gathered = lax.all_to_all(parts, axes, 0, 0, tiled=True)  3.9 us
    all_to_all x1, starting transfers between devices, shards(): recv = lax.all_to_all(send, 'page', 0, 0, tiled=True)  3.5 us
    all_to_all x1, starting transfers between devices, shards(): gathered = lax.all_to_all(parts, axes, 0, 0, tiled=True)  2.95 us
    pallas_call x1, Pallas kernels, shards(): call(stats_kernel, 'stats', matmul // 2, [VMEM] * 5, [table, ((peers, 1,...  2.12 us
    all_to_all x1, waiting for transfers between devices, shards(): recv = lax.all_to_all(send, 'page', 0, 0, tiled=True)  2.01 us
  transfers between devices with their start and end apart: 4, of which 3 were waited for; matrix products, arithmetic and copies ran while one was open for 0% of the time, Pallas kernels for 23%

profile of v5, /device:TPU:0, one launch (start us, length us, event | category | flops | bytes accessed | tf_op | source)
XLA Modules:
  0.0 46.6 jit_solution(3221047174750121705)
XLA Ops:
  0.6 0.0 copy-start
  0.6 0.0 copy-start.1
  0.7 1.1 %start.1 = (bf16[16,2,16,128]{3,2,1,0:T(8,128)(2,1)S(1)}, s32[16,128]{1,0:T(8,128)S(1)}, s32[16,128]{1,0:T(8,128)S(1)}, s32[16,128]{1,0:T(8,128)S(1)}, bf16[2048,128]{1,0:T(8,128)(2,1)S(1)}) custom-call(bf16[2,16,128]{2,1,0:T(8,128)(2,1)} %bitcast.15, s32[2,16]{1,0:T(2,128)} %bitcast.13, s32[1,64]{1,0:T(1,128)} %bitcast.16, bf16[2048,128]{1,0:T(8,128)(2,1)} %p_hbm.1), custom_call_target="tpu_custom_call" | custom-call | flops 134217728 | tf_op jit(solution)/shard_map/start/pallas_call | solution.py:429
  1.8 15.3 %all_to_all.15 = bf16[32,16,128]{2,1,0:T(8,128)(2,1)S(1)} all-to-all(bf16[32,16,128]{2,1,0:T(8,128)(2,1)S(1)} %bitcast.12), channel_id=1, replica_groups=mesh['grp'=2,'page'=16] {'grp','page'}, dimensions={0} | all-to-all | bytes 262144 | tf_op jit(solution)/shard_map/all_to_all | solution.py:442
  17.1 0.3 collective-permute-start
  17.4 1.4 %own.1.own_lse_ref = f32[16,512]{1,0:T(8,128)S(1)} custom-call(s32[16,128]{1,0:T(8,128)S(1)} %get-tuple-element.24.live_ref, bf16[512,128]{1,0:T(8,128)(2,1)S(1)} %bitcast.9, bf16[2048,128]{1,0:T(8,128)(2,1)S(1)} %get-tuple-element.28.p_ref), custom_call_target="tpu_custom_call" | custom-call | flops 268435456 | tf_op jit(solution)/shard_map/own/pallas_call | solution.py:447
  18.8 0.0 collective-permute-done.q_ref.oth_ref
  18.8 2.1 %stats.1 = (f32[16,1024]{1,0:T(8,128)S(1)}, f32[16,1,1152]{2,1,0:T(1,128)}) custom-call(s32[16,128]{1,0:T(8,128)S(1)} %get-tuple-element.25.ids_ref, s32[16,128]{1,0:T(8,128)S(1)} %get-tuple-element.24.live_ref, f32[16,512]{1,0:T(8,128)S(1)} %own.1.own_lse_ref, bf16[512,128]{1,0:T(8,128)(2,1)S(1)} %collective-permute-done.q_ref.oth_ref, ...), custom_call_target="tpu_custom_call" | custom-call | flops 268435456 | tf_op jit(solution)/shard_map/stats/pallas_call | solution.py:450
  20.9 3.5 %all-to-all-start.1 = ((f32[16,1,1152]{2,1,0:T(1,128)}), f32[16,1,1152]{2,1,0:T(1,128)S(1)}, u32[]{:S(2)}, u32[]{:S(2)}) async-start(f32[16,1,1152]{2,1,0:T(1,128)} %get-tuple-element.35), calls=%async_computation.1 | async-start | bytes 147456 | tf_op jit(solution)/shard_map/all_to_all | solution.py:459
  24.4 0.0 copy-done
  24.4 0.0 copy-done.1
  24.4 4.9 %inner.1 = (f32[16,1024]{1,0:T(8,128)S(1)}, f32[16,1024]{1,0:T(8,128)S(1)}, f32[16,1024]{1,0:T(8,128)S(1)}, f32[1,128]{1,0:T(1,128)S(1)}, f32[3,128,1024]{2,1,0:T(8,128)S(1)}) custom-call(s32[2,16]{1,0:T(2,128)S(1)} %bitcast.14, s32[16,128]{1,0:T(8,128)S(1)} %get-tuple-element.25.ids_ref, s32[16,128]{1,0:T(8,128)S(1)} %get-tuple-element.26.number_ref, ...), custom_call_target="tpu_custom_call" | custom-call | flops 1073741824 | tf_op jit(solution)/shard_map/inner/pallas_call | solution.py:460
  29.3 2.0 %all-to-all-done.1.recv_ref = f32[16,1,1152]{2,1,0:T(1,128)S(1)} async-done(((f32[16,1,1152]{2,1,0:T(1,128)}), f32[16,1,1152]{2,1,0:T(1,128)S(1)}, u32[]{:S(2)}, u32[]{:S(2)}) %all-to-all-start.1) | async-done | bytes 73760 | tf_op jit(solution)/shard_map/all_to_all | solution.py:459
  31.4 0.8 %close.1 = (f32[512,128]{1,0:T(8,128)S(1)}, f32[512,128]{1,0:T(8,128)S(1)}, f32[16,1024]{1,0:T(8,128)S(1)}, f32[16,1024]{1,0:T(8,128)S(1)}, f32[1,128]{1,0:T(1,128)S(1)}) custom-call(s32[16,128]{1,0:T(8,128)S(1)} %get-tuple-element.25.ids_ref, s32[16,128]{1,0:T(8,128)S(1)} %get-tuple-element.26.number_ref, f32[16,1024]{1,0:T(8,128)S(1)} %get-tuple-element.30.sign_ref, ...), custom_call_target="tpu_custom_call" | custom-call | flops 536870912 | tf_op jit(solution)/shard_map/close/pallas_call | solution.py:469
  32.2 0.1 collective-permute-start.1
  32.2 1.5 %collective-permute-done.1.give_ref = f32[512,128]{1,0:T(8,128)S(1)} collective-permute-done((f32[512,128]{1,0:T(8,128)S(1)}, f32[512,128]{1,0:T(8,128)S(1)}, u32[]{:S(2)}, u32[]{:S(2)}) %collective-permute-start.1) | collective-permute-done | bytes 262176 | tf_op jit(solution)/shard_map/ppermute | solution.py:482
  33.8 0.8 %join.1 = (bf16[32,9,2,128]{3,2,1,0:T(2,128)(2,1)}, f32[16,1024]{1,0:T(8,128)S(1)}) custom-call(f32[512,128]{1,0:T(8,128)S(1)} %get-tuple-element.37.keep_ref, f32[512,128]{1,0:T(8,128)S(1)} %collective-permute-done.1.give_ref, f32[1,128]{1,0:T(1,128)S(1)} %get-tuple-element.39.part_ref, f32[16,1024]{1,0:T(8,128)S(1)} %get-tuple-element.40.row_ref), custom_call_target="tpu_custom_call" | custom-call | flops 67108864 | tf_op jit(solution)/shard_map/join/pallas_call | solution.py:483
  34.5 3.0 %all-to-all-start.2 = ((bf16[32,9,2,128]{3,2,1,0:T(2,128)(2,1)}), bf16[32,9,2,128]{3,2,1,0:T(2,128)(2,1)S(1)}, u32[]{:S(2)}, u32[]{:S(2)}) async-start(bf16[32,9,2,128]{3,2,1,0:T(2,128)(2,1)} %get-tuple-element.42), calls=%async_computation.2 | async-start | bytes 294912 | tf_op jit(solution)/shard_map/all_to_all | solution.py:490
  37.5 4.5 %patch.1 = f32[2048,128]{1,0:T(8,128)} custom-call(s32[16,128]{1,0:T(8,128)S(1)} %get-tuple-element.24.live_ref, f32[16,1024]{1,0:T(8,128)S(1)} %get-tuple-element.36.lse_ref, f32[16,1024]{1,0:T(8,128)S(1)} %get-tuple-element.41.row_ref, bf16[512,128]{1,0:T(8,128)(2,1)S(1)} %bitcast.11, bf16[512,128]{1,0:T(8,128)(2,1)S(1)} %collective-permute-done.q_ref.oth_ref, ...), custom_call_target="tpu_custom_call" | custom-call | flops 1073741824 | tf_op jit(solution)/shard_map/patch/pallas_call | solution.py:491
  42.0 3.9 %all-to-all-done.2.refs_0_ = bf16[32,9,2,128]{3,2,1,0:T(2,128)(2,1)S(1)} async-done(((bf16[32,9,2,128]{3,2,1,0:T(2,128)(2,1)}), bf16[32,9,2,128]{3,2,1,0:T(2,128)(2,1)S(1)}, u32[]{:S(2)}, u32[]{:S(2)}) %all-to-all-start.2) | async-done | bytes 147488 | tf_op jit(solution)/shard_map/all_to_all | solution.py:490
  45.9 0.7 %final.1 = (f32[1,2,16,128]{3,2,1,0:T(8,128)}, f32[1,128]{1,0:T(1,128)}) custom-call(bf16[32,9,2,128]{3,2,1,0:T(2,128)(2,1)S(1)} %all-to-all-done.2.refs_0_), custom_call_target="tpu_custom_call" | custom-call | flops 131072 | tf_op jit(solution)/shard_map/final/pallas_call | solution.py:494
Async XLA Ops:
  0.6 23.8 %copy-start = (s32[16,2]{0,1:T(2,128)S(1)}, s32[16,2]{0,1:T(2,128)}, u32[]{:S(2)}) copy-start(s32[16,2]{0,1:T(2,128)} %param.7) | copy-start | bytes 388
  0.6 23.8 %copy-start.1 = (s32[32,64]{1,0:T(8,128)S(1)}, s32[32,64]{1,0:T(8,128)}, u32[]{:S(2)}) copy-start(s32[32,64]{1,0:T(8,128)} %lab_ref.1) | copy-start | bytes 24580
  17.1 1.6 %collective-permute-start = (bf16[512,128]{1,0:T(8,128)(2,1)S(1)}, bf16[512,128]{1,0:T(8,128)(2,1)S(1)}, u32[]{:S(2)}, u32[]{:S(2)}) collective-permute-start(bf16[512,128]{1,0:T(8,128)(2,1)S(1)} %bitcast.8), channel_id=1, source_target_pairs={{0,1},{1,0},{2,3},{3,2},{4,5},{5,4},{6,7},{7,6},{8,9},{9,8},{10,11... | collective-permute-start | bytes 393224 | tf_op jit(solution)/shard_map/ppermute | solution.py:446
  20.9 10.5 %all-to-all-start.1 = ((f32[16,1,1152]{2,1,0:T(1,128)}), f32[16,1,1152]{2,1,0:T(1,128)S(1)}, u32[]{:S(2)}, u32[]{:S(2)}) async-start(f32[16,1,1152]{2,1,0:T(1,128)} %get-tuple-element.35), calls=%async_computation.1 | async-start | bytes 147456 | tf_op jit(solution)/shard_map/all_to_all | solution.py:459
  32.2 1.6 %collective-permute-start.1 = (f32[512,128]{1,0:T(8,128)S(1)}, f32[512,128]{1,0:T(8,128)S(1)}, u32[]{:S(2)}, u32[]{:S(2)}) collective-permute-start(f32[512,128]{1,0:T(8,128)S(1)} %get-tuple-element.38), channel_id=1, source_target_pairs={{0,1},{1,0},{2,3},{3,2},{4,5},{5,4},{6,7},{7,6},{8,9},{9,8},{10,11... | collective-permute-start | bytes 786440 | tf_op jit(solution)/shard_map/ppermute | solution.py:482
  34.5 11.4 %all-to-all-start.2 = ((bf16[32,9,2,128]{3,2,1,0:T(2,128)(2,1)}), bf16[32,9,2,128]{3,2,1,0:T(2,128)(2,1)S(1)}, u32[]{:S(2)}, u32[]{:S(2)}) async-start(bf16[32,9,2,128]{3,2,1,0:T(2,128)(2,1)} %get-tuple-element.42), calls=%async_computation.2 | async-start | bytes 294912 | tf_op jit(solution)/shard_map/all_to_all | solution.py:490

commit v6 on v5

--- a/solution.py
+++ b/solution.py
@@ -19,7 +19,7 @@
 CHUNK = 256
 LOW_LANES = 64
 GROUP = 4
-INNER_UNROLL = 1
+INNER_UNROLL = 4
 PATCH_UNROLL = 1
 DEAD = -(2.0**93)
 INSIDE, HEAD, TAIL = 0, 1, 2
@@ -266,8 +266,8 @@
 
 
 def close_kernel(
-    ids_ref, number_ref, sign_ref, page_ref, row_ref, loss_ref, acc_ref, recv_ref, keep_ref, give_ref, lse_ref,
-    full_ref, part_ref,
+    ids_ref, number_ref, sign_ref, page_ref, row_ref, loss_ref, acc_ref, recv_ref, scales_ref, give_ref, lse_ref,
+    full_ref, part_ref, got_ref,
 ):
     slots, rows = page_ref.shape
     peers = recv_ref.shape[0]
@@ -281,25 +281,21 @@
     is_last = pages == last
     alone = first == last
 
-    def gathered(wanted, below):
-        parts = []
-        for peer in range(peers):
-            side = peer < mine if below else peer > mine
-            same = (recv_ref[peer, :, rows : rows + 1] == wanted.astype(f32)) & side
-            row = recv_ref[peer, :, :rows]
-            crossed = jnp.concatenate([row[:, half:], row[:, :half]], axis=1)
-            row = jnp.where(peer % 2 == core, row, crossed)
-            parts.append(jnp.where(same, row, very_low))
-        peak = parts[0]
-        for part in parts[1:]:
-            peak = jnp.maximum(peak, part)
-        mass = jnp.zeros((1, rows), f32)
-        for part in parts:
-            mass = mass + jnp.where(part > 0.5 * very_low, jnp.exp2(part - peak), 0.0)
+    for peer in range(peers):
+        got_ref[peer : peer + 1, :] = recv_ref[peer]
+    peer = lax.broadcasted_iota(jnp.int32, (peers, 1), 0)
+    got = got_ref[:, :rows]
+    crossed = jnp.concatenate([got[:, half:], got[:, :half]], axis=1)
+    got = jnp.where(peer % 2 == core, got, crossed)
+    ids = got_ref[:, rows : rows + 1]
+
+    def gathered(mask):
+        peak = chosen_row(got, mask)
+        mass = jnp.sum(jnp.where(mask, jnp.exp2(got - peak), 0.0), axis=0, keepdims=True)
         return peak + jnp.log2(jnp.maximum(mass, 1e-30))
 
-    below = gathered(first, True)
-    above = gathered(last, False)
+    below = gathered((peer < mine) & (ids == first.astype(f32)))
+    above = gathered((peer > mine) & (ids == last.astype(f32)))
     value = page_ref[...]
     head = value[0:1]
     tail = chosen_row(value, is_last)
@@ -323,16 +319,25 @@
     full_ref[...] = jnp.where(is_last, row[1:2], jnp.where(is_first, row[0:1], row_ref[...]))
     head_scale = row[0:1] * jnp.exp2(head - head_full)
     tail_scale = row[1:2] * jnp.exp2(tail - tail_full)
-    for lo in range(0, rows, CHUNK):
-        span = slice(lo, lo + CHUNK)
+    scales_ref[0:1, :] = head_scale
+    scales_ref[1:2, :] = tail_scale
+    combine(acc_ref, scales_ref, give_ref, half)
+    part_ref[...] = loss
+
+
+def combine(acc_ref, scales_ref, out_ref, base):
+    for lo in range(0, out_ref.shape[0], CHUNK):
+        span = slice(base + lo, base + lo + CHUNK)
         total = (
             acc_ref[INSIDE, :, span]
-            + acc_ref[HEAD, :, span] * head_scale[:, span]
-            + acc_ref[TAIL, :, span] * tail_scale[:, span]
+            + acc_ref[HEAD, :, span] * scales_ref[0:1, span]
+            + acc_ref[TAIL, :, span] * scales_ref[1:2, span]
         )
-        side, at = (keep_ref, lo) if lo < half else (give_ref, lo - half)
-        side[at : at + CHUNK, :] = total.T
-    part_ref[...] = loss
+        out_ref[lo : lo + CHUNK, :] = total.T
+
+
+def keep_kernel(acc_ref, scales_ref, keep_ref):
+    combine(acc_ref, scales_ref, keep_ref, 0)
 
 
 def join_kernel(keep_ref, give_ref, part_ref, row_ref, out_ref, again_ref):
@@ -466,20 +471,22 @@
         [table, ((width, rows), bf16)],
         limit,
     )(pbt, pages, numbers, live, labels, lse, own, other, p)
-    keep, give, full_lse, row_grad, part = call(
+    scales, give, full_lse, row_grad, part = call(
         close_kernel,
         "close",
         matmul,
         [VMEM] * 8,
         [
-            ((half, width), f32),
+            ((2, rows), f32),
             ((half, width), f32),
             table,
             table,
             ((1, BROWS), f32),
         ],
+        [((peers, rows + 128), f32)],
     )(pages, numbers, sign, page_lse, row, loss, acc, recv)
     give = lax.ppermute(give, axes, pairs)
+    (keep,) = call(keep_kernel, "keep", matmul // 4, [VMEM] * 2, [((half, width), f32)])(acc, scales)
     parts, row_grad = call(
         join_kernel,
         "join",

time: 46.9 us -> 46.4 us (0.989)
  Pallas kernels: 16.4 us -> 15.3 us
  waiting for transfers between devices: 7.44 us -> 8.33 us
    all_to_all x1, waiting for transfers between devices: 2.01 us -> 3.05 us  [shards(): recv = lax.all_to_all(send, 'page', 0, 0, tiled=True)]
    pallas_call x1, Pallas kernels: 4.91 us -> 3.87 us  [shards(): call(inner_kernel, 'inner', 2 * matmul, [SMEM] + [VMEM] * 8, [table, tabl...]
  transfers between devices with their start and end apart: 4 -> 4, of which waited for: 3 -> 3; matrix products, arithmetic and copies ran while one was open for 0% -> 0% of each run, Pallas kernels for 23% -> 22%
where the time goes in v6:
time: 46.4 us; the launch traced here: 46.1 us
  Pallas kernels  15.3 us (33%)
  blocking collectives  15.3 us (33%)
  waiting for transfers between devices  8.33 us (18%)
  starting transfers between devices  6.41 us (14%)
  between operations  0.72 us (2%)
    all_to_all x1, blocking collectives, shards(): lax.all_to_all(spread.reshape(devices, local // 2, width), axes, 0, 0, ti...  15.3 us
    pallas_call x1, Pallas kernels, shards(): call(patch_kernel, 'patch', 2 * matmul, [VMEM] * 6, [(patches.shape, f32)...  4.52 us
    all_to_all x1, waiting for transfers between devices, shards(): gathered = lax.all_to_all(parts, axes, 0, 0, tiled=True)  3.9 us
    pallas_call x1, Pallas kernels, shards(): call(inner_kernel, 'inner', 2 * matmul, [SMEM] + [VMEM] * 8, [table, tabl...  3.87 us
    all_to_all x1, starting transfers between devices, shards(): recv = lax.all_to_all(send, 'page', 0, 0, tiled=True)  3.5 us
    all_to_all x1, waiting for transfers between devices, shards(): recv = lax.all_to_all(send, 'page', 0, 0, tiled=True)  3.05 us
    all_to_all x1, starting transfers between devices, shards(): gathered = lax.all_to_all(parts, axes, 0, 0, tiled=True)  2.57 us
    pallas_call x1, Pallas kernels, shards(): call(stats_kernel, 'stats', matmul // 2, [VMEM] * 5, [table, ((peers, 1,...  2.12 us
  transfers between devices with their start and end apart: 4, of which 3 were waited for; matrix products, arithmetic and copies ran while one was open for 0% of the time, Pallas kernels for 22%

profile of v6, /device:TPU:0, one launch (start us, length us, event | category | flops | bytes accessed | tf_op | source)
XLA Modules:
  0.0 46.1 jit_solution(1476724002623673388)
XLA Ops:
  0.6 0.0 copy-start
  0.6 0.0 copy-start.1
  0.7 1.1 %start.1 = (bf16[16,2,16,128]{3,2,1,0:T(8,128)(2,1)S(1)}, s32[16,128]{1,0:T(8,128)S(1)}, s32[16,128]{1,0:T(8,128)S(1)}, s32[16,128]{1,0:T(8,128)S(1)}, bf16[2048,128]{1,0:T(8,128)(2,1)S(1)}) custom-call(bf16[2,16,128]{2,1,0:T(8,128)(2,1)} %bitcast.15, s32[2,16]{1,0:T(2,128)} %bitcast.13, s32[1,64]{1,0:T(1,128)} %bitcast.16, bf16[2048,128]{1,0:T(8,128)(2,1)} %p_hbm.1), custom_call_target="tpu_custom_call" | custom-call | flops 134217728 | tf_op jit(solution)/shard_map/start/pallas_call | solution.py:434
  1.8 15.3 %all_to_all.15 = bf16[32,16,128]{2,1,0:T(8,128)(2,1)S(1)} all-to-all(bf16[32,16,128]{2,1,0:T(8,128)(2,1)S(1)} %bitcast.12), channel_id=1, replica_groups=mesh['grp'=2,'page'=16] {'grp','page'}, dimensions={0} | all-to-all | bytes 262144 | tf_op jit(solution)/shard_map/all_to_all | solution.py:447
  17.1 0.3 collective-permute-start
  17.4 1.4 %own.1.own_lse_ref = f32[16,512]{1,0:T(8,128)S(1)} custom-call(s32[16,128]{1,0:T(8,128)S(1)} %get-tuple-element.24.live_ref, bf16[512,128]{1,0:T(8,128)(2,1)S(1)} %bitcast.9, bf16[2048,128]{1,0:T(8,128)(2,1)S(1)} %get-tuple-element.28.p_ref), custom_call_target="tpu_custom_call" | custom-call | flops 268435456 | tf_op jit(solution)/shard_map/own/pallas_call | solution.py:452
  18.8 0.0 collective-permute-done.q_ref.oth_ref
  18.8 2.1 %stats.1 = (f32[16,1024]{1,0:T(8,128)S(1)}, f32[16,1,1152]{2,1,0:T(1,128)}) custom-call(s32[16,128]{1,0:T(8,128)S(1)} %get-tuple-element.25.ids_ref, s32[16,128]{1,0:T(8,128)S(1)} %get-tuple-element.24.live_ref, f32[16,512]{1,0:T(8,128)S(1)} %own.1.own_lse_ref, bf16[512,128]{1,0:T(8,128)(2,1)S(1)} %collective-permute-done.q_ref.oth_ref, ...), custom_call_target="tpu_custom_call" | custom-call | flops 268435456 | tf_op jit(solution)/shard_map/stats/pallas_call | solution.py:455
  20.9 3.5 %all-to-all-start.1 = ((f32[16,1,1152]{2,1,0:T(1,128)}), f32[16,1,1152]{2,1,0:T(1,128)S(1)}, u32[]{:S(2)}, u32[]{:S(2)}) async-start(f32[16,1,1152]{2,1,0:T(1,128)} %get-tuple-element.35), calls=%async_computation.1 | async-start | bytes 147456 | tf_op jit(solution)/shard_map/all_to_all | solution.py:464
  24.4 0.0 copy-done
  24.4 0.0 copy-done.1
  24.4 3.9 %inner.1 = (f32[16,1024]{1,0:T(8,128)S(1)}, f32[16,1024]{1,0:T(8,128)S(1)}, f32[16,1024]{1,0:T(8,128)S(1)}, f32[1,128]{1,0:T(1,128)S(1)}, f32[3,128,1024]{2,1,0:T(8,128)S(1)}) custom-call(s32[2,16]{1,0:T(2,128)S(1)} %bitcast.14, s32[16,128]{1,0:T(8,128)S(1)} %get-tuple-element.25.ids_ref, s32[16,128]{1,0:T(8,128)S(1)} %get-tuple-element.26.number_ref, ...), custom_call_target="tpu_custom_call" | custom-call | flops 1073741824 | tf_op jit(solution)/shard_map/inner/pallas_call | solution.py:465
  28.3 3.1 %all-to-all-done.1.recv_ref = f32[16,1,1152]{2,1,0:T(1,128)S(1)} async-done(((f32[16,1,1152]{2,1,0:T(1,128)}), f32[16,1,1152]{2,1,0:T(1,128)S(1)}, u32[]{:S(2)}, u32[]{:S(2)}) %all-to-all-start.1) | async-done | bytes 73760 | tf_op jit(solution)/shard_map/all_to_all | solution.py:464
  31.4 0.7 %close.1 = (f32[2,1024]{1,0:T(2,128)S(1)}, f32[512,128]{1,0:T(8,128)S(1)}, f32[16,1024]{1,0:T(8,128)S(1)}, f32[16,1024]{1,0:T(8,128)S(1)}, f32[1,128]{1,0:T(1,128)S(1)}) custom-call(s32[16,128]{1,0:T(8,128)S(1)} %get-tuple-element.25.ids_ref, s32[16,128]{1,0:T(8,128)S(1)} %get-tuple-element.26.number_ref, f32[16,1024]{1,0:T(8,128)S(1)} %get-tuple-element.30.sign_ref, ...), custom_call_target="tpu_custom_call" | custom-call | flops 536870912 | tf_op jit(solution)/shard_map/close/pallas_call | solution.py:474
  32.0 0.1 collective-permute-start.1
  32.1 0.1 keep.1.keep_ref
  32.3 1.4 %collective-permute-done.1.give_ref = f32[512,128]{1,0:T(8,128)S(1)} collective-permute-done((f32[512,128]{1,0:T(8,128)S(1)}, f32[512,128]{1,0:T(8,128)S(1)}, u32[]{:S(2)}, u32[]{:S(2)}) %collective-permute-start.1) | collective-permute-done | bytes 262176 | tf_op jit(solution)/shard_map/ppermute | solution.py:488
  33.6 0.8 %join.1 = (bf16[32,9,2,128]{3,2,1,0:T(2,128)(2,1)}, f32[16,1024]{1,0:T(8,128)S(1)}) custom-call(f32[512,128]{1,0:T(8,128)S(1)} %keep.1.keep_ref, f32[512,128]{1,0:T(8,128)S(1)} %collective-permute-done.1.give_ref, f32[1,128]{1,0:T(1,128)S(1)} %get-tuple-element.39.part_ref, f32[16,1024]{1,0:T(8,128)S(1)} %get-tuple-element.40.row_ref), custom_call_target="tpu_custom_call" | custom-call | flops 67108864 | tf_op jit(solution)/shard_map/join/pallas_call | solution.py:490
  34.4 2.6 %all-to-all-start.2 = ((bf16[32,9,2,128]{3,2,1,0:T(2,128)(2,1)}), bf16[32,9,2,128]{3,2,1,0:T(2,128)(2,1)S(1)}, u32[]{:S(2)}, u32[]{:S(2)}) async-start(bf16[32,9,2,128]{3,2,1,0:T(2,128)(2,1)} %get-tuple-element.42), calls=%async_computation.2 | async-start | bytes 294912 | tf_op jit(solution)/shard_map/all_to_all | solution.py:497
  37.0 4.5 %patch.1 = f32[2048,128]{1,0:T(8,128)} custom-call(s32[16,128]{1,0:T(8,128)S(1)} %get-tuple-element.24.live_ref, f32[16,1024]{1,0:T(8,128)S(1)} %get-tuple-element.36.lse_ref, f32[16,1024]{1,0:T(8,128)S(1)} %get-tuple-element.41.row_ref, bf16[512,128]{1,0:T(8,128)(2,1)S(1)} %bitcast.11, bf16[512,128]{1,0:T(8,128)(2,1)S(1)} %collective-permute-done.q_ref.oth_ref, ...), custom_call_target="tpu_custom_call" | custom-call | flops 1073741824 | tf_op jit(solution)/shard_map/patch/pallas_call | solution.py:498
  41.5 3.9 %all-to-all-done.2.refs_0_ = bf16[32,9,2,128]{3,2,1,0:T(2,128)(2,1)S(1)} async-done(((bf16[32,9,2,128]{3,2,1,0:T(2,128)(2,1)}), bf16[32,9,2,128]{3,2,1,0:T(2,128)(2,1)S(1)}, u32[]{:S(2)}, u32[]{:S(2)}) %all-to-all-start.2) | async-done | bytes 147488 | tf_op jit(solution)/shard_map/all_to_all | solution.py:497
  45.4 0.7 %final.1 = (f32[1,2,16,128]{3,2,1,0:T(8,128)}, f32[1,128]{1,0:T(1,128)}) custom-call(bf16[32,9,2,128]{3,2,1,0:T(2,128)(2,1)S(1)} %all-to-all-done.2.refs_0_), custom_call_target="tpu_custom_call" | custom-call | flops 131072 | tf_op jit(solution)/shard_map/final/pallas_call | solution.py:501
Async XLA Ops:
  0.6 23.8 %copy-start = (s32[16,2]{0,1:T(2,128)S(1)}, s32[16,2]{0,1:T(2,128)}, u32[]{:S(2)}) copy-start(s32[16,2]{0,1:T(2,128)} %param.7) | copy-start | bytes 388
  0.6 23.8 %copy-start.1 = (s32[32,64]{1,0:T(8,128)S(1)}, s32[32,64]{1,0:T(8,128)}, u32[]{:S(2)}) copy-start(s32[32,64]{1,0:T(8,128)} %lab_ref.1) | copy-start | bytes 24580
  17.1 1.7 %collective-permute-start = (bf16[512,128]{1,0:T(8,128)(2,1)S(1)}, bf16[512,128]{1,0:T(8,128)(2,1)S(1)}, u32[]{:S(2)}, u32[]{:S(2)}) collective-permute-start(bf16[512,128]{1,0:T(8,128)(2,1)S(1)} %bitcast.8), channel_id=1, source_target_pairs={{0,1},{1,0},{2,3},{3,2},{4,5},{5,4},{6,7},{7,6},{8,9},{9,8},{10,11... | collective-permute-start | bytes 393224 | tf_op jit(solution)/shard_map/ppermute | solution.py:451
  20.9 10.5 %all-to-all-start.1 = ((f32[16,1,1152]{2,1,0:T(1,128)}), f32[16,1,1152]{2,1,0:T(1,128)S(1)}, u32[]{:S(2)}, u32[]{:S(2)}) async-start(f32[16,1,1152]{2,1,0:T(1,128)} %get-tuple-element.35), calls=%async_computation.1 | async-start | bytes 147456 | tf_op jit(solution)/shard_map/all_to_all | solution.py:464
  32.0 1.6 %collective-permute-start.1 = (f32[512,128]{1,0:T(8,128)S(1)}, f32[512,128]{1,0:T(8,128)S(1)}, u32[]{:S(2)}, u32[]{:S(2)}) collective-permute-start(f32[512,128]{1,0:T(8,128)S(1)} %get-tuple-element.38), channel_id=1, source_target_pairs={{0,1},{1,0},{2,3},{3,2},{4,5},{5,4},{6,7},{7,6},{8,9},{9,8},{10,11... | collective-permute-start | bytes 786440 | tf_op jit(solution)/shard_map/ppermute | solution.py:488
  34.4 11.0 %all-to-all-start.2 = ((bf16[32,9,2,128]{3,2,1,0:T(2,128)(2,1)}), bf16[32,9,2,128]{3,2,1,0:T(2,128)(2,1)S(1)}, u32[]{:S(2)}, u32[]{:S(2)}) async-start(bf16[32,9,2,128]{3,2,1,0:T(2,128)(2,1)} %get-tuple-element.42), calls=%async_computation.2 | async-start | bytes 294912 | tf_op jit(solution)/shard_map/all_to_all | solution.py:497

commit v7 on v6

--- a/solution.py
+++ b/solution.py
@@ -110,15 +110,14 @@
 
 
 def start_kernel(
-    rows_hbm, pbt_hbm, len_hbm, p_hbm, spread_ref, live_ref, page_ref, number_ref, p_ref, rows_ref, pbt_ref,
-    len_ref, sems,
+    rows_hbm, pbt_hbm, len_hbm, spread_ref, live_ref, page_ref, number_ref, rows_ref, pbt_ref, len_ref, sems,
 ):
     slots = live_ref.shape[0]
-    pairs = ((rows_hbm, rows_ref), (pbt_hbm, pbt_ref), (len_hbm, len_ref), (p_hbm, p_ref))
+    pairs = ((rows_hbm, rows_ref), (pbt_hbm, pbt_ref), (len_hbm, len_ref))
     copies = [pltpu.make_async_copy(*pair, sems.at[at]) for at, pair in enumerate(pairs)]
     for copy in copies:
         copy.start()
-    for copy in copies[:-1]:
+    for copy in copies:
         copy.wait()
     spread_ref[...] = jnp.broadcast_to(rows_ref[...][None], spread_ref.shape)
     pages = columns(pbt_ref[0:1, :], slots)
@@ -130,7 +129,6 @@
     live_ref[...] = jnp.broadcast_to(jnp.where(pages < 0, 0, live), live_ref.shape)
     page_ref[...] = jnp.broadcast_to(pages, page_ref.shape)
     number_ref[...] = jnp.broadcast_to(numbers, number_ref.shape)
-    copies[-1].wait()
 
 
 def own_kernel(live_ref, q_ref, p_ref, lse_ref, qt_ref):
@@ -430,18 +428,19 @@
     pbt = page_blocks.T
     questions = local // QUESTION_WORDS
     halves = local_rows.reshape(questions, 2, HALF_WORDS, width).swapaxes(0, 1).reshape(2, local // 2, width)
-    inputs = (halves, page_blocks.T, lengths.reshape(1, -1), patches)
-    spread, live, pages, numbers, p = call(
+    inputs = (halves, page_blocks.T, lengths.reshape(1, -1))
+    p = patches
+    spread, live, pages, numbers = call(
         start_kernel,
         "start",
-        matmul // 4,
-        [HBM] * 4,
-        [((devices // 2, *halves.shape), bf16), ids, ids, ids, (patches.shape, bf16)],
+        4 * matmul,
+        [HBM] * 3,
+        [((devices // 2, *halves.shape), bf16), ids, ids, ids],
         [
             (halves.shape, bf16),
             (pbt.shape, jnp.int32),
             ((1, lengths.shape[0]), jnp.int32),
-            pltpu.SemaphoreType.DMA((4,)),
+            pltpu.SemaphoreType.DMA((3,)),
         ],
     )(*(pltpu.with_memory_space_constraint(x, pltpu.HBM) for x in inputs))
     own = lax.all_to_all(

time: 46.4 us -> 46.3 us (level)
  no operation moved by 1% of the time
where the time goes in v7:
time: 46.3 us; the launch traced here: 46 us
  blocking collectives  15.3 us (33%)
  Pallas kernels  15.1 us (33%)
  waiting for transfers between devices  8.33 us (18%)
  starting transfers between devices  6.41 us (14%)
  between operations  0.73 us (2%)
    all_to_all x1, blocking collectives, shards(): lax.all_to_all(spread.reshape(devices, local // 2, width), axes, 0, 0, ti...  15.3 us
    pallas_call x1, Pallas kernels, shards(): call(patch_kernel, 'patch', 2 * matmul, [VMEM] * 6, [(patches.shape, f32)...  4.51 us
    all_to_all x1, waiting for transfers between devices, shards(): gathered = lax.all_to_all(parts, axes, 0, 0, tiled=True)  3.91 us
    pallas_call x1, Pallas kernels, shards(): call(inner_kernel, 'inner', 2 * matmul, [SMEM] + [VMEM] * 8, [table, tabl...  3.88 us
    all_to_all x1, starting transfers between devices, shards(): recv = lax.all_to_all(send, 'page', 0, 0, tiled=True)  3.5 us
    all_to_all x1, waiting for transfers between devices, shards(): recv = lax.all_to_all(send, 'page', 0, 0, tiled=True)  3.04 us
    all_to_all x1, starting transfers between devices, shards(): gathered = lax.all_to_all(parts, axes, 0, 0, tiled=True)  2.57 us
    pallas_call x1, Pallas kernels, shards(): call(stats_kernel, 'stats', matmul // 2, [VMEM] * 5, [table, ((peers, 1,...  2.12 us
  transfers between devices with their start and end apart: 4, of which 3 were waited for; matrix products, arithmetic and copies ran while one was open for 0% of the time, Pallas kernels for 22%

profile of v7, /device:TPU:0, one launch (start us, length us, event | category | flops | bytes accessed | tf_op | source)
XLA Modules:
  0.0 46.0 jit_solution(17744627418441575703)
XLA Ops:
  0.6 0.0 copy-start
  0.6 0.9 %start.1 = (bf16[16,2,16,128]{3,2,1,0:T(8,128)(2,1)S(1)}, s32[16,128]{1,0:T(8,128)S(1)}, s32[16,128]{1,0:T(8,128)S(1)}, s32[16,128]{1,0:T(8,128)S(1)}) custom-call(bf16[2,16,128]{2,1,0:T(8,128)(2,1)} %bitcast.16, s32[2,16]{1,0:T(2,128)} %bitcast.13, s32[1,64]{1,0:T(1,128)} %bitcast.17), custom_call_target="tpu_custom_call" | custom-call | flops 2147483648 | tf_op jit(solution)/shard_map/start/pallas_call | solution.py:433
  1.6 0.0 copy-start.1
  1.6 0.0 copy-start.2
  1.6 15.3 %all_to_all.15 = bf16[32,16,128]{2,1,0:T(8,128)(2,1)S(1)} all-to-all(bf16[32,16,128]{2,1,0:T(8,128)(2,1)S(1)} %bitcast.12), channel_id=1, replica_groups=mesh['grp'=2,'page'=16] {'grp','page'}, dimensions={0} | all-to-all | bytes 262144 | tf_op jit(solution)/shard_map/all_to_all | solution.py:446
  17.0 0.3 collective-permute-start
  17.2 0.0 copy-done
  17.2 1.4 %own.1.own_lse_ref = f32[16,512]{1,0:T(8,128)S(1)} custom-call(s32[16,128]{1,0:T(8,128)S(1)} %get-tuple-element.23.live_ref, bf16[512,128]{1,0:T(8,128)(2,1)S(1)} %bitcast.9, bf16[2048,128]{1,0:T(8,128)(2,1)S(1)} %copy-done), custom_call_target="tpu_custom_call" | custom-call | flops 268435456 | tf_op jit(solution)/shard_map/own/pallas_call | solution.py:451
  18.6 0.0 collective-permute-done.q_ref.oth_ref
  18.6 2.1 %stats.1 = (f32[16,1024]{1,0:T(8,128)S(1)}, f32[16,1,1152]{2,1,0:T(1,128)}) custom-call(s32[16,128]{1,0:T(8,128)S(1)} %get-tuple-element.24.ids_ref, s32[16,128]{1,0:T(8,128)S(1)} %get-tuple-element.23.live_ref, f32[16,512]{1,0:T(8,128)S(1)} %own.1.own_lse_ref, bf16[512,128]{1,0:T(8,128)(2,1)S(1)} %collective-permute-done.q_ref.oth_ref, ...), custom_call_target="tpu_custom_call" | custom-call | flops 268435456 | tf_op jit(solution)/shard_map/stats/pallas_call | solution.py:454
  20.7 3.5 %all-to-all-start.1 = ((f32[16,1,1152]{2,1,0:T(1,128)}), f32[16,1,1152]{2,1,0:T(1,128)S(1)}, u32[]{:S(2)}, u32[]{:S(2)}) async-start(f32[16,1,1152]{2,1,0:T(1,128)} %get-tuple-element.33), calls=%async_computation.1 | async-start | bytes 147456 | tf_op jit(solution)/shard_map/all_to_all | solution.py:463
  24.2 0.0 copy-done.1
  24.3 0.0 copy-done.2
  24.3 3.9 %inner.1 = (f32[16,1024]{1,0:T(8,128)S(1)}, f32[16,1024]{1,0:T(8,128)S(1)}, f32[16,1024]{1,0:T(8,128)S(1)}, f32[1,128]{1,0:T(1,128)S(1)}, f32[3,128,1024]{2,1,0:T(8,128)S(1)}) custom-call(s32[2,16]{1,0:T(2,128)S(1)} %bitcast.14, s32[16,128]{1,0:T(8,128)S(1)} %get-tuple-element.24.ids_ref, s32[16,128]{1,0:T(8,128)S(1)} %get-tuple-element.25.number_ref, ...), custom_call_target="tpu_custom_call" | custom-call | flops 1073741824 | tf_op jit(solution)/shard_map/inner/pallas_call | solution.py:464
  28.2 3.0 %all-to-all-done.1.recv_ref = f32[16,1,1152]{2,1,0:T(1,128)S(1)} async-done(((f32[16,1,1152]{2,1,0:T(1,128)}), f32[16,1,1152]{2,1,0:T(1,128)S(1)}, u32[]{:S(2)}, u32[]{:S(2)}) %all-to-all-start.1) | async-done | bytes 73760 | tf_op jit(solution)/shard_map/all_to_all | solution.py:463
  31.2 0.7 %close.1 = (f32[2,1024]{1,0:T(2,128)S(1)}, f32[512,128]{1,0:T(8,128)S(1)}, f32[16,1024]{1,0:T(8,128)S(1)}, f32[16,1024]{1,0:T(8,128)S(1)}, f32[1,128]{1,0:T(1,128)S(1)}) custom-call(s32[16,128]{1,0:T(8,128)S(1)} %get-tuple-element.24.ids_ref, s32[16,128]{1,0:T(8,128)S(1)} %get-tuple-element.25.number_ref, f32[16,1024]{1,0:T(8,128)S(1)} %get-tuple-element.28.sign_ref, ...), custom_call_target="tpu_custom_call" | custom-call | flops 536870912 | tf_op jit(solution)/shard_map/close/pallas_call | solution.py:473
  31.9 0.1 collective-permute-start.1
  31.9 0.1 keep.1.keep_ref
  32.1 1.4 %collective-permute-done.1.give_ref = f32[512,128]{1,0:T(8,128)S(1)} collective-permute-done((f32[512,128]{1,0:T(8,128)S(1)}, f32[512,128]{1,0:T(8,128)S(1)}, u32[]{:S(2)}, u32[]{:S(2)}) %collective-permute-start.1) | collective-permute-done | bytes 262176 | tf_op jit(solution)/shard_map/ppermute | solution.py:487
  33.5 0.8 %join.1 = (bf16[32,9,2,128]{3,2,1,0:T(2,128)(2,1)}, f32[16,1024]{1,0:T(8,128)S(1)}) custom-call(f32[512,128]{1,0:T(8,128)S(1)} %keep.1.keep_ref, f32[512,128]{1,0:T(8,128)S(1)} %collective-permute-done.1.give_ref, f32[1,128]{1,0:T(1,128)S(1)} %get-tuple-element.37.part_ref, f32[16,1024]{1,0:T(8,128)S(1)} %get-tuple-element.38.row_ref), custom_call_target="tpu_custom_call" | custom-call | flops 67108864 | tf_op jit(solution)/shard_map/join/pallas_call | solution.py:489
  34.2 2.6 %all-to-all-start.2 = ((bf16[32,9,2,128]{3,2,1,0:T(2,128)(2,1)}), bf16[32,9,2,128]{3,2,1,0:T(2,128)(2,1)S(1)}, u32[]{:S(2)}, u32[]{:S(2)}) async-start(bf16[32,9,2,128]{3,2,1,0:T(2,128)(2,1)} %get-tuple-element.40), calls=%async_computation.2 | async-start | bytes 294912 | tf_op jit(solution)/shard_map/all_to_all | solution.py:496
  36.8 4.5 %patch.1 = f32[2048,128]{1,0:T(8,128)} custom-call(s32[16,128]{1,0:T(8,128)S(1)} %get-tuple-element.23.live_ref, f32[16,1024]{1,0:T(8,128)S(1)} %get-tuple-element.34.lse_ref, f32[16,1024]{1,0:T(8,128)S(1)} %get-tuple-element.39.row_ref, bf16[512,128]{1,0:T(8,128)(2,1)S(1)} %bitcast.11, bf16[512,128]{1,0:T(8,128)(2,1)S(1)} %collective-permute-done.q_ref.oth_ref, ...), custom_call_target="tpu_custom_call" | custom-call | flops 1073741824 | tf_op jit(solution)/shard_map/patch/pallas_call | solution.py:497
  41.3 3.9 %all-to-all-done.2.refs_0_ = bf16[32,9,2,128]{3,2,1,0:T(2,128)(2,1)S(1)} async-done(((bf16[32,9,2,128]{3,2,1,0:T(2,128)(2,1)}), bf16[32,9,2,128]{3,2,1,0:T(2,128)(2,1)S(1)}, u32[]{:S(2)}, u32[]{:S(2)}) %all-to-all-start.2) | async-done | bytes 147488 | tf_op jit(solution)/shard_map/all_to_all | solution.py:496
  45.2 0.7 %final.1 = (f32[1,2,16,128]{3,2,1,0:T(8,128)}, f32[1,128]{1,0:T(1,128)}) custom-call(bf16[32,9,2,128]{3,2,1,0:T(2,128)(2,1)S(1)} %all-to-all-done.2.refs_0_), custom_call_target="tpu_custom_call" | custom-call | flops 131072 | tf_op jit(solution)/shard_map/final/pallas_call | solution.py:500
Async XLA Ops:
  0.6 16.6 %copy-start = (bf16[2048,128]{1,0:T(8,128)(2,1)S(1)}, bf16[2048,128]{1,0:T(8,128)(2,1)}, u32[]{:S(2)}) copy-start(bf16[2048,128]{1,0:T(8,128)(2,1)} %p_ref.7) | copy-start | bytes 1572868
  1.6 22.7 %copy-start.1 = (s32[32,64]{1,0:T(8,128)S(1)}, s32[32,64]{1,0:T(8,128)}, u32[]{:S(2)}) copy-start(s32[32,64]{1,0:T(8,128)} %lab_ref.1) | copy-start | bytes 24580
  1.6 22.7 %copy-start.2 = (s32[16,2]{0,1:T(2,128)S(1)}, s32[16,2]{0,1:T(2,128)}, u32[]{:S(2)}) copy-start(s32[16,2]{0,1:T(2,128)} %param.7) | copy-start | bytes 388
  17.0 1.7 %collective-permute-start = (bf16[512,128]{1,0:T(8,128)(2,1)S(1)}, bf16[512,128]{1,0:T(8,128)(2,1)S(1)}, u32[]{:S(2)}, u32[]{:S(2)}) collective-permute-start(bf16[512,128]{1,0:T(8,128)(2,1)S(1)} %bitcast.8), channel_id=1, source_target_pairs={{0,1},{1,0},{2,3},{3,2},{4,5},{5,4},{6,7},{7,6},{8,9},{9,8},{10,11... | collective-permute-start | bytes 393224 | tf_op jit(solution)/shard_map/ppermute | solution.py:450
  20.7 10.5 %all-to-all-start.1 = ((f32[16,1,1152]{2,1,0:T(1,128)}), f32[16,1,1152]{2,1,0:T(1,128)S(1)}, u32[]{:S(2)}, u32[]{:S(2)}) async-start(f32[16,1,1152]{2,1,0:T(1,128)} %get-tuple-element.33), calls=%async_computation.1 | async-start | bytes 147456 | tf_op jit(solution)/shard_map/all_to_all | solution.py:463
  31.9 1.6 %collective-permute-start.1 = (f32[512,128]{1,0:T(8,128)S(1)}, f32[512,128]{1,0:T(8,128)S(1)}, u32[]{:S(2)}, u32[]{:S(2)}) collective-permute-start(f32[512,128]{1,0:T(8,128)S(1)} %get-tuple-element.36), channel_id=1, source_target_pairs={{0,1},{1,0},{2,3},{3,2},{4,5},{5,4},{6,7},{7,6},{8,9},{9,8},{10,11... | collective-permute-start | bytes 786440 | tf_op jit(solution)/shard_map/ppermute | solution.py:487
  34.2 11.0 %all-to-all-start.2 = ((bf16[32,9,2,128]{3,2,1,0:T(2,128)(2,1)}), bf16[32,9,2,128]{3,2,1,0:T(2,128)(2,1)S(1)}, u32[]{:S(2)}, u32[]{:S(2)}) async-start(bf16[32,9,2,128]{3,2,1,0:T(2,128)(2,1)} %get-tuple-element.40), calls=%async_computation.2 | async-start | bytes 294912 | tf_op jit(solution)/shard_map/all_to_all | solution.py:496

commit v8 on v7

--- a/solution.py
+++ b/solution.py
@@ -89,15 +89,16 @@
 
 def slot_stats(live_ref, q_ref, p_ref, lse_ref, qt_ref, base):
     slots = lse_ref.shape[0]
+    group = slots if q_ref.shape[0] <= 1024 else GROUP
     marked_queries(qt_ref, q_ref)
 
     def one(step, carry):
-        start = step * GROUP
-        blocks = p_ref[pl.ds(pl.multiple_of(start * BROWS, BROWS), GROUP * BROWS), :]
+        start = step * group
+        blocks = p_ref[pl.ds(pl.multiple_of(start * BROWS, BROWS), group * BROWS), :]
         blocks = widened(blocks, live_ref, start)
         for lo in range(0, q_ref.shape[0], CHUNK):
             product = jnp.dot(blocks, qt_ref[:, lo : lo + CHUNK], preferred_element_type=f32)
-            for part in range(GROUP):
+            for part in range(group):
                 slot = start + part
                 z = product[part * BROWS : (part + 1) * BROWS]
                 top = jnp.max(z, axis=0, keepdims=True)
@@ -105,21 +106,19 @@
                 lse_ref[pl.ds(slot, 1), base + lo : base + lo + CHUNK] = top * SCALE2 + jnp.log2(mass)
         return carry
 
-    steps = slots // GROUP
+    steps = slots // group
     lax.fori_loop(0, steps, one, 0, unroll=steps if q_ref.shape[0] <= 1024 else 1)
 
 
-def start_kernel(
-    rows_hbm, pbt_hbm, len_hbm, spread_ref, live_ref, page_ref, number_ref, rows_ref, pbt_ref, len_ref, sems,
-):
-    slots = live_ref.shape[0]
-    pairs = ((rows_hbm, rows_ref), (pbt_hbm, pbt_ref), (len_hbm, len_ref))
-    copies = [pltpu.make_async_copy(*pair, sems.at[at]) for at, pair in enumerate(pairs)]
-    for copy in copies:
-        copy.start()
-    for copy in copies:
-        copy.wait()
+def start_kernel(rows_hbm, spread_ref, rows_ref, sem):
+    copy = pltpu.make_async_copy(rows_hbm, rows_ref, sem)
+    copy.start()
+    copy.wait()
     spread_ref[...] = jnp.broadcast_to(rows_ref[...][None], spread_ref.shape)
+
+
+def own_kernel(pbt_ref, len_ref, q_ref, p_ref, lse_ref, live_ref, page_ref, number_ref, qt_ref):
+    slots = lse_ref.shape[0]
     pages = columns(pbt_ref[0:1, :], slots)
     numbers = columns(pbt_ref[1:2, :], slots)
     page_count = len_ref.shape[1]
@@ -129,9 +128,6 @@
     live_ref[...] = jnp.broadcast_to(jnp.where(pages < 0, 0, live), live_ref.shape)
     page_ref[...] = jnp.broadcast_to(pages, page_ref.shape)
     number_ref[...] = jnp.broadcast_to(numbers, number_ref.shape)
-
-
-def own_kernel(live_ref, q_ref, p_ref, lse_ref, qt_ref):
     slot_stats(live_ref, q_ref, p_ref, lse_ref, qt_ref, 0)
 
 
@@ -264,8 +260,8 @@
 
 
 def close_kernel(
-    ids_ref, number_ref, sign_ref, page_ref, row_ref, loss_ref, acc_ref, recv_ref, scales_ref, give_ref, lse_ref,
-    full_ref, part_ref, got_ref,
+    ids_ref, number_ref, sign_ref, page_ref, loss_ref, acc_ref, recv_ref, scales_ref, give_ref, both_ref, part_ref,
+    got_ref,
 ):
     slots, rows = page_ref.shape
     peers = recv_ref.shape[0]
@@ -275,7 +271,6 @@
     pages = ids_ref[:, 0:1]
     first = pages[0:1]
     last = jnp.max(pages, axis=0, keepdims=True)
-    is_first = pages == first
     is_last = pages == last
     alone = first == last
 
@@ -313,8 +308,8 @@
         keepdims=True,
     )
     loss = (loss + loss_ref[...]) * (1.0 / QUESTION_WORDS)
-    lse_ref[...] = jnp.where(is_last, tail_full, jnp.where(is_first, head_full, value))
-    full_ref[...] = jnp.where(is_last, row[1:2], jnp.where(is_first, row[0:1], row_ref[...]))
+    both_ref[0:2, :] = both
+    both_ref[2:4, :] = row
     head_scale = row[0:1] * jnp.exp2(head - head_full)
     tail_scale = row[1:2] * jnp.exp2(tail - tail_full)
     scales_ref[0:1, :] = head_scale
@@ -334,7 +329,17 @@
         out_ref[lo : lo + CHUNK, :] = total.T
 
 
-def keep_kernel(acc_ref, scales_ref, keep_ref):
+def keep_kernel(ids_ref, page_ref, row_ref, both_ref, acc_ref, scales_ref, keep_ref, lse_ref, full_ref):
+    pages = ids_ref[:, 0:1]
+    is_first = pages == pages[0:1]
+    is_last = pages == jnp.max(pages, axis=0, keepdims=True)
+
+    def filled(at, values):
+        head, tail = both_ref[at : at + 1, :], both_ref[at + 1 : at + 2, :]
+        return jnp.where(is_last, tail, jnp.where(is_first, head, values))
+
+    lse_ref[...] = filled(0, page_ref[...])
+    full_ref[...] = filled(2, row_ref[...])
     combine(acc_ref, scales_ref, keep_ref, 0)
 
 
@@ -428,29 +433,23 @@
     pbt = page_blocks.T
     questions = local // QUESTION_WORDS
     halves = local_rows.reshape(questions, 2, HALF_WORDS, width).swapaxes(0, 1).reshape(2, local // 2, width)
-    inputs = (halves, page_blocks.T, lengths.reshape(1, -1))
     p = patches
-    spread, live, pages, numbers = call(
+    (spread,) = call(
         start_kernel,
         "start",
         4 * matmul,
-        [HBM] * 3,
-        [((devices // 2, *halves.shape), bf16), ids, ids, ids],
-        [
-            (halves.shape, bf16),
-            (pbt.shape, jnp.int32),
-            ((1, lengths.shape[0]), jnp.int32),
-            pltpu.SemaphoreType.DMA((3,)),
-        ],
-    )(*(pltpu.with_memory_space_constraint(x, pltpu.HBM) for x in inputs))
+        [HBM],
+        [((devices // 2, *halves.shape), bf16)],
+        [(halves.shape, bf16), pltpu.SemaphoreType.DMA],
+    )(pltpu.with_memory_space_constraint(halves, pltpu.HBM))
     own = lax.all_to_all(
         spread.reshape(devices, local // 2, width), axes, 0, 0, tiled=True
     ).reshape(half, width)
     pairs = [(i, i ^ 1) for i in range(devices)]
     other = lax.ppermute(own, axes, pairs)
-    (own_lse,) = call(
-        own_kernel, "own", matmul // 2, [VMEM] * 3, [half_table], [turned_half], limit
-    )(live, own, p)
+    own_lse, live, pages, numbers = call(
+        own_kernel, "own", matmul // 2, [VMEM] * 4, [half_table, ids, ids, ids], [turned_half], limit
+    )(pbt, lengths.reshape(1, -1), own, p)
     lse, send = call(
         stats_kernel,
         "stats",
@@ -470,22 +469,18 @@
         [table, ((width, rows), bf16)],
         limit,
     )(pbt, pages, numbers, live, labels, lse, own, other, p)
-    scales, give, full_lse, row_grad, part = call(
+    scales, give, both, part = call(
         close_kernel,
         "close",
         matmul,
-        [VMEM] * 8,
-        [
-            ((2, rows), f32),
-            ((half, width), f32),
-            table,
-            table,
-            ((1, BROWS), f32),
-        ],
+        [VMEM] * 7,
+        [((2, rows), f32), ((half, width), f32), ((4, rows), f32), ((1, BROWS), f32)],
         [((peers, rows + 128), f32)],
-    )(pages, numbers, sign, page_lse, row, loss, acc, recv)
+    )(pages, numbers, sign, page_lse, loss, acc, recv)
     give = lax.ppermute(give, axes, pairs)
-    (keep,) = call(keep_kernel, "keep", matmul // 4, [VMEM] * 2, [((half, width), f32)])(acc, scales)
+    keep, full_lse, row_grad = call(
+        keep_kernel, "keep", matmul // 4, [VMEM] * 6, [((half, width), f32), table, table]
+    )(pages, page_lse, row, both, acc, scales)
     parts, row_grad = call(
         join_kernel,
         "join",

time: 46.3 us -> 46.1 us (level)
  no operation moved by 1% of the time
where the time goes in v8:
time: 46.1 us; the launch traced here: 45.8 us
  blocking collectives  15.3 us (33%)
  Pallas kernels  15 us (33%)
  waiting for transfers between devices  8.35 us (18%)
  starting transfers between devices  6.41 us (14%)
  between operations  0.73 us (2%)
    all_to_all x1, blocking collectives, shards(): lax.all_to_all(spread.reshape(devices, local // 2, width), axes, 0, 0, ti...  15.3 us
    pallas_call x1, Pallas kernels, shards(): call(patch_kernel, 'patch', 2 * matmul, [VMEM] * 6, [(patches.shape, f32)...  4.5 us
    all_to_all x1, waiting for transfers between devices, shards(): gathered = lax.all_to_all(parts, axes, 0, 0, tiled=True)  3.91 us
    pallas_call x1, Pallas kernels, shards(): call(inner_kernel, 'inner', 2 * matmul, [SMEM] + [VMEM] * 8, [table, tabl...  3.84 us
    all_to_all x1, starting transfers between devices, shards(): recv = lax.all_to_all(send, 'page', 0, 0, tiled=True)  3.5 us
    all_to_all x1, waiting for transfers between devices, shards(): recv = lax.all_to_all(send, 'page', 0, 0, tiled=True)  3.09 us
    all_to_all x1, starting transfers between devices, shards(): gathered = lax.all_to_all(parts, axes, 0, 0, tiled=True)  2.57 us
    pallas_call x1, Pallas kernels, shards(): call(stats_kernel, 'stats', matmul // 2, [VMEM] * 5, [table, ((peers, 1,...  2.11 us
  transfers between devices with their start and end apart: 4, of which 3 were waited for; matrix products, arithmetic and copies ran while one was open for 0% of the time, Pallas kernels for 22%

profile of v8, /device:TPU:0, one launch (start us, length us, event | category | flops | bytes accessed | tf_op | source)
XLA Modules:
  0.0 45.8 jit_solution(2353426393040796405)
XLA Ops:
  0.6 0.0 copy-start
  0.6 0.0 copy-start.2
  0.7 0.0 copy-start.3
  0.7 0.8 %start.1 = bf16[16,2,16,128]{3,2,1,0:T(8,128)(2,1)S(1)} custom-call(bf16[2,16,128]{2,1,0:T(8,128)(2,1)} %bitcast.17), custom_call_target="tpu_custom_call" | custom-call | flops 2147483648 | tf_op jit(solution)/shard_map/start/pallas_call | solution.py:437
  1.4 0.0 copy-start.1
  1.5 15.3 %all_to_all.15 = bf16[32,16,128]{2,1,0:T(8,128)(2,1)S(1)} all-to-all(bf16[32,16,128]{2,1,0:T(8,128)(2,1)S(1)} %bitcast.12), channel_id=1, replica_groups=mesh['grp'=2,'page'=16] {'grp','page'}, dimensions={0} | all-to-all | bytes 262144 | tf_op jit(solution)/shard_map/all_to_all | solution.py:445
  16.8 0.3 collective-permute-start
  17.1 0.0 copy-done
  17.1 0.0 copy-done.3
  17.1 1.4 %own.1 = (f32[16,512]{1,0:T(8,128)S(1)}, s32[16,128]{1,0:T(8,128)S(1)}, s32[16,128]{1,0:T(8,128)S(1)}, s32[16,128]{1,0:T(8,128)S(1)}) custom-call(s32[2,16]{1,0:T(2,128)S(1)} %bitcast.13, s32[1,64]{1,0:T(1,128)S(1)} %bitcast.15, bf16[512,128]{1,0:T(8,128)(2,1)S(1)} %bitcast.9, bf16[2048,128]{1,0:T(8,128)(2,1)S(1)} %copy-done), custom_call_target="tpu_custom_call" | custom-call | flops 268435456 | tf_op jit(solution)/shard_map/own/pallas_call | solution.py:450
  18.5 0.0 collective-permute-done.q_ref.oth_ref
  18.5 2.1 %stats.1 = (f32[16,1024]{1,0:T(8,128)S(1)}, f32[16,1,1152]{2,1,0:T(1,128)}) custom-call(s32[16,128]{1,0:T(8,128)S(1)} %get-tuple-element.26.ids_ref, s32[16,128]{1,0:T(8,128)S(1)} %get-tuple-element.25.live_ref, f32[16,512]{1,0:T(8,128)S(1)} %get-tuple-element.28.own_lse_ref, bf16[512,128]{1,0:T(8,128)(2,1)S(1)} %collective-permute-done.q_ref.oth_ref, ...), custom_call_target="tpu_custom_call" | custom-call | flops 268435456 | tf_op jit(solution)/shard_map/stats/pallas_call | solution.py:453
  20.6 3.5 %all-to-all-start.1 = ((f32[16,1,1152]{2,1,0:T(1,128)}), f32[16,1,1152]{2,1,0:T(1,128)S(1)}, u32[]{:S(2)}, u32[]{:S(2)}) async-start(f32[16,1,1152]{2,1,0:T(1,128)} %get-tuple-element.35), calls=%async_computation.1 | async-start | bytes 147456 | tf_op jit(solution)/shard_map/all_to_all | solution.py:462
  24.1 3.8 %inner.1 = (f32[16,1024]{1,0:T(8,128)S(1)}, f32[16,1024]{1,0:T(8,128)S(1)}, f32[16,1024]{1,0:T(8,128)S(1)}, f32[1,128]{1,0:T(1,128)S(1)}, f32[3,128,1024]{2,1,0:T(8,128)S(1)}) custom-call(s32[2,16]{1,0:T(2,128)S(1)} %bitcast.14, s32[16,128]{1,0:T(8,128)S(1)} %get-tuple-element.26.ids_ref, s32[16,128]{1,0:T(8,128)S(1)} %get-tuple-element.27.number_ref, ...), custom_call_target="tpu_custom_call" | custom-call | flops 1073741824 | tf_op jit(solution)/shard_map/inner/pallas_call | solution.py:463
  28.0 3.1 %all-to-all-done.1.recv_ref = f32[16,1,1152]{2,1,0:T(1,128)S(1)} async-done(((f32[16,1,1152]{2,1,0:T(1,128)}), f32[16,1,1152]{2,1,0:T(1,128)S(1)}, u32[]{:S(2)}, u32[]{:S(2)}) %all-to-all-start.1) | async-done | bytes 73760 | tf_op jit(solution)/shard_map/all_to_all | solution.py:462
  31.1 0.7 %close.1 = (f32[2,1024]{1,0:T(2,128)S(1)}, f32[512,128]{1,0:T(8,128)S(1)}, f32[4,1024]{1,0:T(4,128)S(1)}, f32[1,128]{1,0:T(1,128)S(1)}) custom-call(s32[16,128]{1,0:T(8,128)S(1)} %get-tuple-element.26.ids_ref, s32[16,128]{1,0:T(8,128)S(1)} %get-tuple-element.27.number_ref, f32[16,1024]{1,0:T(8,128)S(1)} %get-tuple-element.32.sign_ref, ...), custom_call_target="tpu_custom_call" | custom-call | flops 536870912 | tf_op jit(solution)/shard_map/close/pallas_call | solution.py:472
  31.7 0.1 collective-permute-start.1
  31.8 0.2 keep.1
  32.0 1.3 %collective-permute-done.1.give_ref = f32[512,128]{1,0:T(8,128)S(1)} collective-permute-done((f32[512,128]{1,0:T(8,128)S(1)}, f32[512,128]{1,0:T(8,128)S(1)}, u32[]{:S(2)}, u32[]{:S(2)}) %collective-permute-start.1) | collective-permute-done | bytes 262176 | tf_op jit(solution)/shard_map/ppermute | solution.py:480
  33.3 0.8 %join.1 = (bf16[32,9,2,128]{3,2,1,0:T(2,128)(2,1)}, f32[16,1024]{1,0:T(8,128)S(1)}) custom-call(f32[512,128]{1,0:T(8,128)S(1)} %get-tuple-element.39.keep_ref, f32[512,128]{1,0:T(8,128)S(1)} %collective-permute-done.1.give_ref, f32[1,128]{1,0:T(1,128)S(1)} %get-tuple-element.41.part_ref, f32[16,1024]{1,0:T(8,128)S(1)} %get-tuple-element.42.row_ref), custom_call_target="tpu_custom_call" | custom-call | flops 67108864 | tf_op jit(solution)/shard_map/join/pallas_call | solution.py:484
  34.1 2.6 %all-to-all-start.2 = ((bf16[32,9,2,128]{3,2,1,0:T(2,128)(2,1)}), bf16[32,9,2,128]{3,2,1,0:T(2,128)(2,1)S(1)}, u32[]{:S(2)}, u32[]{:S(2)}) async-start(bf16[32,9,2,128]{3,2,1,0:T(2,128)(2,1)} %get-tuple-element.44), calls=%async_computation.2 | async-start | bytes 294912 | tf_op jit(solution)/shard_map/all_to_all | solution.py:491
  36.7 4.5 %patch.1 = f32[2048,128]{1,0:T(8,128)} custom-call(s32[16,128]{1,0:T(8,128)S(1)} %get-tuple-element.25.live_ref, f32[16,1024]{1,0:T(8,128)S(1)} %get-tuple-element.38.lse_ref, f32[16,1024]{1,0:T(8,128)S(1)} %get-tuple-element.43.row_ref, bf16[512,128]{1,0:T(8,128)(2,1)S(1)} %bitcast.11, bf16[512,128]{1,0:T(8,128)(2,1)S(1)} %collective-permute-done.q_ref.oth_ref, ...), custom_call_target="tpu_custom_call" | custom-call | flops 1073741824 | tf_op jit(solution)/shard_map/patch/pallas_call | solution.py:492
  41.2 3.9 %all-to-all-done.2.refs_0_ = bf16[32,9,2,128]{3,2,1,0:T(2,128)(2,1)S(1)} async-done(((bf16[32,9,2,128]{3,2,1,0:T(2,128)(2,1)}), bf16[32,9,2,128]{3,2,1,0:T(2,128)(2,1)S(1)}, u32[]{:S(2)}, u32[]{:S(2)}) %all-to-all-start.2) | async-done | bytes 147488 | tf_op jit(solution)/shard_map/all_to_all | solution.py:491
  45.1 0.7 %final.1 = (f32[1,2,16,128]{3,2,1,0:T(8,128)}, f32[1,128]{1,0:T(1,128)}) custom-call(bf16[32,9,2,128]{3,2,1,0:T(2,128)(2,1)S(1)} %all-to-all-done.2.refs_0_), custom_call_target="tpu_custom_call" | custom-call | flops 131072 | tf_op jit(solution)/shard_map/final/pallas_call | solution.py:495
  (2 shorter events, 0.0 us)
Async XLA Ops:
  0.6 16.4 %copy-start = (bf16[2048,128]{1,0:T(8,128)(2,1)S(1)}, bf16[2048,128]{1,0:T(8,128)(2,1)}, u32[]{:S(2)}) copy-start(bf16[2048,128]{1,0:T(8,128)(2,1)} %p_ref.7) | copy-start | bytes 1572868
  0.6 16.4 %copy-start.2 = (s32[16,2]{0,1:T(2,128)S(1)}, s32[16,2]{0,1:T(2,128)}, u32[]{:S(2)}) copy-start(s32[16,2]{0,1:T(2,128)} %param.7) | copy-start | bytes 388
  0.7 16.4 %copy-start.3 = (s32[64]{0:T(128)S(1)}, s32[64]{0:T(128)}, u32[]{:S(2)}) copy-start(s32[64]{0:T(128)} %param.8) | copy-start | bytes 772
  1.4 22.7 %copy-start.1 = (s32[32,64]{1,0:T(8,128)S(1)}, s32[32,64]{1,0:T(8,128)}, u32[]{:S(2)}) copy-start(s32[32,64]{1,0:T(8,128)} %lab_ref.1) | copy-start | bytes 24580
  16.8 1.7 %collective-permute-start = (bf16[512,128]{1,0:T(8,128)(2,1)S(1)}, bf16[512,128]{1,0:T(8,128)(2,1)S(1)}, u32[]{:S(2)}, u32[]{:S(2)}) collective-permute-start(bf16[512,128]{1,0:T(8,128)(2,1)S(1)} %bitcast.8), channel_id=1, source_target_pairs={{0,1},{1,0},{2,3},{3,2},{4,5},{5,4},{6,7},{7,6},{8,9},{9,8},{10,11... | collective-permute-start | bytes 393224 | tf_op jit(solution)/shard_map/ppermute | solution.py:449
  20.6 10.5 %all-to-all-start.1 = ((f32[16,1,1152]{2,1,0:T(1,128)}), f32[16,1,1152]{2,1,0:T(1,128)S(1)}, u32[]{:S(2)}, u32[]{:S(2)}) async-start(f32[16,1,1152]{2,1,0:T(1,128)} %get-tuple-element.35), calls=%async_computation.1 | async-start | bytes 147456 | tf_op jit(solution)/shard_map/all_to_all | solution.py:462
  31.7 1.6 %collective-permute-start.1 = (f32[512,128]{1,0:T(8,128)S(1)}, f32[512,128]{1,0:T(8,128)S(1)}, u32[]{:S(2)}, u32[]{:S(2)}) collective-permute-start(f32[512,128]{1,0:T(8,128)S(1)} %get-tuple-element.40), channel_id=1, source_target_pairs={{0,1},{1,0},{2,3},{3,2},{4,5},{5,4},{6,7},{7,6},{8,9},{9,8},{10,11... | collective-permute-start | bytes 786440 | tf_op jit(solution)/shard_map/ppermute | solution.py:480
  34.1 11.0 %all-to-all-start.2 = ((bf16[32,9,2,128]{3,2,1,0:T(2,128)(2,1)}), bf16[32,9,2,128]{3,2,1,0:T(2,128)(2,1)S(1)}, u32[]{:S(2)}, u32[]{:S(2)}) async-start(bf16[32,9,2,128]{3,2,1,0:T(2,128)(2,1)} %get-tuple-element.44), calls=%async_computation.2 | async-start | bytes 294912 | tf_op jit(solution)/shard_map/all_to_all | solution.py:491
